TPU v7x, 8 devices: a whole 2x2x1 slice. The times are simulated.
8 devices in a mesh: dp: 2 (over z, y), tp: 4 (over x, core).
Axes of the slice: x: 2, y: 2, z: 1, core: 2. Of those that a mesh axis runs over, the one named last changes fastest.
Arguments:
- x: bfloat16 [512, 2048], P(('dp', 'tp')), parts along dimension 0
- grad_y: bfloat16 [512, 2048], P(('dp', 'tp')), parts along dimension 0
- gain_attn: float32 [3, 2048], replicated
- gain_mlp: float32 [3, 2048], replicated
- w_qkv: bfloat16 [3, 2048, 6144], P(None, None, 'tp')
- w_out: bfloat16 [3, 2048, 2048], P(None, 'tp')
- w_gate: bfloat16 [3, 2048, 8192], P(None, None, 'tp')
- w_up: bfloat16 [3, 2048, 8192], P(None, None, 'tp')
- w_down: bfloat16 [3, 8192, 2048], P(None, 'tp')
Outputs:
- output 1: bfloat16 [512, 2048], P(('dp', 'tp')), parts along dimension 0
- output 2: bfloat16 [512, 2048], P(('dp', 'tp')), parts along dimension 0
- output 3: bfloat16 [6, 2048, 6144], P('dp', None, 'tp'), parts along dimension 0
- output 4: bfloat16 [6, 2048, 2048], P('dp', 'tp'), parts along dimension 0
- output 5: bfloat16 [6, 2048, 8192], P('dp', None, 'tp'), parts along dimension 0
- output 6: bfloat16 [6, 2048, 8192], P('dp', None, 'tp'), parts along dimension 0
- output 7: bfloat16 [6, 8192, 2048], P('dp', 'tp'), parts along dimension 0
- output 8: float32 [6, 2048], P('dp'), parts along dimension 0
- output 9: float32 [6, 2048], P('dp'), parts along dimension 0
There are 2 independent parts. A program takes and returns all parts, laid end to end along the dimension named above; an argument that names none is the same for every part.
All inputs are finite; a program needn't handle non-finite values.
Results may differ from a plain program's by a relative error of at most 0.02.
Values are sent between devices in bfloat16 or wider.
A program may use at most 1 GiB of HBM per device.

v0:
```python
import jax
import jax.numpy as jnp
from jax import lax
from jax.sharding import PartitionSpec as P

HEAD_DIM = 128
NORM_EPS = 1e-5


def rms_norm(hidden_in, gain_vec):
    hidden_f = hidden_in.astype(jnp.float32)
    inv_rms = lax.rsqrt(jnp.mean(hidden_f * hidden_f, axis=-1, keepdims=True) + NORM_EPS)
    return (hidden_f * inv_rms * gain_vec).astype(jnp.bfloat16)


def swiglu(gate_act, up_act):
    return (jax.nn.silu(gate_act.astype(jnp.float32)) * up_act.astype(jnp.float32)).astype(jnp.bfloat16)


def contract(left_op, right_op, eq_form):
    return jnp.einsum(eq_form, left_op, right_op, preferred_element_type=jnp.float32)


def gather_rows(row_shard):
    return lax.all_gather(row_shard, 'tp', axis=0, tiled=True)


def scatter_rows(part_sum):
    return lax.psum_scatter(part_sum, 'tp', scatter_dimension=0, tiled=True).astype(jnp.bfloat16)


def attention_core(full_in, w_qkv, kv_local, group_size):
    seq_len = full_in.shape[0]
    qkv_out = jnp.dot(full_in, w_qkv, preferred_element_type=jnp.float32).astype(jnp.bfloat16)
    blocks = qkv_out.reshape(seq_len, kv_local, group_size + 2, HEAD_DIM)
    queries = blocks[:, :, :group_size]
    key_rows = blocks[:, :, group_size]
    value_rows = blocks[:, :, group_size + 1]
    scores = contract(queries, key_rows, 'ikqh,jkh->kqij') * HEAD_DIM ** -0.5
    positions = jnp.arange(seq_len)
    causal = positions[:, None] >= positions[None, :]
    prob_f32 = jax.nn.softmax(jnp.where(causal, scores, -1e30), axis=-1)
    prob_low = prob_f32.astype(jnp.bfloat16)
    heads_out = contract(prob_low, value_rows, 'kqij,jkh->ikqh').astype(jnp.bfloat16)
    heads_out = heads_out.reshape(seq_len, kv_local * group_size * HEAD_DIM)
    return queries, key_rows, value_rows, prob_f32, prob_low, heads_out


def mlp_core(full_mid, w_gate, w_up):
    gate_act = jnp.dot(full_mid, w_gate, preferred_element_type=jnp.float32).astype(jnp.bfloat16)
    up_act = jnp.dot(full_mid, w_up, preferred_element_type=jnp.float32).astype(jnp.bfloat16)
    return gate_act, up_act, swiglu(gate_act, up_act)


def layer_forward(hidden_in, weights, kv_local, group_size):
    gain_attn, gain_mlp, w_qkv, w_out, w_gate, w_up, w_down = weights
    full_in = gather_rows(rms_norm(hidden_in, gain_attn))
    attn_parts = attention_core(full_in, w_qkv, kv_local, group_size)
    hidden_mid = hidden_in + scatter_rows(jnp.dot(attn_parts[5], w_out, preferred_element_type=jnp.float32))
    full_mid = gather_rows(rms_norm(hidden_mid, gain_mlp))
    mlp_parts = mlp_core(full_mid, w_gate, w_up)
    layer_out = hidden_mid + scatter_rows(jnp.dot(mlp_parts[2], w_down, preferred_element_type=jnp.float32))
    return layer_out, (full_in, attn_parts, hidden_mid, full_mid, mlp_parts)


def layer_backward(hidden_in, saved_acts, d_out, weights):
    gain_attn, gain_mlp, w_qkv, w_out, w_gate, w_up, w_down = weights
    full_in, attn_parts, hidden_mid, full_mid, mlp_parts = saved_acts
    queries, key_rows, value_rows, prob_f32, prob_low, heads_out = attn_parts
    gate_act, up_act, gated_act = mlp_parts
    seq_len, kv_local, group_size = queries.shape[0], queries.shape[1], queries.shape[2]
    d_down_full = gather_rows(d_out)
    grad_down = contract(gated_act, d_down_full, 'sf,sd->fd').astype(jnp.bfloat16)
    d_gated = contract(d_down_full, w_down, 'sd,fd->sf').astype(jnp.bfloat16)
    _, swiglu_pull = jax.vjp(swiglu, gate_act, up_act)
    d_gate, d_up = swiglu_pull(d_gated)
    grad_gate = contract(full_mid, d_gate, 'sd,sf->df').astype(jnp.bfloat16)
    grad_up = contract(full_mid, d_up, 'sd,sf->df').astype(jnp.bfloat16)
    d_mid = scatter_rows(contract(d_gate, w_gate, 'sf,df->sd') + contract(d_up, w_up, 'sf,df->sd'))
    _, norm_mid_pull = jax.vjp(rms_norm, hidden_mid, gain_mlp)
    d_norm_mid, grad_gain_mlp = norm_mid_pull(d_mid)
    d_hidden_mid = d_out + d_norm_mid
    d_attn_full = gather_rows(d_hidden_mid)
    grad_out = contract(heads_out, d_attn_full, 'sr,sd->rd').astype(jnp.bfloat16)
    d_heads = contract(d_attn_full, w_out, 'sd,rd->sr').astype(jnp.bfloat16).reshape(seq_len, kv_local, group_size, HEAD_DIM)
    d_prob = contract(d_heads, value_rows, 'ikqh,jkh->kqij')
    d_values = contract(prob_low, d_heads, 'kqij,ikqh->jkh').astype(jnp.bfloat16)
    d_scores = (prob_f32 * (d_prob - jnp.sum(d_prob * prob_f32, axis=-1, keepdims=True)) * HEAD_DIM ** -0.5).astype(jnp.bfloat16)
    d_queries = contract(d_scores, key_rows, 'kqij,jkh->ikqh').astype(jnp.bfloat16)
    d_keys = contract(d_scores, queries, 'kqij,ikqh->jkh').astype(jnp.bfloat16)
    d_qkv = jnp.concatenate([d_queries, d_keys[:, :, None], d_values[:, :, None]], axis=2).reshape(seq_len, -1)
    grad_qkv = contract(full_in, d_qkv, 'sd,sc->dc').astype(jnp.bfloat16)
    d_in = scatter_rows(contract(d_qkv, w_qkv, 'sc,dc->sd'))
    _, norm_in_pull = jax.vjp(rms_norm, hidden_in, gain_attn)
    d_norm_in, grad_gain_attn = norm_in_pull(d_in)
    return d_hidden_mid + d_norm_in, (grad_gain_attn, grad_gain_mlp, grad_qkv, grad_out, grad_gate, grad_up, grad_down)


def solution(mesh):
    row_spec = P(('dp', 'tp'), None)
    col_spec = P(None, None, 'tp')
    mid_spec = P(None, 'tp', None)
    in_specs = (row_spec, row_spec, P(None, None), P(None, None), col_spec, mid_spec, col_spec, col_spec, mid_spec)
    out_specs = (row_spec, row_spec, P('dp', None, 'tp'), P('dp', 'tp', None), P('dp', None, 'tp'), P('dp', None, 'tp'), P('dp', 'tp', None), P('dp', None), P('dp', None))

    def device_step(x, grad_y, gain_attn, gain_mlp, w_qkv, w_out, w_gate, w_up, w_down):
        all_weights = (gain_attn, gain_mlp, w_qkv, w_out, w_gate, w_up, w_down)
        num_layers = w_qkv.shape[0]
        rows_local = w_out.shape[1]
        kv_local = (w_qkv.shape[2] - rows_local) // (2 * HEAD_DIM)
        group_size = rows_local // (kv_local * HEAD_DIM)
        layer_inputs = [x]
        for layer_idx in range(num_layers):
            weights = tuple(weight[layer_idx] for weight in all_weights)
            layer_out, _ = layer_forward(layer_inputs[-1], weights, kv_local, group_size)
            layer_inputs.append(layer_out)
        d_hidden = grad_y
        layer_grads = [None] * num_layers
        for layer_idx in reversed(range(num_layers)):
            weights = tuple(weight[layer_idx] for weight in all_weights)
            kept_in, d_hidden = lax.optimization_barrier((layer_inputs[layer_idx], d_hidden))
            _, saved_acts = layer_forward(kept_in, weights, kv_local, group_size)
            d_hidden, layer_grads[layer_idx] = layer_backward(kept_in, saved_acts, d_hidden, weights)
        stacked = [jnp.stack([grads[kind_idx] for grads in layer_grads]) for kind_idx in range(7)]
        gain_grads = lax.psum(jnp.stack([stacked[0], stacked[1]]), 'tp')
        return (layer_inputs[-1], d_hidden, stacked[2], stacked[3], stacked[4], stacked[5], stacked[6], gain_grads[0], gain_grads[1])

    return jax.shard_map(device_step, mesh=mesh, in_specs=in_specs, out_specs=out_specs, check_vma=False)
```

profile of v0, /device:TPU:0, one launch (start us, length us, event | category | flops | bytes accessed | tf_op | source)
XLA Modules:
  0.0 930.8 jit_solution(3052743140881883066)
XLA Ops:
  11.1 16.6 %all-gather.19.cloned.1.call-done = bf16[256,2048]{1,0:T(8,128)(2,1)} async-done(((bf16[64,2048]{1,0:T(8,128)(2,1)}), bf16[256,2048]{1,0:T(8,128)(2,1)}) %all-gather.19.cloned.1.call-update) | async-done | bytes 1048592 | tf_op jit(solution)/shard_map/all_gather | solution.py:25
  38.3 24.9 %reduce-scatter.16.cloned.1.call-done = f32[64,2048]{1,0:T(8,128)} async-done(((f32[256,2048]{1,0:T(8,128)}), f32[64,2048]{1,0:T(8,128)}) %reduce-scatter.16.cloned.1.call-update) | async-done | bytes 524304 | tf_op jit(solution)/shard_map/reduce_scatter | solution.py:29
  65.4 13.8 %all-gather.21.cloned.1.call-done = bf16[256,2048]{1,0:T(8,128)(2,1)} async-done(((bf16[64,2048]{1,0:T(8,128)(2,1)}), bf16[256,2048]{1,0:T(8,128)(2,1)}) %all-gather.21.cloned.1.call-update) | async-done | bytes 1048592 | tf_op jit(solution)/shard_map/all_gather | solution.py:25
  79.2 6.1 fusion.132
  85.3 11.9 %fusion.34 = f32[256,2048]{1,0:T(8,128)} fusion(bf16[3,2048,2048]{2,1,0:T(8,128)(2,1)} %param.17, bf16[256,2048]{1,0:T(8,128)(2,1)S(1)} %copy-done.47, bf16[3,2048,2048]{2,1,0:T(8,128)(2,1)} %param.16, bf16[256,2048]{1,0:T(8,128)(2,1)S(1)} %fusion.132), kind=kOutput, calls=%fused_computation.38 | convolution fusion | flops 4299685888 | bytes 20971520 | tf_op jit(solution)/shard_map/dot_general | solution.py:62
  97.4 25.6 %reduce-scatter.18.cloned.1.call-done = f32[64,2048]{1,0:T(8,128)} async-done(((f32[256,2048]{1,0:T(8,128)}), f32[64,2048]{1,0:T(8,128)}) %reduce-scatter.18.cloned.1.call-update) | async-done | bytes 524304 | tf_op jit(solution)/shard_map/reduce_scatter | solution.py:29
  125.4 13.6 %all-gather.23.cloned.1.call-done = bf16[256,2048]{1,0:T(8,128)(2,1)} async-done(((bf16[64,2048]{1,0:T(8,128)(2,1)}), bf16[256,2048]{1,0:T(8,128)(2,1)}) %all-gather.23.cloned.1.call-update) | async-done | bytes 1048592 | tf_op jit(solution)/shard_map/all_gather | solution.py:25
  148.8 25.6 %reduce-scatter.20.cloned.1.call-done = f32[64,2048]{1,0:T(8,128)} async-done(((f32[256,2048]{1,0:T(8,128)}), f32[64,2048]{1,0:T(8,128)}) %reduce-scatter.20.cloned.1.call-update) | async-done | bytes 524304 | tf_op jit(solution)/shard_map/reduce_scatter | solution.py:29
  176.5 13.8 %all-gather.25.cloned.1.call-done = bf16[256,2048]{1,0:T(8,128)(2,1)} async-done(((bf16[64,2048]{1,0:T(8,128)(2,1)}), bf16[256,2048]{1,0:T(8,128)(2,1)}) %all-gather.25.cloned.1.call-update) | async-done | bytes 1048592 | tf_op jit(solution)/shard_map/all_gather | solution.py:25
  190.4 6.1 fusion.156
  196.5 11.9 %fusion.18 = f32[256,2048]{1,0:T(8,128)} fusion(bf16[3,2048,2048]{2,1,0:T(8,128)(2,1)} %param.17, bf16[256,2048]{1,0:T(8,128)(2,1)S(1)} %copy-done.48, bf16[3,2048,2048]{2,1,0:T(8,128)(2,1)} %param.16, bf16[256,2048]{1,0:T(8,128)(2,1)S(1)} %fusion.156), kind=kOutput, calls=%fused_computation.22 | convolution fusion | flops 4299685888 | bytes 20971520 | tf_op jit(solution)/shard_map/dot_general | solution.py:62
  208.4 25.6 %reduce-scatter.22.cloned.1.call-done = f32[64,2048]{1,0:T(8,128)} async-done(((f32[256,2048]{1,0:T(8,128)}), f32[64,2048]{1,0:T(8,128)}) %reduce-scatter.22.cloned.1.call-update) | async-done | bytes 524304 | tf_op jit(solution)/shard_map/reduce_scatter | solution.py:29
  236.4 13.8 %all-gather.33.cloned.1.call-done = bf16[256,2048]{1,0:T(8,128)(2,1)} async-done(((bf16[64,2048]{1,0:T(8,128)(2,1)}), bf16[256,2048]{1,0:T(8,128)(2,1)}) %all-gather.33.cloned.1.call-update) | async-done | bytes 1048592 | tf_op jit(solution)/shard_map/all_gather | solution.py:25
  260.8 24.9 %reduce-scatter.28.cloned.1.call-done = f32[64,2048]{1,0:T(8,128)} async-done(((f32[256,2048]{1,0:T(8,128)}), f32[64,2048]{1,0:T(8,128)}) %reduce-scatter.28.cloned.1.call-update) | async-done | bytes 524304 | tf_op jit(solution)/shard_map/reduce_scatter | solution.py:29
  288.3 12.7 %all-gather.31.cloned.1.call-done = bf16[256,2048]{1,0:T(8,128)(2,1)} async-done(((bf16[64,2048]{1,0:T(8,128)(2,1)}), bf16[256,2048]{1,0:T(8,128)(2,1)}) %all-gather.31.cloned.1.call-update) | async-done | bytes 1048592 | tf_op jit(solution)/shard_map/all_gather | solution.py:25
  301.0 7.1 fusion.201
  308.1 8.7 all-gather.35.cloned.1.call-done
  322.9 6.3 fusion.4
  335.9 7.7 fusion.111
  343.6 25.6 %reduce-scatter.30.cloned.1.call-done = f32[64,2048]{1,0:T(8,128)} async-done(((f32[256,2048]{1,0:T(8,128)}), f32[64,2048]{1,0:T(8,128)}) %reduce-scatter.30.cloned.1.call-update) | async-done | bytes 524304 | tf_op jit(solution)/shard_map/reduce_scatter | solution.py:29
  373.3 13.6 %all-gather.37.cloned.1.call-done = bf16[256,2048]{1,0:T(8,128)(2,1)} async-done(((bf16[64,2048]{1,0:T(8,128)(2,1)}), bf16[256,2048]{1,0:T(8,128)(2,1)}) %all-gather.37.cloned.1.call-update) | async-done | bytes 1048592 | tf_op jit(solution)/shard_map/all_gather | solution.py:25
  398.4 25.6 %reduce-scatter.32.cloned.1.call-done = f32[64,2048]{1,0:T(8,128)} async-done(((f32[256,2048]{1,0:T(8,128)}), f32[64,2048]{1,0:T(8,128)}) %reduce-scatter.32.cloned.1.call-update) | async-done | bytes 524304 | tf_op jit(solution)/shard_map/reduce_scatter | solution.py:29
  429.6 13.8 %all-gather.41.cloned.1.call-done = bf16[256,2048]{1,0:T(8,128)(2,1)} async-done(((bf16[64,2048]{1,0:T(8,128)(2,1)}), bf16[256,2048]{1,0:T(8,128)(2,1)}) %all-gather.41.cloned.1.call-update) | async-done | bytes 1048592 | tf_op jit(solution)/shard_map/all_gather | solution.py:25
  454.0 25.0 %reduce-scatter.34.cloned.1.call-done = f32[64,2048]{1,0:T(8,128)} async-done(((f32[256,2048]{1,0:T(8,128)}), f32[64,2048]{1,0:T(8,128)}) %reduce-scatter.34.cloned.1.call-update) | async-done | bytes 524304 | tf_op jit(solution)/shard_map/reduce_scatter | solution.py:29
  481.3 13.3 %all-gather.39.cloned.1.call-done = bf16[256,2048]{1,0:T(8,128)(2,1)} async-done(((bf16[64,2048]{1,0:T(8,128)(2,1)}), bf16[256,2048]{1,0:T(8,128)(2,1)}) %all-gather.39.cloned.1.call-update) | async-done | bytes 1048592 | tf_op jit(solution)/shard_map/all_gather | solution.py:25
  494.7 7.1 fusion.177
  501.7 8.8 all-gather.43.cloned.1.call-done
  510.5 6.1 fusion.159
  516.7 6.3 fusion.20
  529.8 7.7 fusion.108
  537.5 25.6 %reduce-scatter.36.cloned.1.call-done = f32[64,2048]{1,0:T(8,128)} async-done(((f32[256,2048]{1,0:T(8,128)}), f32[64,2048]{1,0:T(8,128)}) %reduce-scatter.36.cloned.1.call-update) | async-done | bytes 524304 | tf_op jit(solution)/shard_map/reduce_scatter | solution.py:29
  568.1 12.7 %all-gather.45.cloned.1.call-done = bf16[256,2048]{1,0:T(8,128)(2,1)} async-done(((bf16[64,2048]{1,0:T(8,128)(2,1)}), bf16[256,2048]{1,0:T(8,128)(2,1)}) %all-gather.45.cloned.1.call-update) | async-done | bytes 1048592 | tf_op jit(solution)/shard_map/all_gather | solution.py:25
  606.4 18.8 %reduce-scatter.38.cloned.1.call-done = f32[64,2048]{1,0:T(8,128)} async-done(((f32[256,2048]{1,0:T(8,128)}), f32[64,2048]{1,0:T(8,128)}) %reduce-scatter.38.cloned.1.call-update) | async-done | bytes 524304 | tf_op jit(solution)/shard_map/reduce_scatter | solution.py:29
  630.1 23.6 %reduce-scatter.24.cloned.1.call-done = f32[64,2048]{1,0:T(8,128)} async-done(((f32[256,2048]{1,0:T(8,128)}), f32[64,2048]{1,0:T(8,128)}) %reduce-scatter.24.cloned.1.call-update) | async-done | bytes 524304 | tf_op jit(solution)/shard_map/reduce_scatter | solution.py:29
  655.9 13.7 %all-gather.49.cloned.1.call-done = bf16[256,2048]{1,0:T(8,128)(2,1)} async-done(((bf16[64,2048]{1,0:T(8,128)(2,1)}), bf16[256,2048]{1,0:T(8,128)(2,1)}) %all-gather.49.cloned.1.call-update) | async-done | bytes 1048592 | tf_op jit(solution)/shard_map/all_gather | solution.py:25
  679.7 7.8 convert_bitcast_fusion.3
  704.1 7.1 fusion.180
  716.3 12.2 %fusion.2 = f32[256,2048]{1,0:T(8,128)} fusion(bf16[3,2048,2048]{2,1,0:T(8,128)(2,1)} %param.17, bf16[256,2048]{1,0:T(8,128)(2,1)S(1)} %copy-done.44, bf16[3,2048,2048]{2,1,0:T(8,128)(2,1)} %param.16, bf16[256,2048]{1,0:T(8,128)(2,1)} %fusion.180), kind=kOutput, calls=%fused_computation.6 | convolution fusion | flops 4299685888 | bytes 20971520 | tf_op jit(solution)/shard_map/dot_general | solution.py:62
  735.1 9.8 %all-gather.51.cloned.1.call-done = bf16[256,2048]{1,0:T(8,128)(2,1)} async-done(((bf16[64,2048]{1,0:T(8,128)(2,1)}), bf16[256,2048]{1,0:T(8,128)(2,1)}) %all-gather.51.cloned.1.call-update) | async-done | bytes 1048592 | tf_op jit(solution)/shard_map/all_gather | solution.py:25
  744.9 6.1 fusion.135
  751.0 6.1 fusion.150
  757.2 6.3 fusion.36
  763.5 7.7 fusion.105
  816.5 33.6 %pad_maximum_fusion = (bf16[3,2048,2048]{2,1,0:T(8,128)(2,1)}, bf16[3,2048,2048]{2,1,0:T(8,128)(2,1)}) fusion(bf16[1,2048,2048]{2,1,0:T(8,128)(2,1)} %convert_bitcast_fusion.6, bf16[1,2048,2048]{2,1,0:T(8,128)(2,1)} %convert_bitcast_fusion.7, bf16[1,2048,2048]{2,1,0:T(8,128)(2,1)} %convert_bitcast_fusion.8, bf16[1,2048,2048]{2,1,0:T(8,128)(2,1)} %convert_bitcast_fusion.3, ...), kind=kLoop, calls=%fused_computation | loop fusion | flops 50331648 | bytes 100663296 | tf_op jit(solution)/shard_map/stack | solution.py:124
  850.1 7.9 convert_bitcast_fusion.2
  871.1 20.8 %pad_maximum_fusion.2 = bf16[3,2048,2048]{2,1,0:T(8,128)(2,1)} fusion(bf16[1,2048,2048]{2,1,0:T(8,128)(2,1)} %convert_bitcast_fusion, bf16[1,2048,2048]{2,1,0:T(8,128)(2,1)} %convert_bitcast_fusion.1, bf16[1,2048,2048]{2,1,0:T(8,128)(2,1)} %convert_bitcast_fusion.2), kind=kLoop, calls=%fused_computation.2 | loop fusion | flops 25165824 | bytes 50331648 | tf_op jit(solution)/shard_map/stack | solution.py:124
  900.9 7.8 pad_maximum_fusion.3
  910.1 10.8 %psum.7 = f32[2,3,2048]{2,1,0:T(4,128)S(1)} all-reduce(f32[2,3,2048]{2,1,0:T(4,128)S(1)} %pad_maximum_fusion.8), channel_id=1, replica_groups=mesh['dp'=2,'tp'=4] {'tp'}, use_global_device_ids=true, to_apply=%region_54.55 | all-reduce | flops 12288 | bytes 98304 | tf_op jit(solution)/shard_map/psum | solution.py:125
  (362 shorter events, 246.4 us)
Async XLA Ops:
  7.2 20.6 %all-gather.19.cloned.1.call-start = ((), (), s32[]{:S(2)}) async-start(), calls=%async_computation.15 | async-start | bytes 1310720 | tf_op jit(solution)/shard_map/all_gather | solution.py:25
  8.1 24.6 %copy-start.21 = (f32[1,2048]{1,0:T(1,128)}, f32[1,2048]{1,0:T(1,128)S(1)}, u32[]{:S(2)}) copy-start(f32[1,2048]{1,0:T(1,128)S(1)} %get-tuple-element.55) | copy-start | bytes 24580
  11.1 52.1 %reduce-scatter.16.cloned.1.call-start = ((), (), s32[]{:S(2)}) async-start(), calls=%async_computation.16 | async-start | bytes 2621440 | tf_op jit(solution)/shard_map/reduce_scatter | solution.py:29
  37.5 25.7 %copy-start = (bf16[64,2048]{1,0:T(8,128)(2,1)S(1)}, bf16[64,2048]{1,0:T(8,128)(2,1)}, u32[]{:S(2)}) copy-start(bf16[64,2048]{1,0:T(8,128)(2,1)} %param.9) | copy-start | bytes 786436
  37.5 41.7 %all-gather.21.cloned.1.call-start = ((), (), s32[]{:S(2)}) async-start(), calls=%async_computation.17 | async-start | bytes 1310720 | tf_op jit(solution)/shard_map/all_gather | solution.py:25
  38.3 47.0 %copy-start.24 = (f32[1,2048]{1,0:T(1,128)}, f32[1,2048]{1,0:T(1,128)S(1)}, u32[]{:S(2)}) copy-start(f32[1,2048]{1,0:T(1,128)S(1)} %get-tuple-element.52) | copy-start | bytes 24580
  65.3 57.7 %reduce-scatter.18.cloned.1.call-start = ((), (), s32[]{:S(2)}) async-start(), calls=%async_computation.18 | async-start | bytes 2621440 | tf_op jit(solution)/shard_map/reduce_scatter | solution.py:29
  97.3 41.7 %all-gather.23.cloned.1.call-start = ((), (), s32[]{:S(2)}) async-start(), calls=%async_computation.19 | async-start | bytes 1310720 | tf_op jit(solution)/shard_map/all_gather | solution.py:25
  125.1 49.3 %reduce-scatter.20.cloned.1.call-start = ((), (), s32[]{:S(2)}) async-start(), calls=%async_computation.20 | async-start | bytes 2621440 | tf_op jit(solution)/shard_map/reduce_scatter | solution.py:29
  148.7 41.7 %all-gather.25.cloned.1.call-start = ((), (), s32[]{:S(2)}) async-start(), calls=%async_computation.21 | async-start | bytes 1310720 | tf_op jit(solution)/shard_map/all_gather | solution.py:25
  176.5 57.6 %reduce-scatter.22.cloned.1.call-start = ((), (), s32[]{:S(2)}) async-start(), calls=%async_computation.22 | async-start | bytes 2621440 | tf_op jit(solution)/shard_map/reduce_scatter | solution.py:29
  208.4 41.8 %all-gather.33.cloned.1.call-start = ((), (), s32[]{:S(2)}) async-start(), calls=%async_computation.28 | async-start | bytes 1310720 | tf_op jit(solution)/shard_map/all_gather | solution.py:25
  236.3 49.4 %reduce-scatter.28.cloned.1.call-start = ((), (), s32[]{:S(2)}) async-start(), calls=%async_computation.29 | async-start | bytes 2621440 | tf_op jit(solution)/shard_map/reduce_scatter | solution.py:29
  260.1 40.9 %all-gather.31.cloned.1.call-start = ((), (), s32[]{:S(2)}) async-start(), calls=%async_computation.27 | async-start | bytes 1310720 | tf_op jit(solution)/shard_map/all_gather | solution.py:25
  260.8 55.9 %all-gather.35.cloned.1.call-start = ((), (), s32[]{:S(2)}) async-start(), calls=%async_computation.30 | async-start | bytes 1310720 | tf_op jit(solution)/shard_map/all_gather | solution.py:25
  287.8 81.5 %reduce-scatter.30.cloned.1.call-start = ((), (), s32[]{:S(2)}) async-start(), calls=%async_computation.31 | async-start | bytes 2621440 | tf_op jit(solution)/shard_map/reduce_scatter | solution.py:29
  343.6 27.5 %copy-start.12 = (bf16[64,2048]{1,0:T(8,128)(2,1)S(1)}, bf16[64,2048]{1,0:T(8,128)(2,1)}, u32[]{:S(2)}) copy-start(bf16[64,2048]{1,0:T(8,128)(2,1)} %param.10) | copy-start | bytes 786436
  343.6 43.3 %all-gather.37.cloned.1.call-start = ((), (), s32[]{:S(2)}) async-start(), calls=%async_computation.32 | async-start | bytes 1310720 | tf_op jit(solution)/shard_map/all_gather | solution.py:25
  373.1 51.0 %reduce-scatter.32.cloned.1.call-start = ((), (), s32[]{:S(2)}) async-start(), calls=%async_computation.33 | async-start | bytes 2621440 | tf_op jit(solution)/shard_map/reduce_scatter | solution.py:29
  398.4 28.3 %copy-start.8 = (bf16[64,2048]{1,0:T(8,128)(2,1)S(1)}, bf16[64,2048]{1,0:T(8,128)(2,1)}, u32[]{:S(2)}) copy-start(bf16[64,2048]{1,0:T(8,128)(2,1)} %fusion.389) | copy-start | bytes 786436
  398.4 45.1 %all-gather.41.cloned.1.call-start = ((), (), s32[]{:S(2)}) async-start(), calls=%async_computation.35 | async-start | bytes 1310720 | tf_op jit(solution)/shard_map/all_gather | solution.py:25
  429.6 49.4 %reduce-scatter.34.cloned.1.call-start = ((), (), s32[]{:S(2)}) async-start(), calls=%async_computation.36 | async-start | bytes 2621440 | tf_op jit(solution)/shard_map/reduce_scatter | solution.py:29
  453.3 41.4 %all-gather.39.cloned.1.call-start = ((), (), s32[]{:S(2)}) async-start(), calls=%async_computation.34 | async-start | bytes 1310720 | tf_op jit(solution)/shard_map/all_gather | solution.py:25
  453.9 56.6 %all-gather.43.cloned.1.call-start = ((), (), s32[]{:S(2)}) async-start(), calls=%async_computation.37 | async-start | bytes 1310720 | tf_op jit(solution)/shard_map/all_gather | solution.py:25
  481.1 82.0 %reduce-scatter.36.cloned.1.call-start = ((), (), s32[]{:S(2)}) async-start(), calls=%async_computation.38 | async-start | bytes 2621440 | tf_op jit(solution)/shard_map/reduce_scatter | solution.py:29
  537.4 27.5 %copy-start.7 = (bf16[64,2048]{1,0:T(8,128)(2,1)S(1)}, bf16[64,2048]{1,0:T(8,128)(2,1)}, u32[]{:S(2)}) copy-start(bf16[64,2048]{1,0:T(8,128)(2,1)} %fusion.388) | copy-start | bytes 786436
  537.5 43.3 %all-gather.45.cloned.1.call-start = ((), (), s32[]{:S(2)}) async-start(), calls=%async_computation.39 | async-start | bytes 1310720 | tf_op jit(solution)/shard_map/all_gather | solution.py:25
  566.9 29.7 %all-gather.27.cloned.1.call-start = ((), (), s32[]{:S(2)}) async-start(), calls=%async_computation.23 | async-start | bytes 1310720 | tf_op jit(solution)/shard_map/all_gather | solution.py:25
  567.7 57.6 %reduce-scatter.38.cloned.1.call-start = ((), (), s32[]{:S(2)}) async-start(), calls=%async_computation.40 | async-start | bytes 2621440 | tf_op jit(solution)/shard_map/reduce_scatter | solution.py:29
  592.2 61.5 %reduce-scatter.24.cloned.1.call-start = ((), (), s32[]{:S(2)}) async-start(), calls=%async_computation.24 | async-start | bytes 2621440 | tf_op jit(solution)/shard_map/reduce_scatter | solution.py:29
  606.4 20.7 %copy-start.6 = (bf16[64,2048]{1,0:T(8,128)(2,1)S(1)}, bf16[64,2048]{1,0:T(8,128)(2,1)}, u32[]{:S(2)}) copy-start(bf16[64,2048]{1,0:T(8,128)(2,1)} %fusion.387) | copy-start | bytes 786436
  606.4 22.7 %copy-start.1 = (bf16[64,2048]{1,0:T(8,128)(2,1)S(1)}, bf16[64,2048]{1,0:T(8,128)(2,1)}, u32[]{:S(2)}) copy-start(bf16[64,2048]{1,0:T(8,128)(2,1)} %param.9) | copy-start | bytes 786436
  606.4 22.8 %copy-start.22 = (f32[1,2048]{1,0:T(1,128)S(1)}, f32[1,2048]{1,0:T(1,128)}, u32[]{:S(2)}) copy-start(f32[1,2048]{1,0:T(1,128)} %copy-done.21) | copy-start | bytes 24580
  606.4 63.2 %all-gather.49.cloned.1.call-start = ((), (), s32[]{:S(2)}) async-start(), calls=%async_computation.42 | async-start | bytes 1310720 | tf_op jit(solution)/shard_map/all_gather | solution.py:25
  629.2 45.3 %copy-start.33 = (f32[64]{0:T(128)}, f32[64]{0:T(128)S(1)}, u32[]{:S(2)}) copy-start(f32[64]{0:T(128)S(1)} %fusion.368) | copy-start | bytes 772
  629.2 45.3 %copy-start.31 = (f32[64]{0:T(128)}, f32[64]{0:T(128)S(1)}, u32[]{:S(2)}) copy-start(f32[64]{0:T(128)S(1)} %fusion.400) | copy-start | bytes 772
  630.1 74.0 %all-gather.29.cloned.1.call-start = ((), (), s32[]{:S(2)}) async-start(), calls=%async_computation.25 | async-start | bytes 1310720 | tf_op jit(solution)/shard_map/all_gather | solution.py:25
  655.8 57.9 %reduce-scatter.40.cloned.1.call-start = ((), (), s32[]{:S(2)}) async-start(), calls=%async_computation.43 | async-start | bytes 2621440 | tf_op jit(solution)/shard_map/reduce_scatter | solution.py:29
  679.5 49.5 %all-gather.47.cloned.1.call-start = ((), (), s32[]{:S(2)}) async-start(), calls=%async_computation.41 | async-start | bytes 1310720 | tf_op jit(solution)/shard_map/all_gather | solution.py:25
  704.0 40.9 %all-gather.51.cloned.1.call-start = ((), (), s32[]{:S(2)}) async-start(), calls=%async_computation.44 | async-start | bytes 1310720 | tf_op jit(solution)/shard_map/all_gather | solution.py:25
  715.9 75.5 %reduce-scatter.26.cloned.1.call-start = ((), (), s32[]{:S(2)}) async-start(), calls=%async_computation.26 | async-start | bytes 2621440 | tf_op jit(solution)/shard_map/reduce_scatter | solution.py:29
  728.5 84.6 %reduce-scatter.42.cloned.1.call-start = ((), (), s32[]{:S(2)}) async-start(), calls=%async_computation.45 | async-start | bytes 2621440 | tf_op jit(solution)/shard_map/reduce_scatter | solution.py:29
  735.1 28.4 %copy-start.59 = (bf16[256,2048]{1,0:T(8,128)(2,1)}, bf16[256,2048]{1,0:T(8,128)(2,1)S(1)}, u32[]{:S(2)}) copy-start(bf16[256,2048]{1,0:T(8,128)(2,1)S(1)} %fusion.153) | copy-start | bytes 3145732
  771.2 86.9 %all-gather.53.cloned.1.call-start = ((), (), s32[]{:S(2)}) async-start(), calls=%async_computation.46 | async-start | bytes 1310720 | tf_op jit(solution)/shard_map/all_gather | solution.py:25
  816.5 92.2 %reduce-scatter.44.cloned.1.call-start = ((), (), s32[]{:S(2)}) async-start(), calls=%async_computation.47 | async-start | bytes 2621440 | tf_op jit(solution)/shard_map/reduce_scatter | solution.py:29
  871.1 20.8 %copy-start.11 = (bf16[256,2048]{1,0:T(8,128)(2,1)S(1)}, bf16[256,2048]{1,0:T(8,128)(2,1)}, u32[]{:S(2)}) copy-start(bf16[256,2048]{1,0:T(8,128)(2,1)} %all-gather.53.cloned.1.call-done) | copy-start | bytes 3145732
  871.1 20.8 %copy-start.16 = (bf16[4,128,256]{2,1,0:T(8,128)(2,1)S(1)}, bf16[4,128,256]{2,1,0:T(8,128)(2,1)}, u32[]{:S(2)}) copy-start(bf16[4,128,256]{2,1,0:T(8,128)(2,1)} %copy-done.15) | copy-start | bytes 786436
  900.9 20.8 %copy-start.5 = (bf16[64,2048]{1,0:T(8,128)(2,1)S(1)}, bf16[64,2048]{1,0:T(8,128)(2,1)}, u32[]{:S(2)}) copy-start(bf16[64,2048]{1,0:T(8,128)(2,1)} %fusion.385) | copy-start | bytes 786436
  (56 other events, 337.9 us)
Sparse Core Ops, SparseCore 0:
  11.2 16.5 all-gather.18
  37.6 25.5 reduce-scatter.15
  65.4 13.7 all-gather.20
  97.4 25.5 reduce-scatter.17
  125.2 13.7 all-gather.22
  148.8 25.5 reduce-scatter.19
  176.6 13.7 all-gather.24
  208.5 25.5 reduce-scatter.21
  236.5 13.7 all-gather.32
  260.2 25.4 reduce-scatter.27
  287.2 13.7 all-gather.30
  303.0 13.7 all-gather.34
  343.7 25.5 reduce-scatter.29
  373.2 13.7 all-gather.36
  398.5 25.4 reduce-scatter.31
  429.7 13.7 all-gather.40
  453.4 25.4 reduce-scatter.33
  480.9 13.7 all-gather.38
  496.8 13.7 all-gather.42
  537.6 25.5 reduce-scatter.35
  567.0 13.7 all-gather.44
  582.9 13.7 all-gather.26
  599.7 25.5 reduce-scatter.37
  628.2 25.4 reduce-scatter.23
  655.8 13.7 all-gather.48
  671.5 13.7 all-gather.28
  688.2 25.5 reduce-scatter.39
  715.3 13.6 all-gather.46
  731.1 13.7 all-gather.50
  747.8 25.5 reduce-scatter.25
  776.4 25.5 reduce-scatter.41
  816.6 13.7 all-gather.52
  871.2 25.4 reduce-scatter.43
where the time goes:
time: 940 us; the launch traced here: 931 us
  waiting for transfers between devices  460 us (49%)
  matrix products  314 us (33%)
  other arithmetic  114 us (12%)
  between operations  16.2 us (2%)
  local copies, waits for them, and re-layouts  13 us (1%)
  blocking collectives  10.8 us (1%)
    reduce_scatter x15, waiting for transfers between devices, scatter_rows(): lax.psum_scatter(part_sum, 'tp', scatter_dimension=0, tiled=True)  274 us
    all_gather x18, waiting for transfers between devices, gather_rows(): return lax.all_gather(row_shard, 'tp', axis=0, tiled=True)  184 us
    dot_general x54, matrix products, contract(): jnp.einsum(eq_form, left_op, right_op, preferred_element_type=jnp.float32)  171 us
    another operation x4, other arithmetic, device_step(): jnp.stack([grads[kind_idx] for grads in layer_grads])  65.6 us
    dot_general x6, matrix products, mlp_core(): jnp.dot(full_mid, w_gate, preferred_element_type=jnp.float32)  37.7 us
    dot_general x3, matrix products, layer_forward(): jnp.dot(mlp_parts[2], w_down, preferred_element_type=jnp.float32)  36 us
    dot_general x6, matrix products, attention_core(): jnp.dot(full_in, w_qkv, preferred_element_type=jnp.float32)  29.4 us
    dot_general x6, matrix products, layer_forward(): jnp.dot(attn_parts[5], w_out, preferred_element_type=jnp.float32)  22.1 us
  transfers between devices with their start and end apart: 33, of which 28 were waited for; matrix products, arithmetic and copies ran while one was open for 27% of the time, Pallas kernels for 0%

commit v1 on v0

v1 whole, which is shorter than its diff:
```python
import functools

import jax
import jax.numpy as jnp
from jax import lax
from jax.experimental import pallas as pl
from jax.experimental.pallas import tpu as pltpu
from jax.sharding import PartitionSpec as P

HEAD = 128
EPS = 1e-5
MESH = pl.DeviceIdType.MESH
F32 = jnp.float32
BF16 = jnp.bfloat16
VMEM_LIMIT = 66_000_000

D = 2048
S = 256
R = 64
NQ = 1536
NO = 512
NF = 2048
HEADS = 4
LAYERS = 3

AC = 4
AW = D // AC
RC = 4
RW = D // RC


def dot(a, b):
    return jnp.dot(a, b, preferred_element_type=F32)


def dot_nt(a, b):
    return lax.dot_general(a, b, (((1,), (1,)), ((), ())), preferred_element_type=F32)


def dot_tn(a, b):
    return lax.dot_general(a, b, (((0,), (0,)), ((), ())), preferred_element_type=F32)


def ds(i, n):
    return pl.ds(i * n if isinstance(i, int) else pl.multiple_of(i * n, n), n)


def loop(n, body):
    lax.fori_loop(0, n, lambda i, c: (body(i), c)[1], 0)


class Peers:
    def __init__(self):
        self.me = lax.axis_index("tp")
        core, chip = lax.rem(self.me, 2), self.me // 2
        self.sib = chip * 2 + (1 - core)
        self.cross = (1 - chip) * 2 + core
        self.diag = (1 - chip) * 2 + (1 - core)

    def barrier(self):
        sem = pltpu.get_barrier_semaphore()
        for peer in (self.sib, self.cross):
            pl.semaphore_signal(sem, inc=1, device_id={"tp": peer}, device_id_type=MESH)
        pl.semaphore_wait(sem, 2)


def remote(src, dst, send, recv, peer):
    return pltpu.make_async_remote_copy(
        src_ref=src, dst_ref=dst, send_sem=send, recv_sem=recv, device_id={"tp": peer}, device_id_type=MESH
    )


class Gather:
    def __init__(self, p, buf, send, recv, which):
        self.p, self.buf, self.send, self.recv, self.which = p, buf, send, recv, which

    def _copy(self, kind, chunk, owner, peer):
        part = self.buf.at[ds(owner, R), ds(chunk, AW)]
        return remote(part, part, self.send.at[self.which, kind, chunk], self.recv.at[self.which, kind, chunk], peer)

    def to_cross(self, chunk):
        self._copy(0, chunk, self.p.me, self.p.cross).start()

    def to_sib(self, chunk):
        self._copy(1, chunk, self.p.me, self.p.sib).start()

    def relay(self, chunk):
        self._copy(0, chunk, self.p.cross, self.p.cross).wait_recv()
        self._copy(2, chunk, self.p.cross, self.p.sib).start()

    def arrived(self, chunk):
        self._copy(1, chunk, self.p.sib, self.p.sib).wait_recv()
        self._copy(2, chunk, self.p.diag, self.p.sib).wait_recv()

    def start(self):
        for chunk in range(AC):
            self.to_cross(chunk)
        for chunk in range(AC):
            self.to_sib(chunk)

    def each(self, body):
        for chunk in range(AC + 1):
            if chunk < AC:
                self.relay(chunk)
            if chunk > 0:
                self.arrived(chunk - 1)
                body(chunk - 1)

    def finish(self):
        for chunk in range(AC):
            self._copy(0, chunk, self.p.me, self.p.cross).wait_send()
            self._copy(1, chunk, self.p.me, self.p.sib).wait_send()
            self._copy(2, chunk, self.p.cross, self.p.sib).wait_send()


class Scatter:
    def __init__(self, p, part, near, out, far, send, recv):
        self.p, self.part, self.near, self.out, self.far, self.send, self.recv = p, part, near, out, far, send, recv

    def _near(self, kind, chunk):
        owner = self.p.diag if kind == 0 else self.p.sib
        return remote(
            self.part.at[ds(owner, R), ds(chunk, RW)],
            self.near.at[kind, :, ds(chunk, RW)],
            self.send.at[kind, chunk],
            self.recv.at[kind, chunk],
            self.p.sib,
        )

    def _far(self, chunk):
        return remote(
            self.out.at[:, ds(chunk, RW)],
            self.far.at[:, ds(chunk, RW)],
            self.send.at[2, chunk],
            self.recv.at[2, chunk],
            self.p.cross,
        )

    def _mid(self, chunk):
        self._near(0, chunk).wait_recv()
        cols = ds(chunk, RW)
        self.out[:, cols] = (self.part[ds(self.p.cross, R), cols] + self.near[0, :, cols]).astype(BF16)
        self._far(chunk).start()

    def run(self, compute):
        def step(chunk):
            self.part[:, ds(chunk, RW)] = compute(chunk)
            self._near(0, chunk).start()
            self._near(1, chunk).start()

            @pl.when(chunk > 0)
            def _():
                self._mid(chunk - 1)

        loop(RC, step)
        self._mid(RC - 1)

    def result(self):
        for chunk in range(RC):
            self._near(1, chunk).wait_recv()
            self._far(chunk).wait_recv()
        total = self.part[ds(self.p.me, R), :] + self.near[1] + self.far[...].astype(F32)
        for chunk in range(RC):
            self._near(0, chunk).wait_send()
            self._near(1, chunk).wait_send()
            self._far(chunk).wait_send()
        return total.astype(BF16)


def norm(h, gain):
    hf = h.astype(F32)
    inv = lax.rsqrt(jnp.mean(hf * hf, axis=-1, keepdims=True) + EPS)
    return (hf * inv * gain).astype(BF16)


def norm_back(h, gain, dy):
    hf, dyf = h.astype(F32), dy.astype(F32)
    inv = lax.rsqrt(jnp.mean(hf * hf, axis=-1, keepdims=True) + EPS)
    dgain = jnp.sum(dyf * (hf * inv), axis=0, keepdims=True)
    dn = dyf * gain
    slope = jnp.sum(dn * hf, axis=-1, keepdims=True) * (inv * inv * inv) / D
    return (dn * inv - hf * slope).astype(BF16), dgain


def softmax_scores(q, k):
    scores = dot_nt(q, k) * HEAD**-0.5
    rows = lax.broadcasted_iota(jnp.int32, (S, S), 0)
    cols = lax.broadcasted_iota(jnp.int32, (S, S), 1)
    scores = jnp.where(rows >= cols, scores, -1e30)
    e = jnp.exp(scores - jnp.max(scores, axis=-1, keepdims=True))
    return e / jnp.sum(e, axis=-1, keepdims=True)


def head_cols(head, which):
    return pl.ds(pl.multiple_of(head * 3 * HEAD + which * HEAD, HEAD), HEAD)


def attention(qkv, o, probs=None):
    def one(head):
        prob = softmax_scores(qkv[:, head_cols(head, 0)], qkv[:, head_cols(head, 1)])
        if probs is not None:
            probs[head] = prob
        o[:, ds(head, HEAD)] = dot(prob.astype(BF16), qkv[:, head_cols(head, 2)]).astype(BF16)

    loop(HEADS, one)


def qkv_chunk(u, wq, acc, qkv, tile=768):
    def body(chunk):
        def one(j):
            cols = ds(j, tile)
            part = dot(u[:, ds(chunk, AW)], wq[ds(chunk, AW), cols])
            if chunk > 0:
                part = part + acc[:, cols]
            if chunk < AC - 1:
                acc[:, cols] = part
            else:
                qkv[:, cols] = part.astype(BF16)

        loop(NQ // tile, one)

    return body


def mlp_chunk(n, wg, wu, acc1, acc3, last, tile=512):
    def body(chunk):
        def one(j):
            cols = ds(j, tile)
            z1 = dot(n[:, ds(chunk, AW)], wg[ds(chunk, AW), cols])
            z3 = dot(n[:, ds(chunk, AW)], wu[ds(chunk, AW), cols])
            if chunk > 0:
                z1, z3 = z1 + acc1[:, cols], z3 + acc3[:, cols]
            if chunk < AC - 1:
                acc1[:, cols] = z1
                acc3[:, cols] = z3
            else:
                last(cols, z1.astype(BF16).astype(F32), z3.astype(BF16).astype(F32))

        loop(NF // tile, one)

    return body


def forward_kernel(x, ga, gm, wq_h, wo_h, wg_h, wu_h, wd_h, hs,
                   wq, wo, wg, wu, wd, h, u, n, acc1, acc3, qkv, o, m, part, near, out, far,
                   wsem, gsend, grecv, ssend, srecv):
    p = Peers()
    pairs = ((wq_h, wq), (wo_h, wo), (wg_h, wg), (wu_h, wu), (wd_h, wd))

    def load(i, layer):
        return pltpu.make_async_copy(pairs[i][0].at[layer], pairs[i][1], wsem.at[i])

    for i in range(5):
        load(i, 0).start()
    h[...] = x[...]
    p.barrier()
    mine = ds(p.me, R)

    def layer_step(layer):
        def refill(i):
            @pl.when(layer < LAYERS - 1)
            def _():
                load(i, layer + 1).start()

        u[mine, :] = norm(h[...], ga[pl.ds(layer, 1), :])
        gather = Gather(p, u, gsend, grecv, 0)
        gather.start()
        load(0, layer).wait()
        gather.each(qkv_chunk(u, wq, acc1, qkv))
        gather.finish()
        refill(0)
        attention(qkv, o)
        load(1, layer).wait()
        scatter = Scatter(p, part, near, out, far, ssend, srecv)
        scatter.run(lambda c: dot(o[...], wo[:, ds(c, RW)]))
        refill(1)
        h[...] = h[...] + scatter.result()

        n[mine, :] = norm(h[...], gm[pl.ds(layer, 1), :])
        gather = Gather(p, n, gsend, grecv, 0)
        gather.start()
        load(2, layer).wait()
        load(3, layer).wait()

        def last(cols, z1, z3):
            m[:, cols] = (z1 * jax.nn.sigmoid(z1) * z3).astype(BF16)

        gather.each(mlp_chunk(n, wg, wu, acc1, acc3, last))
        gather.finish()
        refill(2)
        refill(3)
        load(4, layer).wait()
        scatter.run(lambda c: dot(m[...], wd[:, ds(c, RW)]))
        refill(4)
        h[...] = h[...] + scatter.result()
        hs[layer] = h[...]

    loop(LAYERS, layer_step)


def backward_kernel(layer, hin, dy, gin, ga, gm, wq_h, wo_h, wg_h, wu_h, wd_h, *refs):
    last_call = layer == 0
    refs = list(refs)
    take = lambda k: [refs.pop(0) for _ in range(k)]
    (dx,) = take(1)
    gouts = take(2 if last_call else 1)
    saved_h = take(9)
    u, dqkv, o, da, n, dg, du, m, dd = saved = take(9)
    wq, wo, wg, wu, wd = take(5)
    hm, acc1, acc3, qkv, probs, dgated, dh, part, near, out, far, gbuf = take(12)
    gmid, gfar = take(2)
    wsem, osem, gsend, grecv, ssend, srecv, rsend, rrecv = take(8)

    p = Peers()
    pairs = ((wq_h, wq), (wo_h, wo), (wg_h, wg), (wu_h, wu), (wd_h, wd))
    loads = [pltpu.make_async_copy(src.at[layer], dst, wsem.at[i]) for i, (src, dst) in enumerate(pairs)]
    saves = [pltpu.make_async_copy(src, dst, osem.at[i]) for i, (src, dst) in enumerate(zip(saved, saved_h))]
    for i in (0, 1, 4, 2, 3):
        loads[i].start()
    mine = ds(p.me, R)
    h = hin[layer - 1] if layer > 0 else hin[...]
    gain_a, gain_m = ga[pl.ds(layer, 1), :], gm[pl.ds(layer, 1), :]
    u[mine, :] = norm(h, gain_a)
    dd[mine, :] = dy[...]
    p.barrier()
    gu = Gather(p, u, gsend, grecv, 0)
    gd = Gather(p, dd, gsend, grecv, 1)
    gu.start()
    for c in range(AC):
        gd.to_sib(c)
    for c in range(AC // 2):
        gd.to_cross(c)

    loads[0].wait()
    gu.each(qkv_chunk(u, wq, acc1, qkv))
    saves[0].start()
    attention(qkv, o, probs)
    saves[2].start()
    loads[1].wait()
    scatter = Scatter(p, part, near, out, far, ssend, srecv)
    scatter.run(lambda c: dot(o[...], wo[:, ds(c, RW)]))
    for c in range(AC // 2, AC):
        gd.to_cross(c)
    for c in range(AC // 2):
        gd.relay(c)
    h_mid = h + scatter.result()
    hm[...] = h_mid
    n[mine, :] = norm(h_mid, gain_m)
    gn = Gather(p, n, gsend, grecv, 2)
    gn.start()

    for c in range(AC // 2, AC):
        gd.relay(c)
    for c in range(AC):
        gd.arrived(c)
    saves[8].start()
    loads[4].wait()

    def gated(j):
        dgated[:, ds(j, 512)] = dot_nt(dd[...], wd[ds(j, 512), :]).astype(BF16)

    loop(NF // 512, gated)
    loads[2].wait()
    loads[3].wait()

    def last(cols, z1, z3):
        sig = jax.nn.sigmoid(z1)
        silu = z1 * sig
        dm = dgated[:, cols].astype(F32)
        m[:, cols] = (silu * z3).astype(BF16)
        du[:, cols] = (dm * silu).astype(BF16)
        dg[:, cols] = (dm * z3 * (sig + silu * (1.0 - sig))).astype(BF16)

    gn.each(mlp_chunk(n, wg, wu, acc1, acc3, last))
    for i in (4, 5, 6, 7):
        saves[i].start()

    scatter.run(lambda c: dot_nt(dg[...], wg[ds(c, RW), :]) + dot_nt(du[...], wu[ds(c, RW), :]))
    d_norm, dgain_m = norm_back(hm[...], gain_m, scatter.result())
    d_mid = dy[...] + d_norm
    da[mine, :] = d_mid
    ga_ = Gather(p, da, gsend, grecv, 3)
    ga_.start()
    gbuf[...] = gin[...]
    gbuf[pl.ds(LAYERS + layer, 1), :] = dgain_m

    def heads_chunk(chunk):
        part_h = dot_nt(da[:, ds(chunk, AW)], wo[:, ds(chunk, AW)])
        if chunk > 0:
            part_h = part_h + acc1[:, :NO]
        if chunk < AC - 1:
            acc1[:, :NO] = part_h
        else:
            dh[...] = part_h.astype(BF16)

    ga_.each(heads_chunk)
    saves[3].start()

    def back(head):
        prob = probs[head]
        d_o = dh[:, ds(head, HEAD)]
        q, k, v = (qkv[:, head_cols(head, i)] for i in range(3))
        d_prob = dot_nt(d_o, v)
        d_scores = (prob * (d_prob - jnp.sum(d_prob * prob, axis=-1, keepdims=True)) * HEAD**-0.5).astype(BF16)
        dqkv[:, head_cols(head, 0)] = dot(d_scores, k).astype(BF16)
        dqkv[:, head_cols(head, 1)] = dot_tn(d_scores, q).astype(BF16)
        dqkv[:, head_cols(head, 2)] = dot_tn(prob.astype(BF16), d_o).astype(BF16)

    loop(HEADS, back)
    saves[1].start()
    scatter.run(lambda c: dot_nt(dqkv[...], wq[ds(c, RW), :]))
    d_norm, dgain_a = norm_back(h, gain_a, scatter.result())
    dx[...] = da[mine, :] + d_norm
    gbuf[pl.ds(layer, 1), :] = dgain_a

    if last_call:
        near_g = remote(gbuf, gmid, rsend.at[0], rrecv.at[0], p.sib)
        near_g.start()
        near_g.wait()
        gbuf[...] = gbuf[...] + gmid[...]
        far_g = remote(gbuf, gfar, rsend.at[1], rrecv.at[1], p.cross)
        far_g.start()
        far_g.wait()
        total = gbuf[...] + gfar[...]
        gouts[0][...] = total[:LAYERS]
        gouts[1][...] = total[LAYERS:2 * LAYERS]
    else:
        gouts[0][...] = gbuf[...]
    for g in (gu, gd, gn, ga_):
        g.finish()
    for save in saves:
        save.wait()


def wgrad_kernel(layer, n_alias, u_h, dqkv_h, o_h, da_h, n_h, dg_h, du_h, m_h, dd_h, *refs):
    refs = list(refs[n_alias:])
    take = lambda k: [refs.pop(0) for _ in range(k)]
    outs = take(5)
    u, dqkv, o, da, n, dg, du, m, dd = acts = take(9)
    stages = take(5)
    isem, osem = take(2)
    loads = [pltpu.make_async_copy(src, dst, isem.at[i])
             for i, (src, dst) in enumerate(zip((u_h, dqkv_h, o_h, da_h, n_h, dg_h, du_h, m_h, dd_h), acts))]
    order = (0, 1, 4, 5, 6, 7, 8, 2, 3)
    for i in order:
        loads[i].start()
    work = ((0, 0, 1), (2, 4, 5), (3, 4, 6), (4, 7, 8), (1, 2, 3))
    waited = set()
    for out_i, a_i, b_i in work:
        for i in (a_i, b_i):
            if i not in waited:
                loads[i].wait()
                waited.add(i)
        a, b, out, stage = acts[a_i], acts[b_i], outs[out_i], stages[out_i]
        tiles, cols = a.shape[1] // S, b.shape[1]

        def copy(i, slot):
            return pltpu.make_async_copy(stage.at[slot], out.at[layer, ds(i, S), :], osem.at[out_i, slot])

        def step(i):
            slot = lax.rem(i, 2)

            @pl.when(i >= 2)
            def _():
                copy(i - 2, slot).wait()

            lhs = a[:, ds(i, S)].T
            for c in range(cols // 512):
                stage[slot, :, ds(c, 512)] = dot(lhs, b[:, ds(c, 512)]).astype(BF16)
            copy(i, slot).start()

        loop(tiles, step)
    for out_i, a_i, b_i in work:
        out, stage = outs[out_i], stages[out_i]
        tiles = acts[a_i].shape[1] // S
        for i in (tiles - 2, tiles - 1):
            pltpu.make_async_copy(stage.at[i % 2], out.at[layer, ds(i, S), :], osem.at[out_i, i % 2]).wait()


def vmem():
    return pl.BlockSpec(memory_space=pltpu.VMEM)


def hbm():
    return pl.BlockSpec(memory_space=pl.ANY)


WEIGHT_SCRATCH = [
    pltpu.VMEM((D, NQ), BF16),
    pltpu.VMEM((NO, D), BF16),
    pltpu.VMEM((D, NF), BF16),
    pltpu.VMEM((D, NF), BF16),
    pltpu.VMEM((NF, D), BF16),
]
SCATTER_SCRATCH = [
    pltpu.VMEM((S, D), F32),
    pltpu.VMEM((2, R, D), F32),
    pltpu.VMEM((R, D), BF16),
    pltpu.VMEM((R, D), BF16),
]
SAVED = [(S, D), (S, NQ), (S, NO), (S, D), (S, D), (S, NF), (S, NF), (S, NF), (S, D)]
GRADS = [(D, NQ), (NO, D), (D, NF), (D, NF), (NF, D)]


def run_forward(x, ga, gm, weights):
    dma = pltpu.SemaphoreType.DMA
    return pl.pallas_call(
        forward_kernel,
        name="forward",
        out_shape=jax.ShapeDtypeStruct((LAYERS, R, D), BF16),
        in_specs=[vmem()] * 3 + [hbm()] * 5,
        out_specs=vmem(),
        scratch_shapes=WEIGHT_SCRATCH
        + [
            pltpu.VMEM((R, D), BF16),
            pltpu.VMEM((S, D), BF16),
            pltpu.VMEM((S, D), BF16),
            pltpu.VMEM((S, NF), F32),
            pltpu.VMEM((S, NF), F32),
            pltpu.VMEM((S, NQ), BF16),
            pltpu.VMEM((S, NO), BF16),
            pltpu.VMEM((S, NF), BF16),
        ]
        + SCATTER_SCRATCH
        + [dma((5,)), dma((1, 3, AC)), dma((1, 3, AC)), dma((3, RC)), dma((3, RC))],
        compiler_params=pltpu.CompilerParams(collective_id=0, has_side_effects=True, vmem_limit_bytes=VMEM_LIMIT),
    )(x, ga, gm, *weights)


def run_backward(layer, hin, dy, gin, ga, gm, weights):
    dma = pltpu.SemaphoreType.DMA
    last_call = layer == 0
    gshape = [jax.ShapeDtypeStruct((LAYERS, D), F32)] * 2 if last_call else [jax.ShapeDtypeStruct((8, D), F32)]
    saved = [jax.ShapeDtypeStruct(shape, BF16) for shape in SAVED]
    outs = pl.pallas_call(
        functools.partial(backward_kernel, layer),
        name=f"backward{layer}",
        out_shape=[jax.ShapeDtypeStruct((R, D), BF16)] + gshape + saved,
        in_specs=[vmem()] * 5 + [hbm()] * 5,
        out_specs=[vmem()] * (1 + len(gshape)) + [hbm()] * 9,
        scratch_shapes=[pltpu.VMEM(shape, BF16) for shape in SAVED]
        + WEIGHT_SCRATCH
        + [
            pltpu.VMEM((R, D), BF16),
            pltpu.VMEM((S, NF), F32),
            pltpu.VMEM((S, NF), F32),
            pltpu.VMEM((S, NQ), BF16),
            pltpu.VMEM((HEADS, S, S), F32),
            pltpu.VMEM((S, NF), BF16),
            pltpu.VMEM((S, NO), BF16),
        ]
        + SCATTER_SCRATCH
        + [pltpu.VMEM((8, D), F32)] * 3
        + [dma((5,)), dma((9,)), dma((4, 3, AC)), dma((4, 3, AC)), dma((3, RC)), dma((3, RC)), dma((2,)), dma((2,))],
        compiler_params=pltpu.CompilerParams(
            collective_id=1 + layer, has_side_effects=True, vmem_limit_bytes=VMEM_LIMIT
        ),
    )(hin, dy, gin, ga, gm, *weights)
    return outs[0], outs[1 : 1 + len(gshape)], outs[1 + len(gshape) :]


def run_wgrad(layer, saved, grads):
    dma = pltpu.SemaphoreType.DMA
    n_alias = len(grads)
    return pl.pallas_call(
        functools.partial(wgrad_kernel, layer, n_alias),
        name=f"wgrad{layer}",
        out_shape=[jax.ShapeDtypeStruct((LAYERS, *shape), BF16) for shape in GRADS],
        in_specs=[hbm()] * (9 + n_alias),
        out_specs=[hbm()] * 5,
        input_output_aliases={9 + i: i for i in range(n_alias)},
        scratch_shapes=[pltpu.VMEM(shape, BF16) for shape in SAVED]
        + [pltpu.VMEM((2, S, shape[1]), BF16) for shape in GRADS]
        + [dma((9,)), dma((5, 2))],
        compiler_params=pltpu.CompilerParams(vmem_limit_bytes=VMEM_LIMIT),
        cost_estimate=pl.CostEstimate(flops=8_600_000_000, bytes_accessed=42_000_000, transcendentals=0),
    )(*saved, *grads)


def solution(mesh):
    row_spec = P(("dp", "tp"), None)
    col_spec = P(None, None, "tp")
    mid_spec = P(None, "tp", None)
    in_specs = (row_spec, row_spec, P(None, None), P(None, None), col_spec, mid_spec, col_spec, col_spec, mid_spec)
    out_specs = (
        row_spec, row_spec, P("dp", None, "tp"), P("dp", "tp", None), P("dp", None, "tp"), P("dp", None, "tp"),
        P("dp", "tp", None), P("dp", None), P("dp", None),
    )

    def device_step(x, grad_y, gain_attn, gain_mlp, w_qkv, w_out, w_gate, w_up, w_down):
        weights = (w_qkv, w_out, w_gate, w_up, w_down)
        hs = run_forward(x, gain_attn, gain_mlp, weights)
        d_hidden = grad_y
        gains = [jnp.zeros((8, D), F32)]
        grads = ()
        for layer in reversed(range(LAYERS)):
            d_hidden, gains, saved = run_backward(
                layer, hs if layer > 0 else x, d_hidden, gains[0], gain_attn, gain_mlp, weights
            )
            grads = run_wgrad(layer, saved, grads)
            if layer > 0:
                d_hidden, grads = lax.optimization_barrier((d_hidden, grads))
        return (hs[LAYERS - 1], d_hidden, *grads, *gains)

    return jax.shard_map(device_step, mesh=mesh, in_specs=in_specs, out_specs=out_specs, check_vma=False)
```

time: 940 us -> 433 us (0.46); the launches traced: 931 us -> 433 us
  waiting for transfers between devices: 460 us -> 0 us
  Pallas kernels: 0 us -> 428 us
  matrix products: 314 us -> 0 us
  other arithmetic: 114 us -> 0 us
  between operations: 16.2 us -> 0.73 us
  blocking collectives: 10.8 us -> 0 us
    pallas_call x0 -> x7, Pallas kernels: none -> 428 us  [the longest x3 221 us: run_backward(): pl.pallas_call(functools.partial(backward_kernel, layer), name=f'backward...]
    dot_general x78 -> x0, matrix products: 314 us -> none  [the longest x54 171 us: contract(): jnp.einsum(eq_form, left_op, right_op, preferred_element_type=jnp.float32)]
    reduce_scatter x15 -> x0, waiting for transfers between devices: 274 us -> none  [scatter_rows(): lax.psum_scatter(part_sum, 'tp', scatter_dimension=0, tiled=True)]
    all_gather x18 -> x0, waiting for transfers between devices: 184 us -> none  [gather_rows(): return lax.all_gather(row_shard, 'tp', axis=0, tiled=True)]
    another operation x9 -> x0, other arithmetic: 66.5 us -> none  [the longest x4 65.6 us: device_step(): jnp.stack([grads[kind_idx] for grads in layer_grads])]
    reduce_sum x24 -> x0, other arithmetic: 22.9 us -> none  [the longest x12 11.3 us: rms_norm(): jnp.mean(hidden_f * hidden_f, axis=-1, keepdims=True) + NORM_EPS]
    add x7 -> x0, other arithmetic: 13.8 us -> none  [the longest x3 5.94 us: layer_backward(): d_hidden_mid = d_out + d_norm_mid]
    psum x1 -> x0, blocking collectives: 10.8 us -> none  [device_step(): gain_grads = lax.psum(jnp.stack([stacked[0], stacked[1]]), 'tp')]
  transfers between devices with their start and end apart: 33 -> 0, of which waited for: 28 -> 0; matrix products, arithmetic and copies ran while one was open for 27% -> 0% of each run, Pallas kernels for 0% -> 0%
where the time goes in v1:
time: 433 us
  Pallas kernels  428 us (99%)
    pallas_call x3, Pallas kernels, run_backward(): pl.pallas_call(functools.partial(backward_kernel, layer), name=f'backward...  221 us
    pallas_call x1, Pallas kernels, run_forward(): pl.pallas_call(forward_kernel, name='forward', out_shape=jax.ShapeDtypeSt...  135 us
    pallas_call x3, Pallas kernels, run_wgrad(): pl.pallas_call(functools.partial(wgrad_kernel, layer, n_alias), name=f'wg...  71.8 us

profile of v1, /device:TPU:0, one launch (start us, length us, event | category | flops | bytes accessed | tf_op | source)
XLA Modules:
  0.0 433.2 jit_solution(5954020532599026984)
XLA Ops:
  0.6 135.0 %forward.1.hin = bf16[3,64,2048]{2,1,0:T(8,128)(2,1)} custom-call(bf16[64,2048]{1,0:T(8,128)(2,1)} %hin.1, f32[3,2048]{1,0:T(4,128)} %ga.7, f32[3,2048]{1,0:T(4,128)} %gm.7, bf16[3,2048,1536]{2,1,0:T(8,128)(2,1)} %wq_h.7, bf16[3,512,2048]{2,1,0:T(8,128)(2,1)} %wo_h.7, bf16[3,2048,2048]{2,1,0:T(8,128)(2,1)} %wg_h.7, bf16[3,2048,2048]{2,1,0:T(8,128)(2,1)} %wu_h.7, ...), custom_call_target="tpu_custom_call" | custom-call | tf_op jit(solution)/shard_map/forward/pallas_call | solution.py:507
  135.7 1.7 slice_bitcast_fusion
  137.3 0.6 broadcast_in_dim.3.gin
  138.0 72.5 %backward2.1 = (bf16[64,2048]{1,0:T(8,128)(2,1)}, f32[8,2048]{1,0:T(8,128)}, bf16[256,2048]{1,0:T(8,128)(2,1)}, bf16[256,1536]{1,0:T(8,128)(2,1)}, bf16[256,512]...) custom-call(bf16[3,64,2048]{2,1,0:T(8,128)(2,1)} %forward.1.hin, ...), custom_call_target="tpu_custom_call" | custom-call | tf_op jit(solution)/shard_map/backward2/pallas_call | solution.py:535
  210.4 23.8 %wgrad2.1 = (bf16[3,2048,1536]{2,1,0:T(8,128)(2,1)}, bf16[3,512,2048]{2,1,0:T(8,128)(2,1)}, bf16[3,2048,2048]{2,1,0:T(8,128)(2,1)}, bf16[3,2048,2048]{2,1,0:T(8,128)(2,1)}, bf16[3,2048,2048]{2,1,0:T(8,128)(2,1)}) custom-call(bf16[256,2048]{1,0:T(8,128)(2,1)} %get-tuple-element.71.u_h, bf16[256,1536]{1,0:T(8,128)(2,1)} %get-tuple-element.72.dqkv_h, ...), custom_call_target="tpu_custom_call" | custom-call | flops 8600000512 | bytes 42000000 | tf_op jit(solution)/shard_map/wgrad2/pallas_call | solution.py:565
  234.3 72.5 %backward1.1 = (bf16[64,2048]{1,0:T(8,128)(2,1)}, f32[8,2048]{1,0:T(8,128)}, bf16[256,2048]{1,0:T(8,128)(2,1)}, bf16[256,1536]{1,0:T(8,128)(2,1)}, bf16[256,512]...) custom-call(bf16[3,64,2048]{2,1,0:T(8,128)(2,1)} %forward.1.hin, ...), custom_call_target="tpu_custom_call" | custom-call | tf_op jit(solution)/shard_map/backward1/pallas_call | solution.py:535
  306.7 24.1 %wgrad1.1 = (bf16[3,2048,1536]{2,1,0:T(8,128)(2,1)}, bf16[3,512,2048]{2,1,0:T(8,128)(2,1)}, bf16[3,2048,2048]{2,1,0:T(8,128)(2,1)}, bf16[3,2048,2048]{2,1,0:T(8,128)(2,1)}, bf16[3,2048,2048]{2,1,0:T(8,128)(2,1)}) custom-call(bf16[256,2048]{1,0:T(8,128)(2,1)} %get-tuple-element.88.u_h, ...), custom_call_target="tpu_custom_call", output_to_operand_aliasing={{0}: (9, {}), {1}: (10, {}), {2}: (11, {}), {3}: (12, {}), ... | custom-call | flops 8600000512 | bytes 42000000 | tf_op jit(solution)/shard_map/wgrad1/pallas_call | solution.py:565
  330.8 76.5 %backward0.1 = (bf16[64,2048]{1,0:T(8,128)(2,1)}, f32[3,2048]{1,0:T(4,128)}, f32[3,2048]{1,0:T(4,128)}, bf16[256,2048]{1,0:T(8,128)(2,1)}, bf16[256,1536]{1,0:T(...) custom-call(bf16[64,2048]{1,0:T(8,128)(2,1)} %hin.1, ...), custom_call_target="tpu_custom_call" | custom-call | tf_op jit(solution)/shard_map/backward0/pallas_call | solution.py:535
  407.4 0.0 copy-start
  407.4 0.0 copy-start.2
  407.4 0.0 copy-start.1
  407.4 23.9 %wgrad0.1 = (bf16[3,2048,1536]{2,1,0:T(8,128)(2,1)}, bf16[3,512,2048]{2,1,0:T(8,128)(2,1)}, bf16[3,2048,2048]{2,1,0:T(8,128)(2,1)}, bf16[3,2048,2048]{2,1,0:T(8,128)(2,1)}, bf16[3,2048,2048]{2,1,0:T(8,128)(2,1)}) custom-call(bf16[256,2048]{1,0:T(8,128)(2,1)} %get-tuple-element.110.u_h,, ...), custom_call_target="tpu_custom_call", output_to_operand_aliasing={{0}: (9, {}), {1}: (10, {}), {2}: (11, {}), {3}: (12, {}), ... | custom-call | flops 8600000512 | bytes 42000000 | tf_op jit(solution)/shard_map/wgrad0/pallas_call | solution.py:565
  431.3 0.0 copy-done
  431.3 0.7 copy.41
  432.0 0.0 copy-done.2
  432.0 0.6 copy.42
  432.6 0.0 copy-done.1
  432.6 0.6 copy.43
Async XLA Ops:
  407.4 23.9 %copy-start = (bf16[64,2048]{1,0:T(8,128)(2,1)S(1)}, bf16[64,2048]{1,0:T(8,128)(2,1)}, u32[]{:S(2)}) copy-start(bf16[64,2048]{1,0:T(8,128)(2,1)} %get-tuple-element.141) | copy-start | bytes 786436
  407.4 24.6 %copy-start.2 = (f32[3,2048]{1,0:T(4,128)S(1)}, f32[3,2048]{1,0:T(4,128)}, u32[]{:S(2)}) copy-start(f32[3,2048]{1,0:T(4,128)} %get-tuple-element.147) | copy-start | bytes 73732
  407.4 25.2 %copy-start.1 = (f32[3,2048]{1,0:T(4,128)S(1)}, f32[3,2048]{1,0:T(4,128)}, u32[]{:S(2)}) copy-start(f32[3,2048]{1,0:T(4,128)} %get-tuple-element.148) | copy-start | bytes 73732

commit v2 on v1

--- a/solution.py
+++ b/solution.py
@@ -167,6 +167,92 @@
         return total.astype(BF16)
 
 
+HR = R // 2
+HS = S // 2
+HA = 2
+HAW = D // HA
+HC = 4
+HW = D // HC
+
+
+def owned(owner, half):
+    return ds(half * 4 + owner, HR)
+
+
+class HalfGather(Gather):
+    def _copy(self, kind, item, owner, peer):
+        half, chunk = item
+        part = self.buf.at[owned(owner, half), ds(chunk, HAW)]
+        sems = (self.which, kind, half, chunk)
+        return remote(part, part, self.send.at[sems], self.recv.at[sems], peer)
+
+    def start(self, half):
+        for chunk in range(HA):
+            self.to_cross((half, chunk))
+        for chunk in range(HA):
+            self.to_sib((half, chunk))
+
+    def finish(self):
+        for half in range(2):
+            for chunk in range(HA):
+                self._copy(0, (half, chunk), self.p.me, self.p.cross).wait_send()
+                self._copy(1, (half, chunk), self.p.me, self.p.sib).wait_send()
+                self._copy(2, (half, chunk), self.p.cross, self.p.sib).wait_send()
+
+
+class HalfScatter(Scatter):
+    def _near(self, kind, half, chunk):
+        owner = self.p.diag if kind == 0 else self.p.sib
+        return remote(
+            self.part.at[owned(owner, half), ds(chunk, HW)],
+            self.near.at[kind, ds(half, HR), ds(chunk, HW)],
+            self.send.at[kind, half, chunk],
+            self.recv.at[kind, half, chunk],
+            self.p.sib,
+        )
+
+    def _far(self, half, chunk):
+        return remote(
+            self.out.at[ds(half, HR), ds(chunk, HW)],
+            self.far.at[ds(half, HR), ds(chunk, HW)],
+            self.send.at[2, half, chunk],
+            self.recv.at[2, half, chunk],
+            self.p.cross,
+        )
+
+    def run(self, half, compute):
+        def step(chunk):
+            self.part[ds(half, HS), ds(chunk, HW)] = compute(chunk)
+            self._near(0, half, chunk).start()
+            self._near(1, half, chunk).start()
+
+        def mid(chunk):
+            self._near(0, half, chunk).wait_recv()
+            cols = ds(chunk, HW)
+            total = self.part[owned(self.p.cross, half), cols] + self.near[0, ds(half, HR), cols]
+            self.out[ds(half, HR), cols] = total.astype(BF16)
+            self._far(half, chunk).start()
+
+        loop(HC, step)
+        loop(HC, mid)
+
+    def result(self, half):
+        for chunk in range(HC):
+            self._near(1, half, chunk).wait_recv()
+            self._far(half, chunk).wait_recv()
+        rows = ds(half, HR)
+        total = self.part[owned(self.p.me, half), :] + self.near[1, rows, :] + self.far[rows, :].astype(F32)
+        for chunk in range(HC):
+            self._near(0, half, chunk).wait_send()
+            self._near(1, half, chunk).wait_send()
+            self._far(half, chunk).wait_send()
+        return total.astype(BF16)
+
+
+def true_position(row):
+    return lax.rem(row, HS) // HR * R + row // HS * HR + lax.rem(row, HR)
+
+
 def norm(h, gain):
     hf = h.astype(F32)
     inv = lax.rsqrt(jnp.mean(hf * hf, axis=-1, keepdims=True) + EPS)
@@ -182,10 +268,12 @@
     return (dn * inv - hf * slope).astype(BF16), dgain
 
 
-def softmax_scores(q, k):
+def softmax_scores(q, k, halves=False):
     scores = dot_nt(q, k) * HEAD**-0.5
     rows = lax.broadcasted_iota(jnp.int32, (S, S), 0)
     cols = lax.broadcasted_iota(jnp.int32, (S, S), 1)
+    if halves:
+        rows, cols = true_position(rows), true_position(cols)
     scores = jnp.where(rows >= cols, scores, -1e30)
     e = jnp.exp(scores - jnp.max(scores, axis=-1, keepdims=True))
     return e / jnp.sum(e, axis=-1, keepdims=True)
@@ -195,9 +283,9 @@
     return pl.ds(pl.multiple_of(head * 3 * HEAD + which * HEAD, HEAD), HEAD)
 
 
-def attention(qkv, o, probs=None):
+def attention(qkv, o, probs=None, halves=False):
     def one(head):
-        prob = softmax_scores(qkv[:, head_cols(head, 0)], qkv[:, head_cols(head, 1)])
+        prob = softmax_scores(qkv[:, head_cols(head, 0)], qkv[:, head_cols(head, 1)], halves)
         if probs is not None:
             probs[head] = prob
         o[:, ds(head, HEAD)] = dot(prob.astype(BF16), qkv[:, head_cols(head, 2)]).astype(BF16)
@@ -241,6 +329,58 @@
     return body
 
 
+def half_qkv(u, wq, acc, qkv, tile=768):
+    def body(half, chunk):
+        rows, deep = ds(half, HS), ds(chunk, HAW)
+
+        def one(j):
+            cols = ds(j, tile)
+            part = dot(u[rows, deep], wq[deep, cols])
+            if chunk > 0:
+                part = part + acc[rows, cols]
+            if chunk < HA - 1:
+                acc[rows, cols] = part
+            else:
+                qkv[rows, cols] = part.astype(BF16)
+
+        loop(NQ // tile, one)
+
+    return body
+
+
+def half_mlp(n, wg, wu, acc1, acc3, last, tile=512):
+    def body(half, chunk):
+        rows, deep = ds(half, HS), ds(chunk, HAW)
+
+        def one(j):
+            cols = ds(j, tile)
+            z1 = dot(n[rows, deep], wg[deep, cols])
+            z3 = dot(n[rows, deep], wu[deep, cols])
+            if chunk > 0:
+                z1, z3 = z1 + acc1[rows, cols], z3 + acc3[rows, cols]
+            if chunk < HA - 1:
+                acc1[rows, cols] = z1
+                acc3[rows, cols] = z3
+            else:
+                last(rows, cols, z1.astype(BF16).astype(F32), z3.astype(BF16).astype(F32))
+
+        loop(NF // tile, one)
+
+    return body
+
+
+ITEMS = [(half, chunk) for half in range(2) for chunk in range(HA)]
+
+
+def in_order(gather, body):
+    for i in range(len(ITEMS) + 1):
+        if i < len(ITEMS):
+            gather.relay(ITEMS[i])
+        if i > 0:
+            gather.arrived(ITEMS[i - 1])
+            body(*ITEMS[i - 1])
+
+
 def forward_kernel(x, ga, gm, wq_h, wo_h, wg_h, wu_h, wd_h, hs,
                    wq, wo, wg, wu, wd, h, u, n, acc1, acc3, qkv, o, m, part, near, out, far,
                    wsem, gsend, grecv, ssend, srecv):
@@ -254,46 +394,77 @@
         load(i, 0).start()
     h[...] = x[...]
     p.barrier()
-    mine = ds(p.me, R)
+    gu = HalfGather(p, u, gsend, grecv, 0)
+    gn = HalfGather(p, n, gsend, grecv, 1)
+    scatter = HalfScatter(p, part, near, out, far, ssend, srecv)
+
+    def enter(half, layer):
+        u[owned(p.me, half), :] = norm(h[ds(half, HR), :], ga[pl.ds(layer, 1), :])
+        gu.start(half)
+
+    def add(half):
+        rows = ds(half, HR)
+        h[rows, :] = h[rows, :] + scatter.result(half)
+        return h[rows, :]
+
+    enter(0, 0)
+    enter(1, 0)
 
     def layer_step(layer):
+        more = layer < LAYERS - 1
+
         def refill(i):
-            @pl.when(layer < LAYERS - 1)
+            @pl.when(more)
             def _():
                 load(i, layer + 1).start()
 
-        u[mine, :] = norm(h[...], ga[pl.ds(layer, 1), :])
-        gather = Gather(p, u, gsend, grecv, 0)
-        gather.start()
         load(0, layer).wait()
-        gather.each(qkv_chunk(u, wq, acc1, qkv))
-        gather.finish()
+        in_order(gu, half_qkv(u, wq, acc1, qkv))
         refill(0)
-        attention(qkv, o)
+        attention(qkv, o, halves=True)
         load(1, layer).wait()
-        scatter = Scatter(p, part, near, out, far, ssend, srecv)
-        scatter.run(lambda c: dot(o[...], wo[:, ds(c, RW)]))
+        for half in range(2):
+            scatter.run(half, lambda c: dot(o[ds(half, HS), :], wo[:, ds(c, HW)]))
         refill(1)
-        h[...] = h[...] + scatter.result()
-
-        n[mine, :] = norm(h[...], gm[pl.ds(layer, 1), :])
-        gather = Gather(p, n, gsend, grecv, 0)
-        gather.start()
-        load(2, layer).wait()
-        load(3, layer).wait()
-
-        def last(cols, z1, z3):
-            m[:, cols] = (z1 * jax.nn.sigmoid(z1) * z3).astype(BF16)
-
-        gather.each(mlp_chunk(n, wg, wu, acc1, acc3, last))
-        gather.finish()
+        gu.finish()
+        for half in range(2):
+            n[owned(p.me, half), :] = norm(add(half), gm[pl.ds(layer, 1), :])
+            gn.start(half)
+
+        def last(rows, cols, z1, z3):
+            m[rows, cols] = (z1 * jax.nn.sigmoid(z1) * z3).astype(BF16)
+
+        def leave(half):
+            hs[layer, ds(half, HR), :] = add(half)
+
+            @pl.when(more)
+            def _():
+                enter(half, layer + 1)
+
+        gate_up = half_mlp(n, wg, wu, acc1, acc3, last)
+        for i in (2, 3):
+            load(i, layer).wait()
+        gn.relay((0, 0))
+        gn.relay((0, 1))
+        gn.arrived((0, 0))
+        gate_up(0, 0)
+        gn.relay((1, 0))
+        gn.arrived((0, 1))
+        gate_up(0, 1)
+        gn.relay((1, 1))
+        load(4, layer).wait()
+        scatter.run(0, lambda c: dot(m[ds(0, HS), :], wd[:, ds(c, HW)]))
+        gn.arrived((1, 0))
+        gate_up(1, 0)
+        gn.arrived((1, 1))
+        gate_up(1, 1)
         refill(2)
         refill(3)
-        load(4, layer).wait()
-        scatter.run(lambda c: dot(m[...], wd[:, ds(c, RW)]))
+        leave(0)
+        scatter.run(1, lambda c: dot(m[ds(1, HS), :], wd[:, ds(c, HW)]))
         refill(4)
-        h[...] = h[...] + scatter.result()
-        hs[layer] = h[...]
+        gn.finish()
+        leave(1)
 
     loop(LAYERS, layer_step)
 
@@ -445,7 +616,7 @@
     for i in order:
         loads[i].start()
     work = ((0, 0, 1), (2, 4, 5), (3, 4, 6), (4, 7, 8), (1, 2, 3))
-    waited = set()
+    waited, copies = set(), []
     for out_i, a_i, b_i in work:
         for i in (a_i, b_i):
             if i not in waited:
@@ -454,27 +625,20 @@
         a, b, out, stage = acts[a_i], acts[b_i], outs[out_i], stages[out_i]
         tiles, cols = a.shape[1] // S, b.shape[1]
 
-        def copy(i, slot):
-            return pltpu.make_async_copy(stage.at[slot], out.at[layer, ds(i, S), :], osem.at[out_i, slot])
+        def copy(i):
+            rows = ds(i, S)
+            return pltpu.make_async_copy(stage.at[rows, :], out.at[layer, rows, :], osem.at[out_i, i])
 
         def step(i):
-            slot = lax.rem(i, 2)
-
-            @pl.when(i >= 2)
-            def _():
-                copy(i - 2, slot).wait()
-
             lhs = a[:, ds(i, S)].T
             for c in range(cols // 512):
-                stage[slot, :, ds(c, 512)] = dot(lhs, b[:, ds(c, 512)]).astype(BF16)
-            copy(i, slot).start()
+                stage[ds(i, S), ds(c, 512)] = dot(lhs, b[:, ds(c, 512)]).astype(BF16)
+            copy(i).start()
 
         loop(tiles, step)
-    for out_i, a_i, b_i in work:
-        out, stage = outs[out_i], stages[out_i]
-        tiles = acts[a_i].shape[1] // S
-        for i in (tiles - 2, tiles - 1):
-            pltpu.make_async_copy(stage.at[i % 2], out.at[layer, ds(i, S), :], osem.at[out_i, i % 2]).wait()
+        copies += [copy(i) for i in range(tiles)]
+    for each in copies:
+        each.wait()
 
 
 def vmem():
@@ -522,7 +686,7 @@
             pltpu.VMEM((S, NF), BF16),
         ]
         + SCATTER_SCRATCH
-        + [dma((5,)), dma((1, 3, AC)), dma((1, 3, AC)), dma((3, RC)), dma((3, RC))],
+        + [dma((5,)), dma((2, 3, 2, HA)), dma((2, 3, 2, HA)), dma((3, 2, HC)), dma((3, 2, HC))],
         compiler_params=pltpu.CompilerParams(collective_id=0, has_side_effects=True, vmem_limit_bytes=VMEM_LIMIT),
     )(x, ga, gm, *weights)
 
@@ -570,8 +734,8 @@
         out_specs=[hbm()] * 5,
         input_output_aliases={9 + i: i for i in range(n_alias)},
         scratch_shapes=[pltpu.VMEM(shape, BF16) for shape in SAVED]
-        + [pltpu.VMEM((2, S, shape[1]), BF16) for shape in GRADS]
-        + [dma((9,)), dma((5, 2))],
+        + [pltpu.VMEM(shape, BF16) for shape in GRADS]
+        + [dma((9,)), dma((5, 8))],
         compiler_params=pltpu.CompilerParams(vmem_limit_bytes=VMEM_LIMIT),
         cost_estimate=pl.CostEstimate(flops=8_600_000_000, bytes_accessed=42_000_000, transcendentals=0),
     )(*saved, *grads)

time: 433 us -> 407 us (0.940)
  Pallas kernels: 428 us -> 402 us
    pallas_call x3, Pallas kernels: 71.8 us -> 54.8 us  [run_wgrad(): pl.pallas_call(functools.partial(wgrad_kernel, layer, n_alias), name=f'wg...]
    pallas_call x1, Pallas kernels: 135 us -> 125 us  [run_forward(): pl.pallas_call(forward_kernel, name='forward', out_shape=jax.ShapeDtypeSt...]
where the time goes in v2:
time: 407 us
  Pallas kernels  402 us (99%)
  local copies, waits for them, and re-layouts  4.25 us (1%)
    pallas_call x3, Pallas kernels, run_backward(): pl.pallas_call(functools.partial(backward_kernel, layer), name=f'backward...  222 us
    pallas_call x1, Pallas kernels, run_forward(): pl.pallas_call(forward_kernel, name='forward', out_shape=jax.ShapeDtypeSt...  125 us
    pallas_call x3, Pallas kernels, run_wgrad(): pl.pallas_call(functools.partial(wgrad_kernel, layer, n_alias), name=f'wg...  54.8 us

profile of v2, /device:TPU:0, one launch (start us, length us, event | category | flops | bytes accessed | tf_op | source)
XLA Modules:
  0.0 406.7 jit_solution(260737151678638951)
XLA Ops:
  0.6 125.0 %forward.1.hin = bf16[3,64,2048]{2,1,0:T(8,128)(2,1)} custom-call(bf16[64,2048]{1,0:T(8,128)(2,1)} %hin.1, f32[3,2048]{1,0:T(4,128)} %ga.7, f32[3,2048]{1,0:T(4,128)} %gm.7, bf16[3,2048,1536]{2,1,0:T(8,128)(2,1)} %wq_h.7, bf16[3,512,2048]{2,1,0:T(8,128)(2,1)} %wo_h.7, bf16[3,2048,2048]{2,1,0:T(8,128)(2,1)} %wg_h.7, bf16[3,2048,2048]{2,1,0:T(8,128)(2,1)} %wu_h.7, ...), custom_call_target="tpu_custom_call" | custom-call | tf_op jit(solution)/shard_map/forward/pallas_call | solution.py:671
  125.6 1.7 slice_bitcast_fusion
  127.3 0.6 broadcast_in_dim.3.gin
  127.9 72.5 %backward2.1 = (bf16[64,2048]{1,0:T(8,128)(2,1)}, f32[8,2048]{1,0:T(8,128)}, bf16[256,2048]{1,0:T(8,128)(2,1)}, bf16[256,1536]{1,0:T(8,128)(2,1)}, bf16[256,512]...) custom-call(bf16[3,64,2048]{2,1,0:T(8,128)(2,1)} %forward.1.hin, ...), custom_call_target="tpu_custom_call" | custom-call | tf_op jit(solution)/shard_map/backward2/pallas_call | solution.py:699
  200.4 18.2 %wgrad2.1 = (bf16[3,2048,1536]{2,1,0:T(8,128)(2,1)}, bf16[3,512,2048]{2,1,0:T(8,128)(2,1)}, bf16[3,2048,2048]{2,1,0:T(8,128)(2,1)}, bf16[3,2048,2048]{2,1,0:T(8,128)(2,1)}, bf16[3,2048,2048]{2,1,0:T(8,128)(2,1)}) custom-call(bf16[256,2048]{1,0:T(8,128)(2,1)} %get-tuple-element.71.u_h, bf16[256,1536]{1,0:T(8,128)(2,1)} %get-tuple-element.72.dqkv_h, ...), custom_call_target="tpu_custom_call" | custom-call | flops 8600000512 | bytes 42000000 | tf_op jit(solution)/shard_map/wgrad2/pallas_call | solution.py:729
  218.6 72.5 %backward1.1 = (bf16[64,2048]{1,0:T(8,128)(2,1)}, f32[8,2048]{1,0:T(8,128)}, bf16[256,2048]{1,0:T(8,128)(2,1)}, bf16[256,1536]{1,0:T(8,128)(2,1)}, bf16[256,512]...) custom-call(bf16[3,64,2048]{2,1,0:T(8,128)(2,1)} %forward.1.hin, ...), custom_call_target="tpu_custom_call" | custom-call | tf_op jit(solution)/shard_map/backward1/pallas_call | solution.py:699
  291.1 18.4 %wgrad1.1 = (bf16[3,2048,1536]{2,1,0:T(8,128)(2,1)}, bf16[3,512,2048]{2,1,0:T(8,128)(2,1)}, bf16[3,2048,2048]{2,1,0:T(8,128)(2,1)}, bf16[3,2048,2048]{2,1,0:T(8,128)(2,1)}, bf16[3,2048,2048]{2,1,0:T(8,128)(2,1)}) custom-call(bf16[256,2048]{1,0:T(8,128)(2,1)} %get-tuple-element.88.u_h, ...), custom_call_target="tpu_custom_call", output_to_operand_aliasing={{0}: (9, {}), {1}: (10, {}), {2}: (11, {}), {3}: (12, {}), ... | custom-call | flops 8600000512 | bytes 42000000 | tf_op jit(solution)/shard_map/wgrad1/pallas_call | solution.py:729
  309.5 76.9 %backward0.1 = (bf16[64,2048]{1,0:T(8,128)(2,1)}, f32[3,2048]{1,0:T(4,128)}, f32[3,2048]{1,0:T(4,128)}, bf16[256,2048]{1,0:T(8,128)(2,1)}, bf16[256,1536]{1,0:T(...) custom-call(bf16[64,2048]{1,0:T(8,128)(2,1)} %hin.1, ...), custom_call_target="tpu_custom_call" | custom-call | tf_op jit(solution)/shard_map/backward0/pallas_call | solution.py:699
  386.4 0.0 copy-start
  386.5 0.0 copy-start.2
  386.5 0.0 copy-start.1
  386.5 18.2 %wgrad0.1 = (bf16[3,2048,1536]{2,1,0:T(8,128)(2,1)}, bf16[3,512,2048]{2,1,0:T(8,128)(2,1)}, bf16[3,2048,2048]{2,1,0:T(8,128)(2,1)}, bf16[3,2048,2048]{2,1,0:T(8,128)(2,1)}, bf16[3,2048,2048]{2,1,0:T(8,128)(2,1)}) custom-call(bf16[256,2048]{1,0:T(8,128)(2,1)} %get-tuple-element.110.u_h,, ...), custom_call_target="tpu_custom_call", output_to_operand_aliasing={{0}: (9, {}), {1}: (10, {}), {2}: (11, {}), {3}: (12, {}), ... | custom-call | flops 8600000512 | bytes 42000000 | tf_op jit(solution)/shard_map/wgrad0/pallas_call | solution.py:729
  404.7 0.0 copy-done
  404.7 0.7 copy.41
  405.4 0.0 copy-done.2
  405.4 0.6 copy.42
  406.0 0.0 copy-done.1
  406.1 0.6 copy.43
Async XLA Ops:
  386.4 18.3 %copy-start = (bf16[64,2048]{1,0:T(8,128)(2,1)S(1)}, bf16[64,2048]{1,0:T(8,128)(2,1)}, u32[]{:S(2)}) copy-start(bf16[64,2048]{1,0:T(8,128)(2,1)} %get-tuple-element.141) | copy-start | bytes 786436
  386.5 19.0 %copy-start.2 = (f32[3,2048]{1,0:T(4,128)S(1)}, f32[3,2048]{1,0:T(4,128)}, u32[]{:S(2)}) copy-start(f32[3,2048]{1,0:T(4,128)} %get-tuple-element.147) | copy-start | bytes 73732
  386.5 19.6 %copy-start.1 = (f32[3,2048]{1,0:T(4,128)S(1)}, f32[3,2048]{1,0:T(4,128)}, u32[]{:S(2)}) copy-start(f32[3,2048]{1,0:T(4,128)} %get-tuple-element.148) | copy-start | bytes 73732

commit v3 on v2

--- a/solution.py
+++ b/solution.py
@@ -169,7 +169,7 @@
 
 HR = R // 2
 HS = S // 2
-HA = 2
+HA = 4
 HAW = D // HA
 HC = 4
 HW = D // HC
@@ -381,7 +381,7 @@
             body(*ITEMS[i - 1])
 
 
-def forward_kernel(x, ga, gm, wq_h, wo_h, wg_h, wu_h, wd_h, hs,
+def forward_kernel(x, ga, gm, wq_h, wo_h, wg_h, wu_h, wd_h, hs, y,
                    wq, wo, wg, wu, wd, h, u, n, acc1, acc3, qkv, o, m, part, near, out, far,
                    wsem, gsend, grecv, ssend, srecv):
     p = Peers()
@@ -435,44 +435,47 @@
             m[rows, cols] = (z1 * jax.nn.sigmoid(z1) * z3).astype(BF16)
 
         def leave(half):
-            hs[layer, ds(half, HR), :] = add(half)
+            total = add(half)
 
             @pl.when(more)
             def _():
+                hs[layer, ds(half, HR), :] = total
                 enter(half, layer + 1)
+
+            @pl.when(jnp.logical_not(more))
+            def _():
+                y[ds(half, HR), :] = total
 
         gate_up = half_mlp(n, wg, wu, acc1, acc3, last)
         for i in (2, 3):
             load(i, layer).wait()
-        gn.relay((0, 0))
-        gn.relay((0, 1))
-        gn.arrived((0, 0))
-        gate_up(0, 0)
-        gn.relay((1, 0))
-        gn.arrived((0, 1))
-        gate_up(0, 1)
-        gn.relay((1, 1))
-        load(4, layer).wait()
-        scatter.run(0, lambda c: dot(m[ds(0, HS), :], wd[:, ds(c, HW)]))
-        gn.arrived((1, 0))
-        gate_up(1, 0)
-        gn.arrived((1, 1))
-        gate_up(1, 1)
+        for i, item in enumerate(ITEMS):
+            if i == 0:
+                gn.relay(item)
+            if i == HA:
+                load(4, layer).wait()
+                scatter.run(0, lambda c: dot(m[ds(0, HS), :], wd[:, ds(c, HW)]))
+            if i + 1 < len(ITEMS):
+                gn.relay(ITEMS[i + 1])
+            gn.arrived(item)
+            gate_up(*item)
         refill(2)
         refill(3)
-        leave(0)
         scatter.run(1, lambda c: dot(m[ds(1, HS), :], wd[:, ds(c, HW)]))
         refill(4)
+        leave(0)
         gn.finish()
         leave(1)
 
     loop(LAYERS, layer_step)
 
 
-def backward_kernel(layer, hin, dy, gin, ga, gm, wq_h, wo_h, wg_h, wu_h, wd_h, *refs):
-    last_call = layer == 0
+def backward_kernel(layer, hin, dy, *refs):
+    first_call, last_call = layer == LAYERS - 1, layer == 0
     refs = list(refs)
     take = lambda k: [refs.pop(0) for _ in range(k)]
+    gin = None if first_call else take(1)[0]
+    ga, gm, wq_h, wo_h, wg_h, wu_h, wd_h = take(7)
     (dx,) = take(1)
     gouts = take(2 if last_call else 1)
     saved_h = take(9)
@@ -552,7 +555,7 @@
     da[mine, :] = d_mid
     ga_ = Gather(p, da, gsend, grecv, 3)
     ga_.start()
-    gbuf[...] = gin[...]
+    gbuf[...] = jnp.zeros_like(gbuf) if first_call else gin[...]
     gbuf[pl.ds(LAYERS + layer, 1), :] = dgain_m
 
     def heads_chunk(chunk):
@@ -612,12 +615,14 @@
     isem, osem = take(2)
     loads = [pltpu.make_async_copy(src, dst, isem.at[i])
              for i, (src, dst) in enumerate(zip((u_h, dqkv_h, o_h, da_h, n_h, dg_h, du_h, m_h, dd_h), acts))]
-    order = (0, 1, 4, 5, 6, 7, 8, 2, 3)
-    for i in order:
-        loads[i].start()
-    work = ((0, 0, 1), (2, 4, 5), (3, 4, 6), (4, 7, 8), (1, 2, 3))
-    waited, copies = set(), []
-    for out_i, a_i, b_i in work:
+    work = ((2, 4, 5), (3, 4, 6), (4, 7, 8), (0, 0, 1), (1, 2, 3))
+    started, waited, copies = set(), set(), []
+    for number, (out_i, a_i, b_i) in enumerate(work):
+        for _, *pair in work[: number + 2]:
+            for i in pair:
+                if i not in started:
+                    loads[i].start()
+                    started.add(i)
         for i in (a_i, b_i):
             if i not in waited:
                 loads[i].wait()
@@ -671,9 +676,9 @@
     return pl.pallas_call(
         forward_kernel,
         name="forward",
-        out_shape=jax.ShapeDtypeStruct((LAYERS, R, D), BF16),
+        out_shape=[jax.ShapeDtypeStruct((LAYERS - 1, R, D), BF16), jax.ShapeDtypeStruct((R, D), BF16)],
         in_specs=[vmem()] * 3 + [hbm()] * 5,
-        out_specs=vmem(),
+        out_specs=[vmem()] * 2,
         scratch_shapes=WEIGHT_SCRATCH
         + [
             pltpu.VMEM((R, D), BF16),
@@ -700,7 +705,7 @@
         functools.partial(backward_kernel, layer),
         name=f"backward{layer}",
         out_shape=[jax.ShapeDtypeStruct((R, D), BF16)] + gshape + saved,
-        in_specs=[vmem()] * 5 + [hbm()] * 5,
+        in_specs=[vmem()] * (4 + len(gin)) + [hbm()] * 5,
         out_specs=[vmem()] * (1 + len(gshape)) + [hbm()] * 9,
         scratch_shapes=[pltpu.VMEM(shape, BF16) for shape in SAVED]
         + WEIGHT_SCRATCH
@@ -719,7 +724,7 @@
         compiler_params=pltpu.CompilerParams(
             collective_id=1 + layer, has_side_effects=True, vmem_limit_bytes=VMEM_LIMIT
         ),
-    )(hin, dy, gin, ga, gm, *weights)
+    )(hin, dy, *gin, ga, gm, *weights)
     return outs[0], outs[1 : 1 + len(gshape)], outs[1 + len(gshape) :]
 
 
@@ -753,17 +758,17 @@
 
     def device_step(x, grad_y, gain_attn, gain_mlp, w_qkv, w_out, w_gate, w_up, w_down):
         weights = (w_qkv, w_out, w_gate, w_up, w_down)
-        hs = run_forward(x, gain_attn, gain_mlp, weights)
+        hs, y = run_forward(x, gain_attn, gain_mlp, weights)
         d_hidden = grad_y
-        gains = [jnp.zeros((8, D), F32)]
+        gains = []
         grads = ()
         for layer in reversed(range(LAYERS)):
             d_hidden, gains, saved = run_backward(
-                layer, hs if layer > 0 else x, d_hidden, gains[0], gain_attn, gain_mlp, weights
+                layer, hs if layer > 0 else x, d_hidden, gains, gain_attn, gain_mlp, weights
             )
             grads = run_wgrad(layer, saved, grads)
             if layer > 0:
                 d_hidden, grads = lax.optimization_barrier((d_hidden, grads))
-        return (hs[LAYERS - 1], d_hidden, *grads, *gains)
+        return (y, d_hidden, *grads, *gains)
 
     return jax.shard_map(device_step, mesh=mesh, in_specs=in_specs, out_specs=out_specs, check_vma=False)

time: 407 us -> 412 us (1.012)
  Pallas kernels: 402 us -> 408 us
    pallas_call x1, Pallas kernels: 125 us -> 131 us  [run_forward(): pl.pallas_call(forward_kernel, name='forward', out_shape=[jax.ShapeDtypeS...]
where the time goes in v3:
time: 412 us
  Pallas kernels  408 us (99%)
    pallas_call x3, Pallas kernels, run_backward(): pl.pallas_call(functools.partial(backward_kernel, layer), name=f'backward...  222 us
    pallas_call x1, Pallas kernels, run_forward(): pl.pallas_call(forward_kernel, name='forward', out_shape=[jax.ShapeDtypeS...  131 us
    pallas_call x3, Pallas kernels, run_wgrad(): pl.pallas_call(functools.partial(wgrad_kernel, layer, n_alias), name=f'wg...  55.1 us

profile of v3, /device:TPU:0, one launch (start us, length us, event | category | flops | bytes accessed | tf_op | source)
XLA Modules:
  0.0 411.7 jit_solution(11244744069148809064)
XLA Ops:
  0.6 131.4 %forward.1 = (bf16[2,64,2048]{2,1,0:T(8,128)(2,1)}, bf16[64,2048]{1,0:T(8,128)(2,1)}) custom-call(bf16[64,2048]{1,0:T(8,128)(2,1)} %hin.1, f32[3,2048]{1,0:T(4,128)} %refs_1_.5, f32[3,2048]{1,0:T(4,128)} %refs_2_.5, bf16[3,2048,1536]{2,1,0:T(8,128)(2,1)} %refs_3_.5, bf16[3,512,2048]{2,1,0:T(8,128)(2,1)} %refs_4_.5, bf16[3,2048,2048]{2,1,0:T(8,128)(2,1)} %refs_5_.5, ...), custom_call_target="tpu_custom_call" | custom-call | tf_op jit(solution)/shard_map/forward/pallas_call | solution.py:676
  132.0 72.5 %backward2.1 = (bf16[64,2048]{1,0:T(8,128)(2,1)}, f32[8,2048]{1,0:T(8,128)}, bf16[256,2048]{1,0:T(8,128)(2,1)}, bf16[256,1536]{1,0:T(8,128)(2,1)}, bf16[256,512]...) custom-call(bf16[2,64,2048]{2,1,0:T(8,128)(2,1)} %get-tuple-element., ...), custom_call_target="tpu_custom_call" | custom-call | tf_op jit(solution)/shard_map/backward2/pallas_call | solution.py:704
  204.6 18.3 %wgrad2.1 = (bf16[3,2048,1536]{2,1,0:T(8,128)(2,1)}, bf16[3,512,2048]{2,1,0:T(8,128)(2,1)}, bf16[3,2048,2048]{2,1,0:T(8,128)(2,1)}, bf16[3,2048,2048]{2,1,0:T(8,128)(2,1)}, bf16[3,2048,2048]{2,1,0:T(8,128)(2,1)}) custom-call(bf16[256,2048]{1,0:T(8,128)(2,1)} %get-tuple-element.75.u_h, bf16[256,1536]{1,0:T(8,128)(2,1)} %get-tuple-element.76.dqkv_h, ...), custom_call_target="tpu_custom_call" | custom-call | flops 8600000512 | bytes 42000000 | tf_op jit(solution)/shard_map/wgrad2/pallas_call | solution.py:734
  222.9 72.4 %backward1.1 = (bf16[64,2048]{1,0:T(8,128)(2,1)}, f32[8,2048]{1,0:T(8,128)}, bf16[256,2048]{1,0:T(8,128)(2,1)}, bf16[256,1536]{1,0:T(8,128)(2,1)}, bf16[256,512]...) custom-call(bf16[2,64,2048]{2,1,0:T(8,128)(2,1)} %get-tuple-element., ...), custom_call_target="tpu_custom_call" | custom-call | tf_op jit(solution)/shard_map/backward1/pallas_call | solution.py:704
  295.3 18.5 %wgrad1.1 = (bf16[3,2048,1536]{2,1,0:T(8,128)(2,1)}, bf16[3,512,2048]{2,1,0:T(8,128)(2,1)}, bf16[3,2048,2048]{2,1,0:T(8,128)(2,1)}, bf16[3,2048,2048]{2,1,0:T(8,128)(2,1)}, bf16[3,2048,2048]{2,1,0:T(8,128)(2,1)}) custom-call(bf16[256,2048]{1,0:T(8,128)(2,1)} %get-tuple-element.92.u_h, ...), custom_call_target="tpu_custom_call", output_to_operand_aliasing={{0}: (9, {}), {1}: (10, {}), {2}: (11, {}), {3}: (12, {}), ... | custom-call | flops 8600000512 | bytes 42000000 | tf_op jit(solution)/shard_map/wgrad1/pallas_call | solution.py:734
  313.8 76.9 %backward0.1 = (bf16[64,2048]{1,0:T(8,128)(2,1)}, f32[3,2048]{1,0:T(4,128)}, f32[3,2048]{1,0:T(4,128)}, bf16[256,2048]{1,0:T(8,128)(2,1)}, bf16[256,1536]{1,0:T(...) custom-call(bf16[64,2048]{1,0:T(8,128)(2,1)} %hin.1, ...), custom_call_target="tpu_custom_call" | custom-call | tf_op jit(solution)/shard_map/backward0/pallas_call | solution.py:704
  390.7 0.0 copy-start
  390.7 0.0 copy-start.1
  390.7 0.0 copy-start.3
  390.7 0.0 copy-start.2
  390.7 18.3 %wgrad0.1 = (bf16[3,2048,1536]{2,1,0:T(8,128)(2,1)}, bf16[3,512,2048]{2,1,0:T(8,128)(2,1)}, bf16[3,2048,2048]{2,1,0:T(8,128)(2,1)}, bf16[3,2048,2048]{2,1,0:T(8,128)(2,1)}, bf16[3,2048,2048]{2,1,0:T(8,128)(2,1)}) custom-call(bf16[256,2048]{1,0:T(8,128)(2,1)} %get-tuple-element.114.u_h,, ...), custom_call_target="tpu_custom_call", output_to_operand_aliasing={{0}: (9, {}), {1}: (10, {}), {2}: (11, {}), {3}: (12, {}), ... | custom-call | flops 8600000512 | bytes 42000000 | tf_op jit(solution)/shard_map/wgrad0/pallas_call | solution.py:734
  409.1 0.0 copy-done
  409.1 0.7 copy.42
  409.8 0.0 copy-done.1
  409.8 0.7 copy.43
  410.5 0.0 copy-done.3
  410.5 0.6 copy.44
  411.1 0.0 copy-done.2
  411.1 0.6 copy.45
Async XLA Ops:
  390.7 18.4 %copy-start = (bf16[64,2048]{1,0:T(8,128)(2,1)S(1)}, bf16[64,2048]{1,0:T(8,128)(2,1)}, u32[]{:S(2)}) copy-start(bf16[64,2048]{1,0:T(8,128)(2,1)} %get-tuple-element.144) | copy-start | bytes 786436
  390.7 19.1 %copy-start.1 = (bf16[64,2048]{1,0:T(8,128)(2,1)S(1)}, bf16[64,2048]{1,0:T(8,128)(2,1)}, u32[]{:S(2)}) copy-start(bf16[64,2048]{1,0:T(8,128)(2,1)} %get-tuple-element.145) | copy-start | bytes 786436
  390.7 19.8 %copy-start.3 = (f32[3,2048]{1,0:T(4,128)S(1)}, f32[3,2048]{1,0:T(4,128)}, u32[]{:S(2)}) copy-start(f32[3,2048]{1,0:T(4,128)} %get-tuple-element.151) | copy-start | bytes 73732
  390.7 20.4 %copy-start.2 = (f32[3,2048]{1,0:T(4,128)S(1)}, f32[3,2048]{1,0:T(4,128)}, u32[]{:S(2)}) copy-start(f32[3,2048]{1,0:T(4,128)} %get-tuple-element.152) | copy-start | bytes 73732

commit v4 on v1

v4 whole, which is shorter than its diff:
```python
import functools

import jax
import jax.numpy as jnp
from jax import lax
from jax.experimental import pallas as pl
from jax.experimental.pallas import tpu as pltpu
from jax.sharding import PartitionSpec as P

HEAD = 128
EPS = 1e-5
MESH = pl.DeviceIdType.MESH
F32 = jnp.float32
BF16 = jnp.bfloat16
VMEM_LIMIT = 66_000_000

D = 2048
S = 256
R = 64
NQ = 1536
NO = 512
NF = 2048
HEADS = 4
LAYERS = 3

HR = R // 2
HS = S // 2


def dot(a, b):
    return jnp.dot(a, b, preferred_element_type=F32)


def dot_nt(a, b):
    return lax.dot_general(a, b, (((1,), (1,)), ((), ())), preferred_element_type=F32)


def dot_tn(a, b):
    return lax.dot_general(a, b, (((0,), (0,)), ((), ())), preferred_element_type=F32)


def ds(i, n):
    return pl.ds(i * n if isinstance(i, int) else pl.multiple_of(i * n, n), n)


def loop(n, body):
    lax.fori_loop(0, n, lambda i, c: (body(i), c)[1], 0)


class Peers:
    def __init__(self):
        self.me = lax.axis_index("tp")
        core, chip = lax.rem(self.me, 2), self.me // 2
        self.sib = chip * 2 + (1 - core)
        self.cross = (1 - chip) * 2 + core
        self.diag = (1 - chip) * 2 + (1 - core)

    def barrier(self):
        sem = pltpu.get_barrier_semaphore()
        for peer in (self.sib, self.cross):
            pl.semaphore_signal(sem, inc=1, device_id={"tp": peer}, device_id_type=MESH)
        pl.semaphore_wait(sem, 2)


def remote(src, dst, send, recv, peer):
    return pltpu.make_async_remote_copy(
        src_ref=src, dst_ref=dst, send_sem=send, recv_sem=recv, device_id={"tp": peer}, device_id_type=MESH
    )


def owned(owner, half):
    return ds(half * 4 + owner, HR)


def true_position(row):
    return lax.rem(row, HS) // HR * R + row // HS * HR + lax.rem(row, HR)


class Gather:
    def __init__(self, p, buf, send, recv, which):
        self.p, self.buf, self.send, self.recv, self.which = p, buf, send, recv, which

    def _copy(self, kind, half, owner, peer):
        part = self.buf.at[owned(owner, half), :]
        sems = (self.which, kind, half)
        return remote(part, part, self.send.at[sems], self.recv.at[sems], peer)

    def start(self, half):
        self._copy(0, half, self.p.me, self.p.cross).start()
        self._copy(1, half, self.p.me, self.p.sib).start()

    def relay(self, half):
        self._copy(0, half, self.p.cross, self.p.cross).wait_recv()
        self._copy(2, half, self.p.cross, self.p.sib).start()

    def arrived(self, half):
        self._copy(1, half, self.p.sib, self.p.sib).wait_recv()
        self._copy(2, half, self.p.diag, self.p.sib).wait_recv()

    def each(self, body):
        def one(half):
            self.relay(half)
            self.arrived(half)
            body(half)

        loop(2, one)

    def finish(self):
        def one(half):
            self._copy(0, half, self.p.me, self.p.cross).wait_send()
            self._copy(1, half, self.p.me, self.p.sib).wait_send()
            self._copy(2, half, self.p.cross, self.p.sib).wait_send()

        loop(2, one)


class Scatter:
    def __init__(self, p, part, near, out, far, send, recv, chunks):
        self.p, self.part, self.near, self.out, self.far, self.send, self.recv = p, part, near, out, far, send, recv
        self.chunks, self.width = chunks, D // chunks

    def _near(self, kind, half, chunk):
        owner = self.p.diag if kind == 0 else self.p.sib
        cols = ds(chunk, self.width)
        return remote(
            self.part.at[owned(owner, half), cols],
            self.near.at[kind, ds(half, HR), cols],
            self.send.at[kind, half, chunk],
            self.recv.at[kind, half, chunk],
            self.p.sib,
        )

    def _far(self, half, chunk):
        cols = ds(chunk, self.width)
        return remote(
            self.out.at[ds(half, HR), cols],
            self.far.at[ds(half, HR), cols],
            self.send.at[2, half, chunk],
            self.recv.at[2, half, chunk],
            self.p.cross,
        )

    def _mid(self, half, chunk):
        self._near(0, half, chunk).wait_recv()
        cols = ds(chunk, self.width)
        total = self.part[owned(self.p.cross, half), cols] + self.near[0, ds(half, HR), cols]
        self.out[ds(half, HR), cols] = total.astype(BF16)
        self._far(half, chunk).start()

    def run(self, half, compute):
        def step(chunk):
            cols = ds(chunk, self.width)
            self.part[ds(half, HS), cols] = compute(ds(half, HS), cols)
            self._near(0, half, chunk).start()
            self._near(1, half, chunk).start()

        loop(self.chunks, step)
        loop(self.chunks, lambda chunk: self._mid(half, chunk))

    def run_full(self, compute):
        def mids(chunk):
            self._mid(0, chunk)
            self._mid(1, chunk)

        def step(chunk):
            cols = ds(chunk, self.width)
            self.part[:, cols] = compute(cols)
            for kind in range(2):
                for half in range(2):
                    self._near(kind, half, chunk).start()

            @pl.when(chunk > 0)
            def _():
                mids(chunk - 1)

        loop(self.chunks, step)
        mids(self.chunks - 1)

    def result(self, half):
        def waits(chunk):
            self._near(1, half, chunk).wait_recv()
            self._far(half, chunk).wait_recv()

        def sent(chunk):
            self._near(0, half, chunk).wait_send()
            self._near(1, half, chunk).wait_send()
            self._far(half, chunk).wait_send()

        loop(self.chunks, waits)
        rows = ds(half, HR)
        total = self.part[owned(self.p.me, half), :] + self.near[1, rows, :] + self.far[rows, :].astype(F32)
        loop(self.chunks, sent)
        return total.astype(BF16)


def norm(h, gain):
    hf = h.astype(F32)
    inv = lax.rsqrt(jnp.mean(hf * hf, axis=-1, keepdims=True) + EPS)
    return (hf * inv * gain).astype(BF16)


def norm_back(h, gain, dy):
    hf, dyf = h.astype(F32), dy.astype(F32)
    inv = lax.rsqrt(jnp.mean(hf * hf, axis=-1, keepdims=True) + EPS)
    dgain = jnp.sum(dyf * (hf * inv), axis=0, keepdims=True)
    dn = dyf * gain
    slope = jnp.sum(dn * hf, axis=-1, keepdims=True) * (inv * inv * inv) / D
    return (dn * inv - hf * slope).astype(BF16), dgain


def softmax_scores(q, k):
    scores = dot_nt(q, k) * HEAD**-0.5
    rows = true_position(lax.broadcasted_iota(jnp.int32, (S, 1), 0))
    cols = true_position(lax.broadcasted_iota(jnp.int32, (1, S), 1))
    scores = jnp.where(rows >= cols, scores, -1e30)
    e = jnp.exp(scores - jnp.max(scores, axis=-1, keepdims=True))
    return e / jnp.sum(e, axis=-1, keepdims=True)


def head_cols(head, which):
    return ds(head * 3 + which, HEAD)


def per_head(one, together):
    def step(j):
        for i in range(together):
            one(j * together + i)

    loop(HEADS // together, step)


def attention(qkv, o, together, probs=None):
    def one(head):
        prob = softmax_scores(qkv[:, head_cols(head, 0)], qkv[:, head_cols(head, 1)])
        if probs is not None:
            probs[head] = prob
        o[:, ds(head, HEAD)] = dot(prob.astype(BF16), qkv[:, head_cols(head, 2)]).astype(BF16)

    per_head(one, together)


def half_qkv(u, wq, qkv):
    def body(half):
        rows = ds(half, HS)
        for j in range(NQ // 512):
            qkv[rows, ds(j, 512)] = dot(u[rows, :], wq[:, ds(j, 512)]).astype(BF16)

    return body


def half_mlp(n, wg, wu, last, tile):
    def body(half):
        rows = ds(half, HS)

        def one(j):
            for k in range(tile // 512):
                cols = ds(j * (tile // 512) + k, 512)
                z1 = dot(n[rows, :], wg[:, cols]).astype(BF16).astype(F32)
                z3 = dot(n[rows, :], wu[:, cols]).astype(BF16).astype(F32)
                last(rows, cols, z1, z3)

        loop(NF // tile, one)

    return body


def forward_kernel(x, ga, gm, wq_h, wo_h, wg_h, wu_h, wd_h, hs, y,
                   wq, wo, wg, wu, wd, h, u, n, qkv, o, m, part, near, out, far,
                   wsem, gsend, grecv, ssend, srecv):
    p = Peers()
    pairs = ((wq_h, wq), (wo_h, wo), (wg_h, wg), (wu_h, wu), (wd_h, wd))

    def load(i, layer):
        return pltpu.make_async_copy(pairs[i][0].at[layer], pairs[i][1], wsem.at[i])

    for i in range(5):
        load(i, 0).start()
    h[...] = x[...]
    p.barrier()
    gu = Gather(p, u, gsend, grecv, 0)
    gn = Gather(p, n, gsend, grecv, 1)
    scatter = Scatter(p, part, near, out, far, ssend, srecv, 2)

    def enter(half, layer):
        u[owned(p.me, half), :] = norm(h[ds(half, HR), :], ga[pl.ds(layer, 1), :])
        gu.start(half)

    def add(half):
        rows = ds(half, HR)
        total = h[rows, :] + scatter.result(half)
        h[rows, :] = total
        return total

    loop(2, lambda half: enter(half, 0))

    def layer_step(layer):
        more = layer < LAYERS - 1

        def refill(i):
            @pl.when(more)
            def _():
                load(i, layer + 1).start()

        load(0, layer).wait()
        gu.each(half_qkv(u, wq, qkv))
        refill(0)
        attention(qkv, o, 4)
        load(1, layer).wait()
        loop(2, lambda half: scatter.run(half, lambda rows, cols: dot(o[rows, :], wo[:, cols])))
        refill(1)
        gu.finish()

        def between(half):
            n[owned(p.me, half), :] = norm(add(half), gm[pl.ds(layer, 1), :])
            gn.start(half)

        loop(2, between)

        def last(rows, cols, z1, z3):
            m[rows, cols] = (z1 * jax.nn.sigmoid(z1) * z3).astype(BF16)

        gate_up = half_mlp(n, wg, wu, last, 1024)
        for i in (2, 3, 4):
            load(i, layer).wait()
        gn.relay(0)

        def mlp(half):
            gn.arrived(half)
            gate_up(half)

            @pl.when(half == 0)
            def _():
                gn.relay(1)

            scatter.run(half, lambda rows, cols: dot(m[rows, :], wd[:, cols]))

        loop(2, mlp)
        refill(2)
        refill(3)
        refill(4)
        gn.finish()

        def leave(half):
            total = add(half)

            @pl.when(more)
            def _():
                hs[layer, ds(half, HR), :] = total
                enter(half, layer + 1)

            @pl.when(jnp.logical_not(more))
            def _():
                y[ds(half, HR), :] = total

        loop(2, leave)

    loop(LAYERS, layer_step)


def backward_kernel(layer, hin, dy, *refs):
    first_call, last_call = layer == LAYERS - 1, layer == 0
    refs = list(refs)
    take = lambda k: [refs.pop(0) for _ in range(k)]
    gin = None if first_call else take(1)[0]
    ga, gm, wq_h, wo_h, wg_h, wu_h, wd_h = take(7)
    (dx,) = take(1)
    gouts = take(2 if last_call else 1)
    saved_h = take(9)
    u, dqkv, o, da, n, dg, du, m, dd = saved = take(9)
    wq, wo, wg, wu, wd = take(5)
    hm, qkv, probs, dgated, dh, part, near, out, far, gbuf, gmid, gfar = take(12)
    wsem, osem, gsend, grecv, ssend, srecv, rsend, rrecv = take(8)

    p = Peers()
    pairs = ((wq_h, wq), (wo_h, wo), (wg_h, wg), (wu_h, wu), (wd_h, wd))
    loads = [pltpu.make_async_copy(src.at[layer], dst, wsem.at[i]) for i, (src, dst) in enumerate(pairs)]
    saves = [pltpu.make_async_copy(src, dst, osem.at[i]) for i, (src, dst) in enumerate(zip(saved, saved_h))]
    for i in (0, 1, 4, 2, 3):
        loads[i].start()
    h = hin.at[layer - 1] if layer > 0 else hin
    gain_a, gain_m = ga[pl.ds(layer, 1), :], gm[pl.ds(layer, 1), :]
    gu, gd, gn, gda = (Gather(p, buf, gsend, grecv, i) for i, buf in enumerate((u, dd, n, da)))
    two = Scatter(p, part, near, out, far, ssend, srecv, 2)
    four = Scatter(p, part, near, out, far, ssend, srecv, 4)
    p.barrier()

    def enter(half):
        u[owned(p.me, half), :] = norm(h[ds(half, HR), :], gain_a)
        gu.start(half)

    def enter_d(half):
        dd[owned(p.me, half), :] = dy[ds(half, HR), :]
        gd.start(half)

    loop(2, enter)
    loop(2, enter_d)
    gbuf[...] = jnp.zeros_like(gbuf) if first_call else gin[...]

    loads[0].wait()
    gu.each(half_qkv(u, wq, qkv))
    saves[0].start()
    attention(qkv, o, 2, probs)
    saves[2].start()
    loads[1].wait()
    loop(2, lambda half: two.run(half, lambda rows, cols: dot(o[rows, :], wo[:, cols])))

    loop(2, gd.relay)
    loop(2, gd.arrived)
    saves[8].start()
    loads[4].wait()

    def gated(j):
        dgated[:, ds(j, 512)] = dot_nt(dd[...], wd[ds(j, 512), :]).astype(BF16)

    loop(NF // 512, gated)

    def between(half):
        rows = ds(half, HR)
        h_mid = h[rows, :] + two.result(half)
        hm[rows, :] = h_mid
        n[owned(p.me, half), :] = norm(h_mid, gain_m)
        gn.start(half)

    loop(2, between)
    loads[2].wait()
    loads[3].wait()

    def last(rows, cols, z1, z3):
        sig = jax.nn.sigmoid(z1)
        silu = z1 * sig
        dm = dgated[rows, cols].astype(F32)
        m[rows, cols] = (silu * z3).astype(BF16)
        du[rows, cols] = (dm * silu).astype(BF16)
        dg[rows, cols] = (dm * z3 * (sig + silu * (1.0 - sig))).astype(BF16)

    gn.each(half_mlp(n, wg, wu, last, 512))
    for i in (4, 5, 6, 7):
        saves[i].start()

    four.run_full(lambda cols: dot_nt(dg[...], wg[cols, :]) + dot_nt(du[...], wu[cols, :]))

    def mid_back(half):
        rows = ds(half, HR)
        d_norm, dgain = norm_back(hm[rows, :], gain_m, four.result(half))
        da[owned(p.me, half), :] = dy[rows, :] + d_norm
        gda.start(half)
        row = pl.ds(LAYERS + layer, 1)
        gbuf[row, :] = gbuf[row, :] + dgain

    loop(2, mid_back)

    def heads(half):
        rows = ds(half, HS)
        dh[rows, :] = dot_nt(da[rows, :], wo[...]).astype(BF16)

    gda.each(heads)
    saves[3].start()

    def back(head):
        prob = probs[head]
        d_o = dh[:, ds(head, HEAD)]
        q, k, v = (qkv[:, head_cols(head, i)] for i in range(3))
        d_prob = dot_nt(d_o, v)
        d_scores = (prob * (d_prob - jnp.sum(d_prob * prob, axis=-1, keepdims=True)) * HEAD**-0.5).astype(BF16)
        dqkv[:, head_cols(head, 0)] = dot(d_scores, k).astype(BF16)
        dqkv[:, head_cols(head, 1)] = dot_tn(d_scores, q).astype(BF16)
        dqkv[:, head_cols(head, 2)] = dot_tn(prob.astype(BF16), d_o).astype(BF16)

    per_head(back, 2)
    saves[1].start()
    four.run_full(lambda cols: dot_nt(dqkv[...], wq[cols, :]))

    def leave(half):
        rows = ds(half, HR)
        d_norm, dgain = norm_back(h[rows, :], gain_a, four.result(half))
        dx[rows, :] = da[owned(p.me, half), :] + d_norm
        row = pl.ds(layer, 1)
        gbuf[row, :] = gbuf[row, :] + dgain

    loop(2, leave)

    if last_call:
        near_g = remote(gbuf, gmid, rsend.at[0], rrecv.at[0], p.sib)
        near_g.start()
        near_g.wait()
        gbuf[...] = gbuf[...] + gmid[...]
        far_g = remote(gbuf, gfar, rsend.at[1], rrecv.at[1], p.cross)
        far_g.start()
        far_g.wait()
        total = gbuf[...] + gfar[...]
        gouts[0][...] = total[:LAYERS]
        gouts[1][...] = total[LAYERS:2 * LAYERS]
    else:
        gouts[0][...] = gbuf[...]
    for g in (gu, gd, gn, gda):
        g.finish()
    for save in saves:
        save.wait()


def wgrad_kernel(layer, n_alias, u_h, dqkv_h, o_h, da_h, n_h, dg_h, du_h, m_h, dd_h, *refs):
    refs = list(refs[n_alias:])
    take = lambda k: [refs.pop(0) for _ in range(k)]
    gqkv_h, gout_h, ggate_h, gup_h, gdown_h = take(5)
    u, dqkv, o, da, lhs, rhs, gqkv, gout, gmlp = take(9)
    isem, osem = take(2)
    sources = (n_h, dg_h, du_h, m_h, dd_h, u_h, dqkv_h, o_h, da_h)
    targets = (lhs.at[0], rhs.at[0], rhs.at[1], lhs.at[1], rhs.at[2], u, dqkv, o, da)
    loads = [pltpu.make_async_copy(src, dst, isem.at[i]) for i, (src, dst) in enumerate(zip(sources, targets))]
    for load in loads:
        load.start()

    def tiles(a, b, stage, first, count):
        for i in [first + k for k in range(count)]:
            left = a[:, ds(i, S)].T
            for c in range(b.shape[1] // 512):
                stage[ds(i, S), ds(c, 512)] = dot(left, b[:, ds(c, 512)]).astype(BF16)

    def copy(stage, out, i, sem):
        return pltpu.make_async_copy(stage.at[ds(i, 2 * S), :], out.at[layer, ds(i, 2 * S), :], sem)

    mlp_outs = (ggate_h, gup_h, gdown_h)
    loads[0].wait()
    loads[1].wait()

    def mlp(step):
        which, i = step // 4, lax.rem(step, 4)

        @pl.when(step == 4)
        def _():
            loads[2].wait()

        @pl.when(step == 8)
        def _():
            loads[3].wait()
            loads[4].wait()

        stage = gmlp.at[which]
        tiles(lhs.at[which // 2], rhs.at[which], stage, i * 2, 2)
        for k, out in enumerate(mlp_outs):
            @pl.when(which == k)
            def _():
                copy(stage, out, i, osem.at[k, i]).start()

    loop(12, mlp)
    for load in loads[5:]:
        load.wait()

    def qkv(i):
        tiles(u, dqkv, gqkv, i * 2, 2)
        copy(gqkv, gqkv_h, i, osem.at[3, i]).start()

    loop(4, qkv)
    tiles(o, da, gout, 0, 2)
    copy(gout, gout_h, 0, osem.at[4, 0]).start()
    for i in range(4):
        for k, out in enumerate(mlp_outs):
            copy(gmlp.at[k], out, i, osem.at[k, i]).wait()
        copy(gqkv, gqkv_h, i, osem.at[3, i]).wait()
    copy(gout, gout_h, 0, osem.at[4, 0]).wait()


def vmem():
    return pl.BlockSpec(memory_space=pltpu.VMEM)


def hbm():
    return pl.BlockSpec(memory_space=pl.ANY)


WEIGHT_SCRATCH = [
    pltpu.VMEM((D, NQ), BF16),
    pltpu.VMEM((NO, D), BF16),
    pltpu.VMEM((D, NF), BF16),
    pltpu.VMEM((D, NF), BF16),
    pltpu.VMEM((NF, D), BF16),
]
SCATTER_SCRATCH = [
    pltpu.VMEM((S, D), F32),
    pltpu.VMEM((2, R, D), F32),
    pltpu.VMEM((R, D), BF16),
    pltpu.VMEM((R, D), BF16),
]
SAVED = [(S, D), (S, NQ), (S, NO), (S, D), (S, D), (S, NF), (S, NF), (S, NF), (S, D)]
GRADS = [(D, NQ), (NO, D), (D, NF), (D, NF), (NF, D)]


def run_forward(x, ga, gm, weights):
    dma = pltpu.SemaphoreType.DMA
    return pl.pallas_call(
        forward_kernel,
        name="forward",
        out_shape=[jax.ShapeDtypeStruct((LAYERS - 1, R, D), BF16), jax.ShapeDtypeStruct((R, D), BF16)],
        in_specs=[vmem()] * 3 + [hbm()] * 5,
        out_specs=[vmem()] * 2,
        scratch_shapes=WEIGHT_SCRATCH
        + [
            pltpu.VMEM((R, D), BF16),
            pltpu.VMEM((S, D), BF16),
            pltpu.VMEM((S, D), BF16),
            pltpu.VMEM((S, NQ), BF16),
            pltpu.VMEM((S, NO), BF16),
            pltpu.VMEM((S, NF), BF16),
        ]
        + SCATTER_SCRATCH
        + [dma((5,)), dma((2, 3, 2)), dma((2, 3, 2)), dma((3, 2, 2)), dma((3, 2, 2))],
        compiler_params=pltpu.CompilerParams(collective_id=0, has_side_effects=True, vmem_limit_bytes=VMEM_LIMIT),
    )(x, ga, gm, *weights)


def run_backward(layer, hin, dy, gin, ga, gm, weights):
    dma = pltpu.SemaphoreType.DMA
    last_call = layer == 0
    gshape = [jax.ShapeDtypeStruct((LAYERS, D), F32)] * 2 if last_call else [jax.ShapeDtypeStruct((8, D), F32)]
    saved = [jax.ShapeDtypeStruct(shape, BF16) for shape in SAVED]
    outs = pl.pallas_call(
        functools.partial(backward_kernel, layer),
        name=f"backward{layer}",
        out_shape=[jax.ShapeDtypeStruct((R, D), BF16)] + gshape + saved,
        in_specs=[vmem()] * (4 + len(gin)) + [hbm()] * 5,
        out_specs=[vmem()] * (1 + len(gshape)) + [hbm()] * 9,
        scratch_shapes=[pltpu.VMEM(shape, BF16) for shape in SAVED]
        + WEIGHT_SCRATCH
        + [
            pltpu.VMEM((R, D), BF16),
            pltpu.VMEM((S, NQ), BF16),
            pltpu.VMEM((HEADS, S, S), F32),
            pltpu.VMEM((S, NF), BF16),
            pltpu.VMEM((S, NO), BF16),
        ]
        + SCATTER_SCRATCH
        + [pltpu.VMEM((8, D), F32)] * 3
        + [dma((5,)), dma((9,)), dma((4, 3, 2)), dma((4, 3, 2)), dma((3, 2, 4)), dma((3, 2, 4)), dma((2,)), dma((2,))],
        compiler_params=pltpu.CompilerParams(
            collective_id=1 + layer, has_side_effects=True, vmem_limit_bytes=VMEM_LIMIT
        ),
    )(hin, dy, *gin, ga, gm, *weights)
    return outs[0], outs[1 : 1 + len(gshape)], outs[1 + len(gshape) :]


def run_wgrad(layer, saved, grads):
    dma = pltpu.SemaphoreType.DMA
    n_alias = len(grads)
    return pl.pallas_call(
        functools.partial(wgrad_kernel, layer, n_alias),
        name=f"wgrad{layer}",
        out_shape=[jax.ShapeDtypeStruct((LAYERS, *shape), BF16) for shape in GRADS],
        in_specs=[hbm()] * (9 + n_alias),
        out_specs=[hbm()] * 5,
        input_output_aliases={9 + i: i for i in range(n_alias)},
        scratch_shapes=[pltpu.VMEM(shape, BF16) for shape in SAVED[:4]]
        + [pltpu.VMEM(shape, BF16) for shape in ((2, S, D), (3, S, D), GRADS[0], GRADS[1], (3, D, D))]
        + [dma((9,)), dma((5, 4))],
        compiler_params=pltpu.CompilerParams(vmem_limit_bytes=VMEM_LIMIT),
        cost_estimate=pl.CostEstimate(flops=8_600_000_000, bytes_accessed=42_000_000, transcendentals=0),
    )(*saved, *grads)


def solution(mesh):
    row_spec = P(("dp", "tp"), None)
    col_spec = P(None, None, "tp")
    mid_spec = P(None, "tp", None)
    in_specs = (row_spec, row_spec, P(None, None), P(None, None), col_spec, mid_spec, col_spec, col_spec, mid_spec)
    out_specs = (
        row_spec, row_spec, P("dp", None, "tp"), P("dp", "tp", None), P("dp", None, "tp"), P("dp", None, "tp"),
        P("dp", "tp", None), P("dp", None), P("dp", None),
    )

    def device_step(x, grad_y, gain_attn, gain_mlp, w_qkv, w_out, w_gate, w_up, w_down):
        weights = (w_qkv, w_out, w_gate, w_up, w_down)
        hs, y = run_forward(x, gain_attn, gain_mlp, weights)
        d_hidden = grad_y
        gains = []
        grads = ()
        for layer in reversed(range(LAYERS)):
            d_hidden, gains, saved = run_backward(
                layer, hs if layer > 0 else x, d_hidden, gains, gain_attn, gain_mlp, weights
            )
            grads = run_wgrad(layer, saved, grads)
            if layer > 0:
                d_hidden, grads = lax.optimization_barrier((d_hidden, grads))
        return (y, d_hidden, *grads, *gains)

    return jax.shard_map(device_step, mesh=mesh, in_specs=in_specs, out_specs=out_specs, check_vma=False)
```

time: 433 us -> 378 us (0.87)
  Pallas kernels: 428 us -> 374 us
    pallas_call x3, Pallas kernels: 71.8 us -> 46 us  [run_wgrad(): pl.pallas_call(functools.partial(wgrad_kernel, layer, n_alias), name=f'wg...]
    pallas_call x1, Pallas kernels: 135 us -> 117 us  [run_forward(): pl.pallas_call(forward_kernel, name='forward', out_shape=[jax.ShapeDtypeS...]
    pallas_call x3, Pallas kernels: 221 us -> 212 us  [run_backward(): pl.pallas_call(functools.partial(backward_kernel, layer), name=f'backward...]
where the time goes in v4:
time: 378 us
  Pallas kernels  374 us (99%)
    pallas_call x3, Pallas kernels, run_backward(): pl.pallas_call(functools.partial(backward_kernel, layer), name=f'backward...  212 us
    pallas_call x1, Pallas kernels, run_forward(): pl.pallas_call(forward_kernel, name='forward', out_shape=[jax.ShapeDtypeS...  117 us
    pallas_call x3, Pallas kernels, run_wgrad(): pl.pallas_call(functools.partial(wgrad_kernel, layer, n_alias), name=f'wg...  46 us

profile of v4, /device:TPU:0, one launch (start us, length us, event | category | flops | bytes accessed | tf_op | source)
XLA Modules:
  0.0 377.5 jit_solution(2737857419989205437)
XLA Ops:
  0.6 116.6 %forward.1 = (bf16[2,64,2048]{2,1,0:T(8,128)(2,1)}, bf16[64,2048]{1,0:T(8,128)(2,1)}) custom-call(bf16[64,2048]{1,0:T(8,128)(2,1)} %hin.1, f32[3,2048]{1,0:T(4,128)} %refs_1_.5, f32[3,2048]{1,0:T(4,128)} %refs_2_.5, bf16[3,2048,1536]{2,1,0:T(8,128)(2,1)} %refs_3_.5, bf16[3,512,2048]{2,1,0:T(8,128)(2,1)} %refs_4_.5, bf16[3,2048,2048]{2,1,0:T(8,128)(2,1)} %refs_5_.5, ...), custom_call_target="tpu_custom_call" | custom-call | tf_op jit(solution)/shard_map/forward/pallas_call | solution.py:590
  117.3 68.7 %backward2.1 = (bf16[64,2048]{1,0:T(8,128)(2,1)}, f32[8,2048]{1,0:T(8,128)}, bf16[256,2048]{1,0:T(8,128)(2,1)}, bf16[256,1536]{1,0:T(8,128)(2,1)}, bf16[256,512]...) custom-call(bf16[2,64,2048]{2,1,0:T(8,128)(2,1)} %get-tuple-element., ...), custom_call_target="tpu_custom_call" | custom-call | tf_op jit(solution)/shard_map/backward2/pallas_call | solution.py:616
  186.0 15.4 %wgrad2.1 = (bf16[3,2048,1536]{2,1,0:T(8,128)(2,1)}, bf16[3,512,2048]{2,1,0:T(8,128)(2,1)}, bf16[3,2048,2048]{2,1,0:T(8,128)(2,1)}, bf16[3,2048,2048]{2,1,0:T(8,128)(2,1)}, bf16[3,2048,2048]{2,1,0:T(8,128)(2,1)}) custom-call(bf16[256,2048]{1,0:T(8,128)(2,1)} %get-tuple-element.75.u_h, bf16[256,1536]{1,0:T(8,128)(2,1)} %get-tuple-element.76.dqkv_h, ...), custom_call_target="tpu_custom_call" | custom-call | flops 8600000512 | bytes 42000000 | tf_op jit(solution)/shard_map/wgrad2/pallas_call | solution.py:644
  201.4 68.7 %backward1.1 = (bf16[64,2048]{1,0:T(8,128)(2,1)}, f32[8,2048]{1,0:T(8,128)}, bf16[256,2048]{1,0:T(8,128)(2,1)}, bf16[256,1536]{1,0:T(8,128)(2,1)}, bf16[256,512]...) custom-call(bf16[2,64,2048]{2,1,0:T(8,128)(2,1)} %get-tuple-element., ...), custom_call_target="tpu_custom_call" | custom-call | tf_op jit(solution)/shard_map/backward1/pallas_call | solution.py:616
  270.1 15.2 %wgrad1.1 = (bf16[3,2048,1536]{2,1,0:T(8,128)(2,1)}, bf16[3,512,2048]{2,1,0:T(8,128)(2,1)}, bf16[3,2048,2048]{2,1,0:T(8,128)(2,1)}, bf16[3,2048,2048]{2,1,0:T(8,128)(2,1)}, bf16[3,2048,2048]{2,1,0:T(8,128)(2,1)}) custom-call(bf16[256,2048]{1,0:T(8,128)(2,1)} %get-tuple-element.92.u_h, ...), custom_call_target="tpu_custom_call", output_to_operand_aliasing={{0}: (9, {}), {1}: (10, {}), {2}: (11, {}), {3}: (12, {}), ... | custom-call | flops 8600000512 | bytes 42000000 | tf_op jit(solution)/shard_map/wgrad1/pallas_call | solution.py:644
  285.4 74.1 %backward0.1 = (bf16[64,2048]{1,0:T(8,128)(2,1)}, f32[3,2048]{1,0:T(4,128)}, f32[3,2048]{1,0:T(4,128)}, bf16[256,2048]{1,0:T(8,128)(2,1)}, bf16[256,1536]{1,0:T(...) custom-call(bf16[64,2048]{1,0:T(8,128)(2,1)} %hin.1, ...), custom_call_target="tpu_custom_call" | custom-call | tf_op jit(solution)/shard_map/backward0/pallas_call | solution.py:616
  359.5 0.0 copy-start
  359.5 0.0 copy-start.1
  359.5 0.0 copy-start.3
  359.5 0.0 copy-start.2
  359.6 15.3 %wgrad0.1 = (bf16[3,2048,1536]{2,1,0:T(8,128)(2,1)}, bf16[3,512,2048]{2,1,0:T(8,128)(2,1)}, bf16[3,2048,2048]{2,1,0:T(8,128)(2,1)}, bf16[3,2048,2048]{2,1,0:T(8,128)(2,1)}, bf16[3,2048,2048]{2,1,0:T(8,128)(2,1)}) custom-call(bf16[256,2048]{1,0:T(8,128)(2,1)} %get-tuple-element.114.u_h,, ...), custom_call_target="tpu_custom_call", output_to_operand_aliasing={{0}: (9, {}), {1}: (10, {}), {2}: (11, {}), {3}: (12, {}), ... | custom-call | flops 8600000512 | bytes 42000000 | tf_op jit(solution)/shard_map/wgrad0/pallas_call | solution.py:644
  374.9 0.0 copy-done
  374.9 0.7 copy.42
  375.6 0.0 copy-done.1
  375.6 0.7 copy.43
  376.3 0.0 copy-done.3
  376.3 0.6 copy.44
  376.9 0.0 copy-done.2
  376.9 0.6 copy.45
Async XLA Ops:
  359.5 15.3 %copy-start = (bf16[64,2048]{1,0:T(8,128)(2,1)S(1)}, bf16[64,2048]{1,0:T(8,128)(2,1)}, u32[]{:S(2)}) copy-start(bf16[64,2048]{1,0:T(8,128)(2,1)} %get-tuple-element.144) | copy-start | bytes 786436
  359.5 16.1 %copy-start.1 = (bf16[64,2048]{1,0:T(8,128)(2,1)S(1)}, bf16[64,2048]{1,0:T(8,128)(2,1)}, u32[]{:S(2)}) copy-start(bf16[64,2048]{1,0:T(8,128)(2,1)} %get-tuple-element.145) | copy-start | bytes 786436
  359.5 16.7 %copy-start.3 = (f32[3,2048]{1,0:T(4,128)S(1)}, f32[3,2048]{1,0:T(4,128)}, u32[]{:S(2)}) copy-start(f32[3,2048]{1,0:T(4,128)} %get-tuple-element.151) | copy-start | bytes 73732
  359.5 17.4 %copy-start.2 = (f32[3,2048]{1,0:T(4,128)S(1)}, f32[3,2048]{1,0:T(4,128)}, u32[]{:S(2)}) copy-start(f32[3,2048]{1,0:T(4,128)} %get-tuple-element.152) | copy-start | bytes 73732

commit v5 on v4

--- a/solution.py
+++ b/solution.py
@@ -12,7 +12,7 @@
 MESH = pl.DeviceIdType.MESH
 F32 = jnp.float32
 BF16 = jnp.bfloat16
-VMEM_LIMIT = 66_000_000
+VMEM_LIMIT = 67_000_000
 
 D = 2048
 S = 256
@@ -55,11 +55,11 @@
         self.cross = (1 - chip) * 2 + core
         self.diag = (1 - chip) * 2 + (1 - core)
 
-    def barrier(self):
+    def barrier(self, *more):
         sem = pltpu.get_barrier_semaphore()
-        for peer in (self.sib, self.cross):
+        for peer in (self.sib, self.cross, *more):
             pl.semaphore_signal(sem, inc=1, device_id={"tp": peer}, device_id_type=MESH)
-        pl.semaphore_wait(sem, 2)
+        pl.semaphore_wait(sem, 2 + len(more))
 
 
 def remote(src, dst, send, recv, peer):
@@ -140,12 +140,16 @@
             self.p.cross,
         )
 
-    def _mid(self, half, chunk):
+    def _mid(self, half, chunk, send=True):
         self._near(0, half, chunk).wait_recv()
         cols = ds(chunk, self.width)
         total = self.part[owned(self.p.cross, half), cols] + self.near[0, ds(half, HR), cols]
         self.out[ds(half, HR), cols] = total.astype(BF16)
-        self._far(half, chunk).start()
+        if send:
+            self._far(half, chunk).start()
+
+    def mids(self, half):
+        loop(self.chunks, lambda chunk: self._mid(half, chunk))
 
     def run(self, half, compute):
         def step(chunk):
@@ -155,12 +159,11 @@
             self._near(1, half, chunk).start()
 
         loop(self.chunks, step)
-        loop(self.chunks, lambda chunk: self._mid(half, chunk))
-
-    def run_full(self, compute):
+
+    def run_full(self, compute, send=True):
         def mids(chunk):
-            self._mid(0, chunk)
-            self._mid(1, chunk)
+            self._mid(0, chunk, send)
+            self._mid(1, chunk, send)
 
         def step(chunk):
             cols = ds(chunk, self.width)
@@ -191,6 +194,17 @@
         total = self.part[owned(self.p.me, half), :] + self.near[1, rows, :] + self.far[rows, :].astype(F32)
         loop(self.chunks, sent)
         return total.astype(BF16)
+
+
+    def own_sum(self, own):
+        for half in range(2):
+            for chunk in range(self.chunks):
+                self._near(1, half, chunk).wait_recv()
+            own[ds(half, HR), :] = self.part[owned(self.p.me, half), :] + self.near[1, ds(half, HR), :]
+        for half in range(2):
+            for chunk in range(self.chunks):
+                for kind in range(2):
+                    self._near(kind, half, chunk).wait_send()
 
 
 def norm(h, gain):
@@ -248,11 +262,13 @@
     return body
 
 
-def half_mlp(n, wg, wu, last, tile):
+def half_mlp(n, wg, wu, last, tile, hook=None):
     def body(half):
         rows = ds(half, HS)
 
         def one(j):
+            if hook is not None:
+                hook(half, j)
             for k in range(tile // 512):
                 cols = ds(j * (tile // 512) + k, 512)
                 z1 = dot(n[rows, :], wg[:, cols]).astype(BF16).astype(F32)
@@ -306,7 +322,12 @@
         refill(0)
         attention(qkv, o, 4)
         load(1, layer).wait()
-        loop(2, lambda half: scatter.run(half, lambda rows, cols: dot(o[rows, :], wo[:, cols])))
+
+        def project(half):
+            scatter.run(half, lambda rows, cols: dot(o[rows, :], wo[:, cols]))
+            scatter.mids(half)
+
+        loop(2, project)
         refill(1)
         gu.finish()
 
@@ -319,7 +340,12 @@
         def last(rows, cols, z1, z3):
             m[rows, cols] = (z1 * jax.nn.sigmoid(z1) * z3).astype(BF16)
 
-        gate_up = half_mlp(n, wg, wu, last, 1024)
+        def send_first(half, j):
+            @pl.when((half == 1) & (j == 1))
+            def _():
+                scatter.mids(0)
+
+        gate_up = half_mlp(n, wg, wu, last, 1024, send_first)
         for i in (2, 3, 4):
             load(i, layer).wait()
         gn.relay(0)
@@ -335,6 +361,7 @@
             scatter.run(half, lambda rows, cols: dot(m[rows, :], wd[:, cols]))
 
         loop(2, mlp)
+        scatter.mids(1)
         refill(2)
         refill(3)
         refill(4)
@@ -357,18 +384,26 @@
     loop(LAYERS, layer_step)
 
 
-def backward_kernel(layer, hin, dy, *refs):
+def finish_layer(h, gain, own, far, d_mid, rows):
+    d_in = (own[rows, :] + far[rows, :].astype(F32)).astype(BF16)
+    d_norm, dgain = norm_back(h[rows, :], gain, d_in)
+    return d_mid[rows, :] + d_norm, dgain
+
+
+def backward_kernel(layer, hin, *refs):
     first_call, last_call = layer == LAYERS - 1, layer == 0
     refs = list(refs)
     take = lambda k: [refs.pop(0) for _ in range(k)]
-    gin = None if first_call else take(1)[0]
+    if first_call:
+        (dy,) = take(1)
+    else:
+        h_above, above_own, above_far, above_mid, gin = take(5)
     ga, gm, wq_h, wo_h, wg_h, wu_h, wd_h = take(7)
-    (dx,) = take(1)
-    gouts = take(2 if last_call else 1)
+    own_out, far_out, mid_out, gout = take(4)
     saved_h = take(9)
     u, dqkv, o, da, n, dg, du, m, dd = saved = take(9)
     wq, wo, wg, wu, wd = take(5)
-    hm, qkv, probs, dgated, dh, part, near, out, far, gbuf, gmid, gfar = take(12)
+    hm, qkv, probs, dgated, dh, part, near, out, far, gbuf, gmid, gfar, dy_buf = take(13)
     wsem, osem, gsend, grecv, ssend, srecv, rsend, rrecv = take(8)
 
     p = Peers()
@@ -378,6 +413,8 @@
     for i in (0, 1, 4, 2, 3):
         loads[i].start()
     h = hin.at[layer - 1] if layer > 0 else hin
+    if not first_call:
+        h_above = h_above.at[layer]
     gain_a, gain_m = ga[pl.ds(layer, 1), :], gm[pl.ds(layer, 1), :]
     gu, gd, gn, gda = (Gather(p, buf, gsend, grecv, i) for i, buf in enumerate((u, dd, n, da)))
     two = Scatter(p, part, near, out, far, ssend, srecv, 2)
@@ -388,13 +425,24 @@
         u[owned(p.me, half), :] = norm(h[ds(half, HR), :], gain_a)
         gu.start(half)
 
+    if first_call:
+        gbuf[...] = jnp.zeros_like(gbuf)
+    else:
+        dy = dy_buf
+        gbuf[...] = gin[...]
+
     def enter_d(half):
-        dd[owned(p.me, half), :] = dy[ds(half, HR), :]
+        rows = ds(half, HR)
+        if not first_call:
+            above = layer + 1
+            total, dgain = finish_layer(h_above, ga[above : above + 1, :], above_own, above_far, above_mid, rows)
+            dy[rows, :] = total
+            gbuf[above : above + 1, :] = gbuf[above : above + 1, :] + dgain
+        dd[owned(p.me, half), :] = dy[rows, :]
         gd.start(half)
 
     loop(2, enter)
     loop(2, enter_d)
-    gbuf[...] = jnp.zeros_like(gbuf) if first_call else gin[...]
 
     loads[0].wait()
     gu.each(half_qkv(u, wq, qkv))
@@ -402,7 +450,12 @@
     attention(qkv, o, 2, probs)
     saves[2].start()
     loads[1].wait()
-    loop(2, lambda half: two.run(half, lambda rows, cols: dot(o[rows, :], wo[:, cols])))
+
+    def project(half):
+        two.run(half, lambda rows, cols: dot(o[rows, :], wo[:, cols]))
+        two.mids(half)
+
+    loop(2, project)
 
     loop(2, gd.relay)
     loop(2, gd.arrived)
@@ -433,7 +486,7 @@
         du[rows, cols] = (dm * silu).astype(BF16)
         dg[rows, cols] = (dm * z3 * (sig + silu * (1.0 - sig))).astype(BF16)
 
-    gn.each(half_mlp(n, wg, wu, last, 512))
+    gn.each(half_mlp(n, wg, wu, last, 1024))
     for i in (4, 5, 6, 7):
         saves[i].start()
 
@@ -448,6 +501,9 @@
         gbuf[row, :] = gbuf[row, :] + dgain
 
     loop(2, mid_back)
+    if last_call:
+        near_g = remote(gbuf, gmid, rsend.at[0], rrecv.at[0], p.sib)
+        near_g.start()
 
     def heads(half):
         rows = ds(half, HS)
@@ -466,44 +522,64 @@
         dqkv[:, head_cols(head, 1)] = dot_tn(d_scores, q).astype(BF16)
         dqkv[:, head_cols(head, 2)] = dot_tn(prob.astype(BF16), d_o).astype(BF16)
 
-    per_head(back, 2)
+    per_head(back, 4)
     saves[1].start()
-    four.run_full(lambda cols: dot_nt(dqkv[...], wq[cols, :]))
-
-    def leave(half):
-        rows = ds(half, HR)
-        d_norm, dgain = norm_back(h[rows, :], gain_a, four.result(half))
-        dx[rows, :] = da[owned(p.me, half), :] + d_norm
-        row = pl.ds(layer, 1)
-        gbuf[row, :] = gbuf[row, :] + dgain
-
-    loop(2, leave)
-
     if last_call:
-        near_g = remote(gbuf, gmid, rsend.at[0], rrecv.at[0], p.sib)
-        near_g.start()
         near_g.wait()
         gbuf[...] = gbuf[...] + gmid[...]
         far_g = remote(gbuf, gfar, rsend.at[1], rrecv.at[1], p.cross)
         far_g.start()
+    last_sum = Scatter(p, part, near, far_out, None, ssend, srecv, 4)
+    last_sum.run_full(lambda cols: dot_nt(dqkv[...], wq[cols, :]), send=False)
+    for half in range(2):
+        mid_out[ds(half, HR), :] = da[owned(p.me, half), :]
+    last_sum.own_sum(own_out)
+    if last_call:
         far_g.wait()
-        total = gbuf[...] + gfar[...]
-        gouts[0][...] = total[:LAYERS]
-        gouts[1][...] = total[LAYERS:2 * LAYERS]
+        gout[...] = gbuf[...] + gfar[...]
     else:
-        gouts[0][...] = gbuf[...]
+        gout[...] = gbuf[...]
     for g in (gu, gd, gn, gda):
         g.finish()
     for save in saves:
         save.wait()
 
 
+def closing_kernel(x, own, far, d_mid, gin, ga, dx, ga_out, gm_out, mine, others, send, recv):
+    p = Peers()
+    p.barrier(p.diag)
+    mine[...] = jnp.zeros_like(mine)
+
+    def finish(half):
+        rows = ds(half, HR)
+        total, dgain = finish_layer(x, ga[0:1, :], own, far, d_mid, rows)
+        dx[rows, :] = total
+        mine[0:1, :] = mine[0:1, :] + dgain
+
+    loop(2, finish)
+    copies = [
+        remote(mine, others.at[i], send.at[i], recv.at[i], peer) for i, peer in enumerate((p.cross, p.diag, p.sib))
+    ]
+    for copy in copies:
+        copy.start()
+    ga_out[1:LAYERS, :] = gin[1:LAYERS, :]
+    gm_out[...] = gin[LAYERS : 2 * LAYERS, :]
+    for copy in copies:
+        copy.wait()
+    ga_out[0:1, :] = ((mine[...] + others[2]) + (others[0] + others[1]))[0:1, :]
+
+
 def wgrad_kernel(layer, n_alias, u_h, dqkv_h, o_h, da_h, n_h, dg_h, du_h, m_h, dd_h, *refs):
-    refs = list(refs[n_alias:])
+    refs = list(refs)
     take = lambda k: [refs.pop(0) for _ in range(k)]
+    take(n_alias)
+    y_in = take(1) if n_alias == 0 else ()
     gqkv_h, gout_h, ggate_h, gup_h, gdown_h = take(5)
+    y_out = take(1) if n_alias == 0 else ()
     u, dqkv, o, da, lhs, rhs, gqkv, gout, gmlp = take(9)
     isem, osem = take(2)
+    for y, result in zip(y_in, y_out):
+        result[...] = y[...]
     sources = (n_h, dg_h, du_h, m_h, dd_h, u_h, dqkv_h, o_h, da_h)
     targets = (lhs.at[0], rhs.at[0], rhs.at[1], lhs.at[1], rhs.at[2], u, dqkv, o, da)
     loads = [pltpu.make_async_copy(src, dst, isem.at[i]) for i, (src, dst) in enumerate(zip(sources, targets))]
@@ -565,7 +641,7 @@
 
 
 def hbm():
-    return pl.BlockSpec(memory_space=pl.ANY)
+    return pl.BlockSpec(memory_space=pltpu.HBM)
 
 
 WEIGHT_SCRATCH = [
@@ -608,17 +684,15 @@
     )(x, ga, gm, *weights)
 
 
-def run_backward(layer, hin, dy, gin, ga, gm, weights):
+def run_backward(layer, hin, above, ga, gm, weights):
     dma = pltpu.SemaphoreType.DMA
-    last_call = layer == 0
-    gshape = [jax.ShapeDtypeStruct((LAYERS, D), F32)] * 2 if last_call else [jax.ShapeDtypeStruct((8, D), F32)]
-    saved = [jax.ShapeDtypeStruct(shape, BF16) for shape in SAVED]
+    results = [((R, D), F32), ((R, D), BF16), ((R, D), BF16), ((8, D), F32)] + [(shape, BF16) for shape in SAVED]
     outs = pl.pallas_call(
         functools.partial(backward_kernel, layer),
         name=f"backward{layer}",
-        out_shape=[jax.ShapeDtypeStruct((R, D), BF16)] + gshape + saved,
-        in_specs=[vmem()] * (4 + len(gin)) + [hbm()] * 5,
-        out_specs=[vmem()] * (1 + len(gshape)) + [hbm()] * 9,
+        out_shape=[jax.ShapeDtypeStruct(*result) for result in results],
+        in_specs=[vmem()] * (3 + len(above)) + [hbm()] * 5,
+        out_specs=[vmem()] * 4 + [hbm()] * 9,
         scratch_shapes=[pltpu.VMEM(shape, BF16) for shape in SAVED]
         + WEIGHT_SCRATCH
         + [
@@ -630,30 +704,47 @@
         ]
         + SCATTER_SCRATCH
         + [pltpu.VMEM((8, D), F32)] * 3
+        + [pltpu.VMEM((R, D), BF16)]
         + [dma((5,)), dma((9,)), dma((4, 3, 2)), dma((4, 3, 2)), dma((3, 2, 4)), dma((3, 2, 4)), dma((2,)), dma((2,))],
         compiler_params=pltpu.CompilerParams(
             collective_id=1 + layer, has_side_effects=True, vmem_limit_bytes=VMEM_LIMIT
         ),
-    )(hin, dy, *gin, ga, gm, *weights)
-    return outs[0], outs[1 : 1 + len(gshape)], outs[1 + len(gshape) :]
-
-
-def run_wgrad(layer, saved, grads):
+    )(hin, *above, ga, gm, *weights)
+    return outs[:4], outs[4:]
+
+
+def run_closing(x, above, ga):
+    dma = pltpu.SemaphoreType.DMA
+    return pl.pallas_call(
+        closing_kernel,
+        name="closing",
+        out_shape=[jax.ShapeDtypeStruct((R, D), BF16)] + [jax.ShapeDtypeStruct((LAYERS, D), F32)] * 2,
+        in_specs=[vmem()] * 6,
+        out_specs=[vmem()] * 3,
+        scratch_shapes=[pltpu.VMEM((8, D), F32), pltpu.VMEM((3, 8, D), F32), dma((3,)), dma((3,))],
+        compiler_params=pltpu.CompilerParams(
+            collective_id=1 + LAYERS, has_side_effects=True, vmem_limit_bytes=VMEM_LIMIT
+        ),
+    )(x, *above, ga)
+
+
+def run_wgrad(layer, saved, grads, y=()):
     dma = pltpu.SemaphoreType.DMA
     n_alias = len(grads)
     return pl.pallas_call(
         functools.partial(wgrad_kernel, layer, n_alias),
         name=f"wgrad{layer}",
-        out_shape=[jax.ShapeDtypeStruct((LAYERS, *shape), BF16) for shape in GRADS],
-        in_specs=[hbm()] * (9 + n_alias),
-        out_specs=[hbm()] * 5,
+        out_shape=[jax.ShapeDtypeStruct((LAYERS, *shape), BF16) for shape in GRADS]
+        + [jax.ShapeDtypeStruct((R, D), BF16)] * len(y),
+        in_specs=[hbm()] * (9 + n_alias) + [vmem()] * len(y),
+        out_specs=[hbm()] * 5 + [vmem()] * len(y),
         input_output_aliases={9 + i: i for i in range(n_alias)},
         scratch_shapes=[pltpu.VMEM(shape, BF16) for shape in SAVED[:4]]
         + [pltpu.VMEM(shape, BF16) for shape in ((2, S, D), (3, S, D), GRADS[0], GRADS[1], (3, D, D))]
         + [dma((9,)), dma((5, 4))],
         compiler_params=pltpu.CompilerParams(vmem_limit_bytes=VMEM_LIMIT),
         cost_estimate=pl.CostEstimate(flops=8_600_000_000, bytes_accessed=42_000_000, transcendentals=0),
-    )(*saved, *grads)
+    )(*saved, *grads, *y)
 
 
 def solution(mesh):
@@ -669,16 +760,19 @@
     def device_step(x, grad_y, gain_attn, gain_mlp, w_qkv, w_out, w_gate, w_up, w_down):
         weights = (w_qkv, w_out, w_gate, w_up, w_down)
         hs, y = run_forward(x, gain_attn, gain_mlp, weights)
-        d_hidden = grad_y
-        gains = []
-        grads = ()
+        above = (grad_y,)
+        grads, y = (), (y,)
         for layer in reversed(range(LAYERS)):
-            d_hidden, gains, saved = run_backward(
-                layer, hs if layer > 0 else x, d_hidden, gains, gain_attn, gain_mlp, weights
+            (own, chip_sum, d_mid, gains), saved = run_backward(
+                layer, hs if layer > 0 else x, above, gain_attn, gain_mlp, weights
             )
-            grads = run_wgrad(layer, saved, grads)
-            if layer > 0:
-                d_hidden, grads = lax.optimization_barrier((d_hidden, grads))
-        return (y, d_hidden, *grads, *gains)
+            far = lax.ppermute(chip_sum, "tp", [(0, 2), (1, 3), (2, 0), (3, 1)])
+            grads = run_wgrad(layer, saved, grads, y if layer == LAYERS - 1 else ())
+            if layer == LAYERS - 1:
+                *grads, y = grads
+            far, grads = lax.optimization_barrier((far, tuple(grads)))
+            above = (*((hs,) if layer > 0 else ()), own, far, d_mid, gains)
+        grad_x, *gains = run_closing(x, above, gain_attn)
+        return (y, grad_x, *grads, *gains)
 
     return jax.shard_map(device_step, mesh=mesh, in_specs=in_specs, out_specs=out_specs, check_vma=False)

time: 378 us -> 367 us (0.971)
  Pallas kernels: 374 us -> 362 us
    pallas_call x3, Pallas kernels: 212 us -> 193 us  [run_backward(): pl.pallas_call(functools.partial(backward_kernel, layer), name=f'backward...]
    pallas_call x0 -> x1, Pallas kernels: none -> 8.36 us  [run_closing(): pl.pallas_call(closing_kernel, name='closing', out_shape=[jax.ShapeDtypeS...]
  transfers between devices with their start and end apart: 0 -> 3, of which waited for: 0 -> 0; matrix products, arithmetic and copies ran while one was open for 0% -> 0% of each run, Pallas kernels for 0% -> 13%
where the time goes in v5:
time: 367 us
  Pallas kernels  362 us (99%)
  local copies, waits for them, and re-layouts  4.42 us (1%)
    pallas_call x3, Pallas kernels, run_backward(): pl.pallas_call(functools.partial(backward_kernel, layer), name=f'backward...  193 us
    pallas_call x1, Pallas kernels, run_forward(): pl.pallas_call(forward_kernel, name='forward', out_shape=[jax.ShapeDtypeS...  113 us
    pallas_call x3, Pallas kernels, run_wgrad(): pl.pallas_call(functools.partial(wgrad_kernel, layer, n_alias), name=f'wg...  47.4 us
    pallas_call x1, Pallas kernels, run_closing(): pl.pallas_call(closing_kernel, name='closing', out_shape=[jax.ShapeDtypeS...  8.36 us
  transfers between devices with their start and end apart: 3, of which 0 were waited for; matrix products, arithmetic and copies ran while one was open for 0% of the time, Pallas kernels for 13%

profile of v5, /device:TPU:0, one launch (start us, length us, event | category | flops | bytes accessed | tf_op | source)
XLA Modules:
  0.0 366.8 jit_solution(8068426908978237074)
XLA Ops:
  0.6 112.9 %forward.1 = (bf16[2,64,2048]{2,1,0:T(8,128)(2,1)}, bf16[64,2048]{1,0:T(8,128)(2,1)}) custom-call(bf16[64,2048]{1,0:T(8,128)(2,1)} %x.3, f32[3,2048]{1,0:T(4,128)} %ga.3, f32[3,2048]{1,0:T(4,128)} %refs_6_.5, bf16[3,2048,1536]{2,1,0:T(8,128)(2,1)} %refs_7_.5, bf16[3,512,2048]{2,1,0:T(8,128)(2,1)} %refs_8_.3, bf16[3,2048,2048]{2,1,0:T(8,128)(2,1)} %refs_9_.3, ...), custom_call_target="tpu_custom_call" | custom-call | tf_op jit(solution)/shard_map/forward/pallas_call | solution.py:666
  113.5 64.2 %backward2.1 = (f32[64,2048]{1,0:T(8,128)}, bf16[64,2048]{1,0:T(8,128)(2,1)}, bf16[64,2048]{1,0:T(8,128)(2,1)}, f32[8,2048]{1,0:T(8,128)}, bf16[256,2048]{1,0:T(...) custom-call(bf16[2,64,2048]{2,1,0:T(8,128)(2,1)} %get-tuple-element., ...), custom_call_target="tpu_custom_call" | custom-call | tf_op jit(solution)/shard_map/backward2/pallas_call | solution.py:690
  177.7 0.0 collective-permute-start
  177.8 16.9 %wgrad2.1 = (bf16[3,2048,1536]{2,1,0:T(8,128)(2,1)}, bf16[3,512,2048]{2,1,0:T(8,128)(2,1)}, bf16[3,2048,2048]{2,1,0:T(8,128)(2,1)}, bf16[3,2048,2048]{2,1,0:T(8,...) custom-call(bf16[256,2048]{1,0:T(8,128)(2,1)} %get-tuple-element.88.u_h, ...), custom_call_target="tpu_custom_call" | custom-call | flops 8600000512 | bytes 42000000 | tf_op jit(solution)/shard_map/wgrad2/pallas_call | solution.py:734
  194.7 0.0 collective-permute-done.refs_2_
  194.7 64.4 %backward1.1 = (f32[64,2048]{1,0:T(8,128)}, bf16[64,2048]{1,0:T(8,128)(2,1)}, bf16[64,2048]{1,0:T(8,128)(2,1)}, f32[8,2048]{1,0:T(8,128)}, bf16[256,2048]{1,0:T(...) custom-call(bf16[2,64,2048]{2,1,0:T(8,128)(2,1)} %get-tuple-element., ...), custom_call_target="tpu_custom_call" | custom-call | tf_op jit(solution)/shard_map/backward1/pallas_call | solution.py:690
  259.1 0.0 collective-permute-start.1
  259.1 15.3 %wgrad1.1 = (bf16[3,2048,1536]{2,1,0:T(8,128)(2,1)}, bf16[3,512,2048]{2,1,0:T(8,128)(2,1)}, bf16[3,2048,2048]{2,1,0:T(8,128)(2,1)}, bf16[3,2048,2048]{2,1,0:T(8,128)(2,1)}, bf16[3,2048,2048]{2,1,0:T(8,128)(2,1)}) custom-call(bf16[256,2048]{1,0:T(8,128)(2,1)} %get-tuple-element.111.u_h,, ...), custom_call_target="tpu_custom_call", output_to_operand_aliasing={{0}: (9, {}), {1}: (10, {}), {2}: (11, {}), {3}: (12, {}), ... | custom-call | flops 8600000512 | bytes 42000000 | tf_op jit(solution)/shard_map/wgrad1/pallas_call | solution.py:734
  274.4 0.0 collective-permute-done.1.refs_2_
  274.4 64.3 %backward0.1 = (f32[64,2048]{1,0:T(8,128)}, bf16[64,2048]{1,0:T(8,128)(2,1)}, bf16[64,2048]{1,0:T(8,128)(2,1)}, f32[8,2048]{1,0:T(8,128)}, bf16[256,2048]{1,0:T(...) custom-call(bf16[64,2048]{1,0:T(8,128)(2,1)} %x.3, ...), custom_call_target="tpu_custom_call" | custom-call | tf_op jit(solution)/shard_map/backward0/pallas_call | solution.py:690
  338.7 0.1 collective-permute-start.2
  338.8 15.2 %wgrad0.1 = (bf16[3,2048,1536]{2,1,0:T(8,128)(2,1)}, bf16[3,512,2048]{2,1,0:T(8,128)(2,1)}, bf16[3,2048,2048]{2,1,0:T(8,128)(2,1)}, bf16[3,2048,2048]{2,1,0:T(8,128)(2,1)}, bf16[3,2048,2048]{2,1,0:T(8,128)(2,1)}) custom-call(bf16[256,2048]{1,0:T(8,128)(2,1)} %get-tuple-element.135.u_h,, ...), custom_call_target="tpu_custom_call", output_to_operand_aliasing={{0}: (9, {}), {1}: (10, {}), {2}: (11, {}), {3}: (12, {}), ... | custom-call | flops 8600000512 | bytes 42000000 | tf_op jit(solution)/shard_map/wgrad0/pallas_call | solution.py:734
  354.0 0.0 collective-permute-done.2.far
  354.0 8.4 %closing.1 = (bf16[64,2048]{1,0:T(8,128)(2,1)}, f32[3,2048]{1,0:T(4,128)}, f32[3,2048]{1,0:T(4,128)}) custom-call(bf16[64,2048]{1,0:T(8,128)(2,1)} %x.3, f32[64,2048]{1,0:T(8,128)} %get-tuple-element.133.own, bf16[64,2048]{1,0:T(8,128)(2,1)} %collective-permute-done.2.far, bf16[64,2048]{1,0:T(8,128)(2,1)} %get-tuple-element.155.d_mid, ...), custom_call_target="tpu_custom_call" | custom-call | tf_op jit(solution)/shard_map/closing/pallas_call | solution.py:718
  362.4 1.7 copy.41
  364.1 1.4 copy.42
  365.4 1.4 copy.43
Async XLA Ops:
  177.7 16.9 %collective-permute-start = (bf16[64,2048]{1,0:T(8,128)(2,1)}, bf16[64,2048]{1,0:T(8,128)(2,1)}, u32[]{:S(2)}, u32[]{:S(2)}) collective-permute-start(bf16[64,2048]{1,0:T(8,128)(2,1)} %get-tuple-element.100), channel_id=1, source_target_pairs={{0,2},{1,3},{2,0},{3,1},{4,6},{5,7},{6,4},{7,5}} | collective-permute-start | bytes 786440 | tf_op jit(solution)/shard_map/ppermute | solution.py:769
  259.1 15.3 %collective-permute-start.1 = (bf16[64,2048]{1,0:T(8,128)(2,1)}, bf16[64,2048]{1,0:T(8,128)(2,1)}, u32[]{:S(2)}, u32[]{:S(2)}) collective-permute-start(bf16[64,2048]{1,0:T(8,128)(2,1)} %get-tuple-element.110), channel_id=1, source_target_pairs={{0,2},{1,3},{2,0},{3,1},{4,6},{5,7},{6,4},{7,5}} | collective-permute-start | bytes 786440 | tf_op jit(solution)/shard_map/ppermute | solution.py:769
  338.7 15.3 %collective-permute-start.2 = (bf16[64,2048]{1,0:T(8,128)(2,1)}, bf16[64,2048]{1,0:T(8,128)(2,1)}, u32[]{:S(2)}, u32[]{:S(2)}) collective-permute-start(bf16[64,2048]{1,0:T(8,128)(2,1)} %get-tuple-element.134), channel_id=1, source_target_pairs={{0,2},{1,3},{2,0},{3,1},{4,6},{5,7},{6,4},{7,5}} | collective-permute-start | bytes 786440 | tf_op jit(solution)/shard_map/ppermute | solution.py:769

commit v6 on v5

--- a/solution.py
+++ b/solution.py
@@ -80,36 +80,68 @@
     def __init__(self, p, buf, send, recv, which):
         self.p, self.buf, self.send, self.recv, self.which = p, buf, send, recv, which
 
-    def _copy(self, kind, half, owner, peer):
-        part = self.buf.at[owned(owner, half), :]
-        sems = (self.which, kind, half)
+    def _copy(self, kind, half, chunk, owner, peer):
+        part = self.buf.at[owned(owner, half), ds(chunk, D // 2)]
+        sems = (self.which, kind, half, chunk)
         return remote(part, part, self.send.at[sems], self.recv.at[sems], peer)
 
     def start(self, half):
-        self._copy(0, half, self.p.me, self.p.cross).start()
-        self._copy(1, half, self.p.me, self.p.sib).start()
-
-    def relay(self, half):
-        self._copy(0, half, self.p.cross, self.p.cross).wait_recv()
-        self._copy(2, half, self.p.cross, self.p.sib).start()
-
-    def arrived(self, half):
-        self._copy(1, half, self.p.sib, self.p.sib).wait_recv()
-        self._copy(2, half, self.p.diag, self.p.sib).wait_recv()
-
-    def each(self, body):
+        for chunk in range(2):
+            self._copy(0, half, chunk, self.p.me, self.p.cross).start()
+        for chunk in range(2):
+            self._copy(1, half, chunk, self.p.me, self.p.sib).start()
+
+    def relay(self, half, chunk):
+        self._copy(0, half, chunk, self.p.cross, self.p.cross).wait_recv()
+        self._copy(2, half, chunk, self.p.cross, self.p.sib).start()
+
+    def arrived(self, half, chunk):
+        self._copy(1, half, chunk, self.p.sib, self.p.sib).wait_recv()
+        self._copy(2, half, chunk, self.p.diag, self.p.sib).wait_recv()
+
+    def each(self, bodies, middle=None, after=None):
+        self.relay(0, 0)
+
         def one(half):
-            self.relay(half)
-            self.arrived(half)
-            body(half)
+            @pl.when(half == 0)
+            def _():
+                self.relay(0, 1)
+
+            self.arrived(half, 0)
+            bodies[0](half)
+
+            @pl.when(half == 0)
+            def _():
+                self.relay(1, 0)
+
+            if middle is not None:
+                middle(half)
+            self.arrived(half, 1)
+            bodies[1](half)
+
+            @pl.when(half == 0)
+            def _():
+                self.relay(1, 1)
+
+            if after is not None:
+                after(half)
 
         loop(2, one)
+
+    def all(self):
+        for half in range(2):
+            for chunk in range(2):
+                self.relay(half, chunk)
+        for half in range(2):
+            for chunk in range(2):
+                self.arrived(half, chunk)
 
     def finish(self):
         def one(half):
-            self._copy(0, half, self.p.me, self.p.cross).wait_send()
-            self._copy(1, half, self.p.me, self.p.sib).wait_send()
-            self._copy(2, half, self.p.cross, self.p.sib).wait_send()
+            for chunk in range(2):
+                self._copy(0, half, chunk, self.p.me, self.p.cross).wait_send()
+                self._copy(1, half, chunk, self.p.me, self.p.sib).wait_send()
+                self._copy(2, half, chunk, self.p.cross, self.p.sib).wait_send()
 
         loop(2, one)
 
@@ -253,35 +285,44 @@
     per_head(one, together)
 
 
-def half_qkv(u, wq, qkv):
-    def body(half):
-        rows = ds(half, HS)
+def half_qkv(u, wq, acc, qkv):
+    def body(chunk, half):
+        rows, deep = ds(half, HS), ds(chunk, D // 2)
         for j in range(NQ // 512):
-            qkv[rows, ds(j, 512)] = dot(u[rows, :], wq[:, ds(j, 512)]).astype(BF16)
-
-    return body
-
-
-def half_mlp(n, wg, wu, last, tile, hook=None):
-    def body(half):
-        rows = ds(half, HS)
+            cols = ds(j, 512)
+            part = dot(u[rows, deep], wq[deep, cols])
+            if chunk == 0:
+                acc[:, cols] = part
+            else:
+                qkv[rows, cols] = (acc[:, cols] + part).astype(BF16)
+
+    return [functools.partial(body, chunk) for chunk in range(2)]
+
+
+def half_mlp(n, wg, wu, acc1, acc3, last, tile):
+    def body(chunk, half):
+        rows, deep = ds(half, HS), ds(chunk, D // 2)
 
         def one(j):
-            if hook is not None:
-                hook(half, j)
             for k in range(tile // 512):
                 cols = ds(j * (tile // 512) + k, 512)
-                z1 = dot(n[rows, :], wg[:, cols]).astype(BF16).astype(F32)
-                z3 = dot(n[rows, :], wu[:, cols]).astype(BF16).astype(F32)
-                last(rows, cols, z1, z3)
+                z1 = dot(n[rows, deep], wg[deep, cols])
+                z3 = dot(n[rows, deep], wu[deep, cols])
+                if chunk == 0:
+                    acc1[:, cols] = z1
+                    acc3[:, cols] = z3
+                else:
+                    z1 = (acc1[:, cols] + z1).astype(BF16).astype(F32)
+                    z3 = (acc3[:, cols] + z3).astype(BF16).astype(F32)
+                    last(rows, cols, z1, z3)
 
         loop(NF // tile, one)
 
-    return body
-
-
-def forward_kernel(x, ga, gm, wq_h, wo_h, wg_h, wu_h, wd_h, hs, y,
-                   wq, wo, wg, wu, wd, h, u, n, qkv, o, m, part, near, out, far,
+    return [functools.partial(body, chunk) for chunk in range(2)]
+
+
+def forward_kernel(x, ga, gm, wq_h, wo_h, wg_h, wu_h, wd_h, h1, h2, y,
+                   wq, wo, wg, wu, wd, h, u, n, acc1, acc3, qkv, o, m, part, near, out, far,
                    wsem, gsend, grecv, ssend, srecv):
     p = Peers()
     pairs = ((wq_h, wq), (wo_h, wo), (wg_h, wg), (wu_h, wu), (wd_h, wd))
@@ -318,7 +359,7 @@
                 load(i, layer + 1).start()
 
         load(0, layer).wait()
-        gu.each(half_qkv(u, wq, qkv))
+        gu.each(half_qkv(u, wq, acc1, qkv))
         refill(0)
         attention(qkv, o, 4)
         load(1, layer).wait()
@@ -340,27 +381,19 @@
         def last(rows, cols, z1, z3):
             m[rows, cols] = (z1 * jax.nn.sigmoid(z1) * z3).astype(BF16)
 
-        def send_first(half, j):
-            @pl.when((half == 1) & (j == 1))
+        for i in (2, 3, 4):
+            load(i, layer).wait()
+
+        def send_first(half):
+            @pl.when(half == 1)
             def _():
                 scatter.mids(0)
 
-        gate_up = half_mlp(n, wg, wu, last, 1024, send_first)
-        for i in (2, 3, 4):
-            load(i, layer).wait()
-        gn.relay(0)
-
-        def mlp(half):
-            gn.arrived(half)
-            gate_up(half)
-
-            @pl.when(half == 0)
-            def _():
-                gn.relay(1)
-
-            scatter.run(half, lambda rows, cols: dot(m[rows, :], wd[:, cols]))
-
-        loop(2, mlp)
+        gn.each(
+            half_mlp(n, wg, wu, acc1, acc3, last, 1024),
+            send_first,
+            lambda half: scatter.run(half, lambda rows, cols: dot(m[rows, :], wd[:, cols])),
+        )
         scatter.mids(1)
         refill(2)
         refill(3)
@@ -370,14 +403,14 @@
         def leave(half):
             total = add(half)
 
+            for i, kept in enumerate((h1, h2, y)):
+                @pl.when(layer == i)
+                def _():
+                    kept[ds(half, HR), :] = total
+
             @pl.when(more)
             def _():
-                hs[layer, ds(half, HR), :] = total
                 enter(half, layer + 1)
-
-            @pl.when(jnp.logical_not(more))
-            def _():
-                y[ds(half, HR), :] = total
 
         loop(2, leave)
 
@@ -403,7 +436,7 @@
     saved_h = take(9)
     u, dqkv, o, da, n, dg, du, m, dd = saved = take(9)
     wq, wo, wg, wu, wd = take(5)
-    hm, qkv, probs, dgated, dh, part, near, out, far, gbuf, gmid, gfar, dy_buf = take(13)
+    hm, acc1, acc3, qkv, probs, dgated, dh, part, near, out, far, gbuf, gmid, gfar, dy_buf = take(15)
     wsem, osem, gsend, grecv, ssend, srecv, rsend, rrecv = take(8)
 
     p = Peers()
@@ -412,9 +445,7 @@
     saves = [pltpu.make_async_copy(src, dst, osem.at[i]) for i, (src, dst) in enumerate(zip(saved, saved_h))]
     for i in (0, 1, 4, 2, 3):
         loads[i].start()
-    h = hin.at[layer - 1] if layer > 0 else hin
-    if not first_call:
-        h_above = h_above.at[layer]
+    h = hin
     gain_a, gain_m = ga[pl.ds(layer, 1), :], gm[pl.ds(layer, 1), :]
     gu, gd, gn, gda = (Gather(p, buf, gsend, grecv, i) for i, buf in enumerate((u, dd, n, da)))
     two = Scatter(p, part, near, out, far, ssend, srecv, 2)
@@ -445,7 +476,7 @@
     loop(2, enter_d)
 
     loads[0].wait()
-    gu.each(half_qkv(u, wq, qkv))
+    gu.each(half_qkv(u, wq, acc1, qkv))
     saves[0].start()
     attention(qkv, o, 2, probs)
     saves[2].start()
@@ -457,8 +488,7 @@
 
     loop(2, project)
 
-    loop(2, gd.relay)
-    loop(2, gd.arrived)
+    gd.all()
     saves[8].start()
     loads[4].wait()
 
@@ -486,7 +516,7 @@
         du[rows, cols] = (dm * silu).astype(BF16)
         dg[rows, cols] = (dm * z3 * (sig + silu * (1.0 - sig))).astype(BF16)
 
-    gn.each(half_mlp(n, wg, wu, last, 1024))
+    gn.each(half_mlp(n, wg, wu, acc1, acc3, last, 1024))
     for i in (4, 5, 6, 7):
         saves[i].start()
 
@@ -505,11 +535,15 @@
         near_g = remote(gbuf, gmid, rsend.at[0], rrecv.at[0], p.sib)
         near_g.start()
 
-    def heads(half):
-        rows = ds(half, HS)
-        dh[rows, :] = dot_nt(da[rows, :], wo[...]).astype(BF16)
-
-    gda.each(heads)
+    def heads(chunk, half):
+        rows, deep = ds(half, HS), ds(chunk, D // 2)
+        part_h = dot_nt(da[rows, deep], wo[:, deep])
+        if chunk == 0:
+            acc1[:, :NO] = part_h
+        else:
+            dh[rows, :] = (acc1[:, :NO] + part_h).astype(BF16)
+
+    gda.each([functools.partial(heads, chunk) for chunk in range(2)])
     saves[3].start()
 
     def back(head):
@@ -573,13 +607,9 @@
     refs = list(refs)
     take = lambda k: [refs.pop(0) for _ in range(k)]
     take(n_alias)
-    y_in = take(1) if n_alias == 0 else ()
     gqkv_h, gout_h, ggate_h, gup_h, gdown_h = take(5)
-    y_out = take(1) if n_alias == 0 else ()
     u, dqkv, o, da, lhs, rhs, gqkv, gout, gmlp = take(9)
     isem, osem = take(2)
-    for y, result in zip(y_in, y_out):
-        result[...] = y[...]
     sources = (n_h, dg_h, du_h, m_h, dd_h, u_h, dqkv_h, o_h, da_h)
     targets = (lhs.at[0], rhs.at[0], rhs.at[1], lhs.at[1], rhs.at[2], u, dqkv, o, da)
     loads = [pltpu.make_async_copy(src, dst, isem.at[i]) for i, (src, dst) in enumerate(zip(sources, targets))]
@@ -666,20 +696,22 @@
     return pl.pallas_call(
         forward_kernel,
         name="forward",
-        out_shape=[jax.ShapeDtypeStruct((LAYERS - 1, R, D), BF16), jax.ShapeDtypeStruct((R, D), BF16)],
+        out_shape=[jax.ShapeDtypeStruct((R, D), BF16)] * 3,
         in_specs=[vmem()] * 3 + [hbm()] * 5,
-        out_specs=[vmem()] * 2,
+        out_specs=[vmem()] * 3,
         scratch_shapes=WEIGHT_SCRATCH
         + [
             pltpu.VMEM((R, D), BF16),
             pltpu.VMEM((S, D), BF16),
             pltpu.VMEM((S, D), BF16),
+            pltpu.VMEM((HS, NF), F32),
+            pltpu.VMEM((HS, NF), F32),
             pltpu.VMEM((S, NQ), BF16),
             pltpu.VMEM((S, NO), BF16),
             pltpu.VMEM((S, NF), BF16),
         ]
         + SCATTER_SCRATCH
-        + [dma((5,)), dma((2, 3, 2)), dma((2, 3, 2)), dma((3, 2, 2)), dma((3, 2, 2))],
+        + [dma((5,)), dma((2, 3, 2, 2)), dma((2, 3, 2, 2)), dma((3, 2, 2)), dma((3, 2, 2))],
         compiler_params=pltpu.CompilerParams(collective_id=0, has_side_effects=True, vmem_limit_bytes=VMEM_LIMIT),
     )(x, ga, gm, *weights)
 
@@ -697,6 +729,8 @@
         + WEIGHT_SCRATCH
         + [
             pltpu.VMEM((R, D), BF16),
+            pltpu.VMEM((HS, NF), F32),
+            pltpu.VMEM((HS, NF), F32),
             pltpu.VMEM((S, NQ), BF16),
             pltpu.VMEM((HEADS, S, S), F32),
             pltpu.VMEM((S, NF), BF16),
@@ -705,7 +739,7 @@
         + SCATTER_SCRATCH
         + [pltpu.VMEM((8, D), F32)] * 3
         + [pltpu.VMEM((R, D), BF16)]
-        + [dma((5,)), dma((9,)), dma((4, 3, 2)), dma((4, 3, 2)), dma((3, 2, 4)), dma((3, 2, 4)), dma((2,)), dma((2,))],
+        + [dma((5,)), dma((9,)), dma((4, 3, 2, 2)), dma((4, 3, 2, 2)), dma((3, 2, 4)), dma((3, 2, 4)), dma((2,)), dma((2,))],
         compiler_params=pltpu.CompilerParams(
             collective_id=1 + layer, has_side_effects=True, vmem_limit_bytes=VMEM_LIMIT
         ),
@@ -713,7 +747,7 @@
     return outs[:4], outs[4:]
 
 
-def run_closing(x, above, ga):
+def run_closing(above, ga):
     dma = pltpu.SemaphoreType.DMA
     return pl.pallas_call(
         closing_kernel,
@@ -723,28 +757,27 @@
         out_specs=[vmem()] * 3,
         scratch_shapes=[pltpu.VMEM((8, D), F32), pltpu.VMEM((3, 8, D), F32), dma((3,)), dma((3,))],
         compiler_params=pltpu.CompilerParams(
-            collective_id=1 + LAYERS, has_side_effects=True, vmem_limit_bytes=VMEM_LIMIT
+            collective_id=1 + LAYERS, has_side_effects=True, vmem_limit_bytes=8_000_000
         ),
-    )(x, *above, ga)
-
-
-def run_wgrad(layer, saved, grads, y=()):
+    )(*above, ga)
+
+
+def run_wgrad(layer, saved, grads):
     dma = pltpu.SemaphoreType.DMA
     n_alias = len(grads)
     return pl.pallas_call(
         functools.partial(wgrad_kernel, layer, n_alias),
         name=f"wgrad{layer}",
-        out_shape=[jax.ShapeDtypeStruct((LAYERS, *shape), BF16) for shape in GRADS]
-        + [jax.ShapeDtypeStruct((R, D), BF16)] * len(y),
-        in_specs=[hbm()] * (9 + n_alias) + [vmem()] * len(y),
-        out_specs=[hbm()] * 5 + [vmem()] * len(y),
+        out_shape=[jax.ShapeDtypeStruct((LAYERS, *shape), BF16) for shape in GRADS],
+        in_specs=[hbm()] * (9 + n_alias),
+        out_specs=[hbm()] * 5,
         input_output_aliases={9 + i: i for i in range(n_alias)},
         scratch_shapes=[pltpu.VMEM(shape, BF16) for shape in SAVED[:4]]
         + [pltpu.VMEM(shape, BF16) for shape in ((2, S, D), (3, S, D), GRADS[0], GRADS[1], (3, D, D))]
         + [dma((9,)), dma((5, 4))],
-        compiler_params=pltpu.CompilerParams(vmem_limit_bytes=VMEM_LIMIT),
+        compiler_params=pltpu.CompilerParams(vmem_limit_bytes=VMEM_LIMIT if layer > 0 else 66_200_000),
         cost_estimate=pl.CostEstimate(flops=8_600_000_000, bytes_accessed=42_000_000, transcendentals=0),
-    )(*saved, *grads, *y)
+    )(*saved, *grads)
 
 
 def solution(mesh):
@@ -759,20 +792,18 @@
 
     def device_step(x, grad_y, gain_attn, gain_mlp, w_qkv, w_out, w_gate, w_up, w_down):
         weights = (w_qkv, w_out, w_gate, w_up, w_down)
-        hs, y = run_forward(x, gain_attn, gain_mlp, weights)
-        above = (grad_y,)
-        grads, y = (), (y,)
+        h1, h2, y = run_forward(x, gain_attn, gain_mlp, weights)
+        kept, above = (x, h1, h2), (grad_y,)
+        grads = ()
         for layer in reversed(range(LAYERS)):
             (own, chip_sum, d_mid, gains), saved = run_backward(
-                layer, hs if layer > 0 else x, above, gain_attn, gain_mlp, weights
+                layer, kept[layer], above, gain_attn, gain_mlp, weights
             )
             far = lax.ppermute(chip_sum, "tp", [(0, 2), (1, 3), (2, 0), (3, 1)])
-            grads = run_wgrad(layer, saved, grads, y if layer == LAYERS - 1 else ())
-            if layer == LAYERS - 1:
-                *grads, y = grads
+            grads = run_wgrad(layer, saved, grads)
             far, grads = lax.optimization_barrier((far, tuple(grads)))
-            above = (*((hs,) if layer > 0 else ()), own, far, d_mid, gains)
-        grad_x, *gains = run_closing(x, above, gain_attn)
+            above = (kept[layer], own, far, d_mid, gains)
+        grad_x, *gains = run_closing(above, gain_attn)
         return (y, grad_x, *grads, *gains)
 
     return jax.shard_map(device_step, mesh=mesh, in_specs=in_specs, out_specs=out_specs, check_vma=False)

time: 367 us -> 358 us (0.975)
  Pallas kernels: 362 us -> 349 us
    pallas_call x3, Pallas kernels: 193 us -> 183 us  [run_backward(): pl.pallas_call(functools.partial(backward_kernel, layer), name=f'backward...]
where the time goes in v6:
time: 358 us
  Pallas kernels  349 us (97%)
  local copies, waits for them, and re-layouts  5.39 us (2%)
    pallas_call x3, Pallas kernels, run_backward(): pl.pallas_call(functools.partial(backward_kernel, layer), name=f'backward...  183 us
    pallas_call x1, Pallas kernels, run_forward(): pl.pallas_call(forward_kernel, name='forward', out_shape=[jax.ShapeDtypeS...  113 us
    pallas_call x3, Pallas kernels, run_wgrad(): pl.pallas_call(functools.partial(wgrad_kernel, layer, n_alias), name=f'wg...  46 us
  transfers between devices with their start and end apart: 3, of which 0 were waited for; matrix products, arithmetic and copies ran while one was open for 0% of the time, Pallas kernels for 13%

profile of v6, /device:TPU:0, one launch (start us, length us, event | category | flops | bytes accessed | tf_op | source)
XLA Modules:
  0.0 357.8 jit_solution(16328388086161753833)
XLA Ops:
  0.6 112.8 %forward.1 = (bf16[64,2048]{1,0:T(8,128)(2,1)}, bf16[64,2048]{1,0:T(8,128)(2,1)}, bf16[64,2048]{1,0:T(8,128)(2,1)}) custom-call(bf16[64,2048]{1,0:T(8,128)(2,1)} %x.3, f32[3,2048]{1,0:T(4,128)} %ga.3, f32[3,2048]{1,0:T(4,128)} %refs_6_.5, bf16[3,2048,1536]{2,1,0:T(8,128)(2,1)} %refs_7_.5, bf16[3,512,2048]{2,1,0:T(8,128)(2,1)} %refs_8_.3, ...), custom_call_target="tpu_custom_call" | custom-call | tf_op jit(solution)/shard_map/forward/pallas_call | solution.py:696
  113.5 60.9 %backward2.1 = (f32[64,2048]{1,0:T(8,128)}, bf16[64,2048]{1,0:T(8,128)(2,1)}, bf16[64,2048]{1,0:T(8,128)(2,1)}, f32[8,2048]{1,0:T(8,128)}, bf16[256,2048]{1,0:T(...) custom-call(bf16[64,2048]{1,0:T(8,128)(2,1)} %get-tuple-element.89.h, ...), custom_call_target="tpu_custom_call" | custom-call | tf_op jit(solution)/shard_map/backward2/pallas_call | solution.py:722
  174.3 1.0 collective-permute-start
  175.3 15.3 %wgrad2.1 = (bf16[3,2048,1536]{2,1,0:T(8,128)(2,1)}, bf16[3,512,2048]{2,1,0:T(8,128)(2,1)}, bf16[3,2048,2048]{2,1,0:T(8,128)(2,1)}, bf16[3,2048,2048]{2,1,0:T(8,128)(2,1)}, bf16[3,2048,2048]{2,1,0:T(8,128)(2,1)}) custom-call(bf16[256,2048]{1,0:T(8,128)(2,1)} %get-tuple-element.92.u_h, bf16[256,1536]{1,0:T(8,128)(2,1)} %get-tuple-element.93.dqkv_h, ...), custom_call_target="tpu_custom_call" | custom-call | flops 8600000512 | bytes 42000000 | tf_op jit(solution)/shard_map/wgrad2/pallas_call | solution.py:768
  190.6 0.0 collective-permute-done.refs_2_
  190.6 61.2 %backward1.1 = (f32[64,2048]{1,0:T(8,128)}, bf16[64,2048]{1,0:T(8,128)(2,1)}, bf16[64,2048]{1,0:T(8,128)(2,1)}, f32[8,2048]{1,0:T(8,128)}, bf16[256,2048]{1,0:T(...) custom-call(bf16[64,2048]{1,0:T(8,128)(2,1)} %get-tuple-element.88.h, ...), custom_call_target="tpu_custom_call" | custom-call | tf_op jit(solution)/shard_map/backward1/pallas_call | solution.py:722
  251.8 1.0 collective-permute-start.1
  252.7 15.4 %wgrad1.1 = (bf16[3,2048,1536]{2,1,0:T(8,128)(2,1)}, bf16[3,512,2048]{2,1,0:T(8,128)(2,1)}, bf16[3,2048,2048]{2,1,0:T(8,128)(2,1)}, bf16[3,2048,2048]{2,1,0:T(8,128)(2,1)}, bf16[3,2048,2048]{2,1,0:T(8,128)(2,1)}) custom-call(bf16[256,2048]{1,0:T(8,128)(2,1)} %get-tuple-element.111.u_h,, ...), custom_call_target="tpu_custom_call", output_to_operand_aliasing={{0}: (9, {}), {1}: (10, {}), {2}: (11, {}), {3}: (12, {}), ... | custom-call | flops 8600000512 | bytes 42000000 | tf_op jit(solution)/shard_map/wgrad1/pallas_call | solution.py:768
  268.2 0.0 collective-permute-done.1.refs_2_
  268.2 61.2 %backward0.1 = (f32[64,2048]{1,0:T(8,128)}, bf16[64,2048]{1,0:T(8,128)(2,1)}, bf16[64,2048]{1,0:T(8,128)(2,1)}, f32[8,2048]{1,0:T(8,128)}, bf16[256,2048]{1,0:T(...) custom-call(bf16[64,2048]{1,0:T(8,128)(2,1)} %x.3, ...), custom_call_target="tpu_custom_call" | custom-call | tf_op jit(solution)/shard_map/backward0/pallas_call | solution.py:722
  329.4 1.0 collective-permute-start.2
  330.4 0.0 copy-start
  330.4 0.0 copy-start.1
  330.4 0.0 copy-start.2
  330.4 15.3 %wgrad0.1 = (bf16[3,2048,1536]{2,1,0:T(8,128)(2,1)}, bf16[3,512,2048]{2,1,0:T(8,128)(2,1)}, bf16[3,2048,2048]{2,1,0:T(8,128)(2,1)}, bf16[3,2048,2048]{2,1,0:T(8,128)(2,1)}, bf16[3,2048,2048]{2,1,0:T(8,128)(2,1)}) custom-call(bf16[256,2048]{1,0:T(8,128)(2,1)} %get-tuple-element.135.u_h,, ...), custom_call_target="tpu_custom_call", output_to_operand_aliasing={{0}: (9, {}), {1}: (10, {}), {2}: (11, {}), {3}: (12, {}), ... | custom-call | flops 8600000512 | bytes 42000000 | tf_op jit(solution)/shard_map/wgrad0/pallas_call | solution.py:768
  345.7 0.0 collective-permute-done.2.far
  345.8 0.0 copy-done
  345.8 0.0 copy-done.1
  345.8 0.0 copy-done.2
  345.8 0.0 copy-start.3
  345.8 0.9 copy-done.3
  346.7 0.0 copy-start.4
  346.7 0.8 copy-done.4
  347.6 6.7 %closing.1 = (bf16[64,2048]{1,0:T(8,128)(2,1)S(1)}, f32[3,2048]{1,0:T(4,128)S(1)}, f32[3,2048]{1,0:T(4,128)S(1)}) custom-call(bf16[64,2048]{1,0:T(8,128)(2,1)S(1)} %copy-done, f32[64,2048]{1,0:T(8,128)S(1)} %copy-done.2, bf16[64,2048]{1,0:T(8,128)(2,1)} %collective-permute-done.2.far, bf16[64,2048]{1,0:T(8,128)(2,1)S(1)} %copy-done.3, ...), custom_call_target="tpu_custom_call" | custom-call | tf_op jit(solution)/shard_map/closing/pallas_call | solution.py:752
  354.2 1.7 copy.42
  355.9 0.7 copy.43
  356.6 0.6 copy.44
  357.2 0.6 copy.45
Async XLA Ops:
  174.3 16.2 %collective-permute-start = (bf16[64,2048]{1,0:T(8,128)(2,1)}, bf16[64,2048]{1,0:T(8,128)(2,1)}, u32[]{:S(2)}, u32[]{:S(2)}) collective-permute-start(bf16[64,2048]{1,0:T(8,128)(2,1)} %get-tuple-element.91), channel_id=1, source_target_pairs={{0,2},{1,3},{2,0},{3,1},{4,6},{5,7},{6,4},{7,5}} | collective-permute-start | bytes 786440 | tf_op jit(solution)/shard_map/ppermute | solution.py:802
  251.8 16.4 %collective-permute-start.1 = (bf16[64,2048]{1,0:T(8,128)(2,1)}, bf16[64,2048]{1,0:T(8,128)(2,1)}, u32[]{:S(2)}, u32[]{:S(2)}) collective-permute-start(bf16[64,2048]{1,0:T(8,128)(2,1)} %get-tuple-element.110), channel_id=1, source_target_pairs={{0,2},{1,3},{2,0},{3,1},{4,6},{5,7},{6,4},{7,5}} | collective-permute-start | bytes 786440 | tf_op jit(solution)/shard_map/ppermute | solution.py:802
  329.4 16.3 %collective-permute-start.2 = (bf16[64,2048]{1,0:T(8,128)(2,1)}, bf16[64,2048]{1,0:T(8,128)(2,1)}, u32[]{:S(2)}, u32[]{:S(2)}) collective-permute-start(bf16[64,2048]{1,0:T(8,128)(2,1)} %get-tuple-element.134), channel_id=1, source_target_pairs={{0,2},{1,3},{2,0},{3,1},{4,6},{5,7},{6,4},{7,5}} | collective-permute-start | bytes 786440 | tf_op jit(solution)/shard_map/ppermute | solution.py:802
  330.4 15.3 %copy-start = (bf16[64,2048]{1,0:T(8,128)(2,1)S(1)}, bf16[64,2048]{1,0:T(8,128)(2,1)}, u32[]{:S(2)}) copy-start(bf16[64,2048]{1,0:T(8,128)(2,1)} %x.3) | copy-start | bytes 786436
  330.4 15.3 %copy-start.1 = (f32[3,2048]{1,0:T(4,128)S(1)}, f32[3,2048]{1,0:T(4,128)}, u32[]{:S(2)}) copy-start(f32[3,2048]{1,0:T(4,128)} %ga.3) | copy-start | bytes 73732
  330.4 15.4 %copy-start.2 = (f32[64,2048]{1,0:T(8,128)S(1)}, f32[64,2048]{1,0:T(8,128)}, u32[]{:S(2)}) copy-start(f32[64,2048]{1,0:T(8,128)} %get-tuple-element.133.own) | copy-start | bytes 1572868
  345.8 1.0 copy-start.3
  346.7 0.8 copy-start.4

commit v7 on v6

--- a/solution.py
+++ b/solution.py
@@ -55,11 +55,13 @@
         self.cross = (1 - chip) * 2 + core
         self.diag = (1 - chip) * 2 + (1 - core)
 
-    def barrier(self, *more):
-        sem = pltpu.get_barrier_semaphore()
+    def here(self, *more):
+        self.partners = 2 + len(more)
         for peer in (self.sib, self.cross, *more):
-            pl.semaphore_signal(sem, inc=1, device_id={"tp": peer}, device_id_type=MESH)
-        pl.semaphore_wait(sem, 2 + len(more))
+            pl.semaphore_signal(pltpu.get_barrier_semaphore(), inc=1, device_id={"tp": peer}, device_id_type=MESH)
+
+    def ready(self):
+        pl.semaphore_wait(pltpu.get_barrier_semaphore(), self.partners)
 
 
 def remote(src, dst, send, recv, peer):
@@ -183,14 +185,18 @@
     def mids(self, half):
         loop(self.chunks, lambda chunk: self._mid(half, chunk))
 
-    def run(self, half, compute):
+    def run(self, half, compute, unrolled=False):
         def step(chunk):
             cols = ds(chunk, self.width)
             self.part[ds(half, HS), cols] = compute(ds(half, HS), cols)
             self._near(0, half, chunk).start()
             self._near(1, half, chunk).start()
 
-        loop(self.chunks, step)
+        if unrolled:
+            for chunk in range(self.chunks):
+                step(chunk)
+        else:
+            loop(self.chunks, step)
 
     def run_full(self, compute, send=True):
         def mids(chunk):
@@ -316,7 +322,10 @@
                     z3 = (acc3[:, cols] + z3).astype(BF16).astype(F32)
                     last(rows, cols, z1, z3)
 
-        loop(NF // tile, one)
+        if tile == NF:
+            one(0)
+        else:
+            loop(NF // tile, one)
 
     return [functools.partial(body, chunk) for chunk in range(2)]
 
@@ -330,17 +339,16 @@
     def load(i, layer):
         return pltpu.make_async_copy(pairs[i][0].at[layer], pairs[i][1], wsem.at[i])
 
+    p.here()
     for i in range(5):
         load(i, 0).start()
     h[...] = x[...]
-    p.barrier()
     gu = Gather(p, u, gsend, grecv, 0)
     gn = Gather(p, n, gsend, grecv, 1)
     scatter = Scatter(p, part, near, out, far, ssend, srecv, 2)
 
     def enter(half, layer):
         u[owned(p.me, half), :] = norm(h[ds(half, HR), :], ga[pl.ds(layer, 1), :])
-        gu.start(half)
 
     def add(half):
         rows = ds(half, HR)
@@ -349,6 +357,8 @@
         return total
 
     loop(2, lambda half: enter(half, 0))
+    p.ready()
+    loop(2, gu.start)
 
     def layer_step(layer):
         more = layer < LAYERS - 1
@@ -390,9 +400,9 @@
                 scatter.mids(0)
 
         gn.each(
-            half_mlp(n, wg, wu, acc1, acc3, last, 1024),
+            half_mlp(n, wg, wu, acc1, acc3, last, NF),
             send_first,
-            lambda half: scatter.run(half, lambda rows, cols: dot(m[rows, :], wd[:, cols])),
+            lambda half: scatter.run(half, lambda rows, cols: dot(m[rows, :], wd[:, cols]), True),
         )
         scatter.mids(1)
         refill(2)
@@ -411,6 +421,7 @@
             @pl.when(more)
             def _():
                 enter(half, layer + 1)
+                gu.start(half)
 
         loop(2, leave)
 
@@ -443,6 +454,7 @@
     pairs = ((wq_h, wq), (wo_h, wo), (wg_h, wg), (wu_h, wu), (wd_h, wd))
     loads = [pltpu.make_async_copy(src.at[layer], dst, wsem.at[i]) for i, (src, dst) in enumerate(pairs)]
     saves = [pltpu.make_async_copy(src, dst, osem.at[i]) for i, (src, dst) in enumerate(zip(saved, saved_h))]
+    p.here()
     for i in (0, 1, 4, 2, 3):
         loads[i].start()
     h = hin
@@ -450,11 +462,9 @@
     gu, gd, gn, gda = (Gather(p, buf, gsend, grecv, i) for i, buf in enumerate((u, dd, n, da)))
     two = Scatter(p, part, near, out, far, ssend, srecv, 2)
     four = Scatter(p, part, near, out, far, ssend, srecv, 4)
-    p.barrier()
 
     def enter(half):
         u[owned(p.me, half), :] = norm(h[ds(half, HR), :], gain_a)
-        gu.start(half)
 
     if first_call:
         gbuf[...] = jnp.zeros_like(gbuf)
@@ -473,6 +483,8 @@
         gd.start(half)
 
     loop(2, enter)
+    p.ready()
+    loop(2, gu.start)
     loop(2, enter_d)
 
     loads[0].wait()
@@ -581,7 +593,7 @@
 
 def closing_kernel(x, own, far, d_mid, gin, ga, dx, ga_out, gm_out, mine, others, send, recv):
     p = Peers()
-    p.barrier(p.diag)
+    p.here(p.diag)
     mine[...] = jnp.zeros_like(mine)
 
     def finish(half):
@@ -591,6 +603,7 @@
         mine[0:1, :] = mine[0:1, :] + dgain
 
     loop(2, finish)
+    p.ready()
     copies = [
         remote(mine, others.at[i], send.at[i], recv.at[i], peer) for i, peer in enumerate((p.cross, p.diag, p.sib))
     ]
@@ -607,13 +620,18 @@
     refs = list(refs)
     take = lambda k: [refs.pop(0) for _ in range(k)]
     take(n_alias)
+    passed = n_alias == 0
+    y_in = take(1) if passed else ()
     gqkv_h, gout_h, ggate_h, gup_h, gdown_h = take(5)
-    u, dqkv, o, da, lhs, rhs, gqkv, gout, gmlp = take(9)
-    isem, osem = take(2)
-    sources = (n_h, dg_h, du_h, m_h, dd_h, u_h, dqkv_h, o_h, da_h)
-    targets = (lhs.at[0], rhs.at[0], rhs.at[1], lhs.at[1], rhs.at[2], u, dqkv, o, da)
+    y_out = take(1) if passed else ()
+    u, dqkv, lhs, rhs, gqkv, gwide, y_buf = take(7)
+    isem, osem, ysem = take(3)
+    y_load = [pltpu.make_async_copy(y, y_buf, ysem.at[0]) for y in y_in]
+    y_save = [pltpu.make_async_copy(y_buf, y, ysem.at[1]) for y in y_out]
+    sources = (n_h, dg_h, du_h, m_h, dd_h, o_h, da_h, u_h, dqkv_h)
+    targets = (lhs.at[0], rhs.at[0], rhs.at[1], lhs.at[1], rhs.at[2], lhs.at[2, :, :NO], rhs.at[3], u, dqkv)
     loads = [pltpu.make_async_copy(src, dst, isem.at[i]) for i, (src, dst) in enumerate(zip(sources, targets))]
-    for load in loads:
+    for load in loads + y_load:
         load.start()
 
     def tiles(a, b, stage, first, count):
@@ -625,45 +643,43 @@
     def copy(stage, out, i, sem):
         return pltpu.make_async_copy(stage.at[ds(i, 2 * S), :], out.at[layer, ds(i, 2 * S), :], sem)
 
-    mlp_outs = (ggate_h, gup_h, gdown_h)
+    wide_outs = (ggate_h, gup_h, gdown_h, gout_h)
     loads[0].wait()
     loads[1].wait()
 
-    def mlp(step):
+    def wide(step):
         which, i = step // 4, lax.rem(step, 4)
-
-        @pl.when(step == 4)
-        def _():
-            loads[2].wait()
-
-        @pl.when(step == 8)
-        def _():
-            loads[3].wait()
-            loads[4].wait()
-
-        stage = gmlp.at[which]
-        tiles(lhs.at[which // 2], rhs.at[which], stage, i * 2, 2)
-        for k, out in enumerate(mlp_outs):
+        for at, needed in ((4, loads[2:3]), (8, loads[3:5]), (12, loads[5:7])):
+            @pl.when(step == at)
+            def _():
+                for load in needed:
+                    load.wait()
+
+        stage = gwide.at[which]
+        tiles(lhs.at[jnp.maximum(which - 1, 0)], rhs.at[which], stage, i * 2, 2)
+        for k, out in enumerate(wide_outs):
             @pl.when(which == k)
             def _():
-                copy(stage, out, i, osem.at[k, i]).start()
-
-    loop(12, mlp)
-    for load in loads[5:]:
+                copy(stage, out, i if k < 3 else 0, osem.at[k, i]).start()
+
+    loop(13, wide)
+    for load in loads[7:] + y_load:
         load.wait()
+    for save in y_save:
+        save.start()
 
     def qkv(i):
         tiles(u, dqkv, gqkv, i * 2, 2)
-        copy(gqkv, gqkv_h, i, osem.at[3, i]).start()
+        copy(gqkv, gqkv_h, i, osem.at[4, i]).start()
 
     loop(4, qkv)
-    tiles(o, da, gout, 0, 2)
-    copy(gout, gout_h, 0, osem.at[4, 0]).start()
     for i in range(4):
-        for k, out in enumerate(mlp_outs):
-            copy(gmlp.at[k], out, i, osem.at[k, i]).wait()
-        copy(gqkv, gqkv_h, i, osem.at[3, i]).wait()
-    copy(gout, gout_h, 0, osem.at[4, 0]).wait()
+        for k, out in enumerate(wide_outs[:3]):
+            copy(gwide.at[k], out, i, osem.at[k, i]).wait()
+        copy(gqkv, gqkv_h, i, osem.at[4, i]).wait()
+    copy(gwide.at[3], gout_h, 0, osem.at[3, 0]).wait()
+    for save in y_save:
+        save.wait()
 
 
 def vmem():
@@ -762,22 +778,23 @@
     )(*above, ga)
 
 
-def run_wgrad(layer, saved, grads):
+def run_wgrad(layer, saved, grads, y):
     dma = pltpu.SemaphoreType.DMA
     n_alias = len(grads)
     return pl.pallas_call(
         functools.partial(wgrad_kernel, layer, n_alias),
         name=f"wgrad{layer}",
-        out_shape=[jax.ShapeDtypeStruct((LAYERS, *shape), BF16) for shape in GRADS],
-        in_specs=[hbm()] * (9 + n_alias),
-        out_specs=[hbm()] * 5,
+        out_shape=[jax.ShapeDtypeStruct((LAYERS, *shape), BF16) for shape in GRADS]
+        + [jax.ShapeDtypeStruct((R, D), BF16)] * len(y),
+        in_specs=[hbm()] * (9 + n_alias + len(y)),
+        out_specs=[hbm()] * (5 + len(y)),
         input_output_aliases={9 + i: i for i in range(n_alias)},
-        scratch_shapes=[pltpu.VMEM(shape, BF16) for shape in SAVED[:4]]
-        + [pltpu.VMEM(shape, BF16) for shape in ((2, S, D), (3, S, D), GRADS[0], GRADS[1], (3, D, D))]
-        + [dma((9,)), dma((5, 4))],
+        scratch_shapes=[pltpu.VMEM(shape, BF16) for shape in SAVED[:2]]
+        + [pltpu.VMEM(shape, BF16) for shape in ((3, S, D), (4, S, D), GRADS[0], (4, D, D), (R, D))]
+        + [dma((9,)), dma((5, 4)), dma((2,))],
         compiler_params=pltpu.CompilerParams(vmem_limit_bytes=VMEM_LIMIT if layer > 0 else 66_200_000),
         cost_estimate=pl.CostEstimate(flops=8_600_000_000, bytes_accessed=42_000_000, transcendentals=0),
-    )(*saved, *grads)
+    )(*saved, *grads, *y)
 
 
 def solution(mesh):
@@ -800,7 +817,9 @@
                 layer, kept[layer], above, gain_attn, gain_mlp, weights
             )
             far = lax.ppermute(chip_sum, "tp", [(0, 2), (1, 3), (2, 0), (3, 1)])
-            grads = run_wgrad(layer, saved, grads)
+            grads = run_wgrad(layer, saved, grads, () if grads else (y,))
+            if len(grads) > len(GRADS):
+                *grads, y = grads
             far, grads = lax.optimization_barrier((far, tuple(grads)))
             above = (kept[layer], own, far, d_mid, gains)
         grad_x, *gains = run_closing(above, gain_attn)

time: 358 us -> 352 us (0.983)
  Pallas kernels: 349 us -> 344 us
where the time goes in v7:
time: 352 us
  Pallas kernels  344 us (98%)
  local copies, waits for them, and re-layouts  3.73 us (1%)
    pallas_call x3, Pallas kernels, run_backward(): pl.pallas_call(functools.partial(backward_kernel, layer), name=f'backward...  183 us
    pallas_call x1, Pallas kernels, run_forward(): pl.pallas_call(forward_kernel, name='forward', out_shape=[jax.ShapeDtypeS...  110 us
    pallas_call x3, Pallas kernels, run_wgrad(): pl.pallas_call(functools.partial(wgrad_kernel, layer, n_alias), name=f'wg...  45.4 us
  transfers between devices with their start and end apart: 3, of which 0 were waited for; matrix products, arithmetic and copies ran while one was open for 0% of the time, Pallas kernels for 13%

profile of v7, /device:TPU:0, one launch (start us, length us, event | category | flops | bytes accessed | tf_op | source)
XLA Modules:
  0.0 351.7 jit_solution(11114812695725343714)
XLA Ops:
  0.6 109.6 %forward.1 = (bf16[64,2048]{1,0:T(8,128)(2,1)}, bf16[64,2048]{1,0:T(8,128)(2,1)}, bf16[64,2048]{1,0:T(8,128)(2,1)}) custom-call(bf16[64,2048]{1,0:T(8,128)(2,1)} %x.3, f32[3,2048]{1,0:T(4,128)} %ga.3, f32[3,2048]{1,0:T(4,128)} %refs_6_.5, bf16[3,2048,1536]{2,1,0:T(8,128)(2,1)} %refs_7_.5, bf16[3,512,2048]{2,1,0:T(8,128)(2,1)} %refs_8_.3, ...), custom_call_target="tpu_custom_call" | custom-call | tf_op jit(solution)/shard_map/forward/pallas_call | solution.py:712
  110.2 60.9 %backward2.1 = (f32[64,2048]{1,0:T(8,128)}, bf16[64,2048]{1,0:T(8,128)(2,1)}, bf16[64,2048]{1,0:T(8,128)(2,1)}, f32[8,2048]{1,0:T(8,128)}, bf16[256,2048]{1,0:T(...) custom-call(bf16[64,2048]{1,0:T(8,128)(2,1)} %get-tuple-element.88.h, ...), custom_call_target="tpu_custom_call" | custom-call | tf_op jit(solution)/shard_map/backward2/pallas_call | solution.py:738
  171.1 1.0 collective-permute-start
  172.1 15.1 %wgrad2.1 = (bf16[3,2048,1536]{2,1,0:T(8,128)(2,1)}, bf16[3,512,2048]{2,1,0:T(8,128)(2,1)}, bf16[3,2048,2048]{2,1,0:T(8,128)(2,1)}, bf16[3,2048,2048]{2,1,0:T(8,...) custom-call(bf16[256,2048]{1,0:T(8,128)(2,1)} %get-tuple-element.89.u_h, ...), custom_call_target="tpu_custom_call" | custom-call | flops 8600000512 | bytes 42000000 | tf_op jit(solution)/shard_map/wgrad2/pallas_call | solution.py:784
  187.2 0.0 collective-permute-done.refs_2_
  187.2 61.1 %backward1.1 = (f32[64,2048]{1,0:T(8,128)}, bf16[64,2048]{1,0:T(8,128)(2,1)}, bf16[64,2048]{1,0:T(8,128)(2,1)}, f32[8,2048]{1,0:T(8,128)}, bf16[256,2048]{1,0:T(...) custom-call(bf16[64,2048]{1,0:T(8,128)(2,1)} %get-tuple-element.100., ...), custom_call_target="tpu_custom_call" | custom-call | tf_op jit(solution)/shard_map/backward1/pallas_call | solution.py:738
  248.3 1.0 collective-permute-start.1
  249.3 15.1 %wgrad1.1 = (bf16[3,2048,1536]{2,1,0:T(8,128)(2,1)}, bf16[3,512,2048]{2,1,0:T(8,128)(2,1)}, bf16[3,2048,2048]{2,1,0:T(8,128)(2,1)}, bf16[3,2048,2048]{2,1,0:T(8,128)(2,1)}, bf16[3,2048,2048]{2,1,0:T(8,128)(2,1)}) custom-call(bf16[256,2048]{1,0:T(8,128)(2,1)} %get-tuple-element.113.u_h,, ...), custom_call_target="tpu_custom_call", output_to_operand_aliasing={{0}: (9, {}), {1}: (10, {}), {2}: (11, {}), {3}: (12, {}), ... | custom-call | flops 8600000512 | bytes 42000000 | tf_op jit(solution)/shard_map/wgrad1/pallas_call | solution.py:784
  264.4 0.0 collective-permute-done.1.refs_2_
  264.4 61.1 %backward0.1 = (f32[64,2048]{1,0:T(8,128)}, bf16[64,2048]{1,0:T(8,128)(2,1)}, bf16[64,2048]{1,0:T(8,128)(2,1)}, f32[8,2048]{1,0:T(8,128)}, bf16[256,2048]{1,0:T(...) custom-call(bf16[64,2048]{1,0:T(8,128)(2,1)} %x.3, ...), custom_call_target="tpu_custom_call" | custom-call | tf_op jit(solution)/shard_map/backward0/pallas_call | solution.py:738
  325.5 1.0 collective-permute-start.2
  326.5 0.0 copy-start
  326.5 0.0 copy-start.1
  326.5 0.0 copy-start.2
  326.5 15.2 %wgrad0.1 = (bf16[3,2048,1536]{2,1,0:T(8,128)(2,1)}, bf16[3,512,2048]{2,1,0:T(8,128)(2,1)}, bf16[3,2048,2048]{2,1,0:T(8,128)(2,1)}, bf16[3,2048,2048]{2,1,0:T(8,128)(2,1)}, bf16[3,2048,2048]{2,1,0:T(8,128)(2,1)}) custom-call(bf16[256,2048]{1,0:T(8,128)(2,1)} %get-tuple-element.137.u_h,, ...), custom_call_target="tpu_custom_call", output_to_operand_aliasing={{0}: (9, {}), {1}: (10, {}), {2}: (11, {}), {3}: (12, {}), ... | custom-call | flops 8600000512 | bytes 42000000 | tf_op jit(solution)/shard_map/wgrad0/pallas_call | solution.py:784
  341.6 0.0 collective-permute-done.2.far
  341.6 0.0 copy-done
  341.7 0.0 copy-done.1
  341.7 0.0 copy-done.2
  341.7 0.0 copy-start.3
  341.7 0.9 copy-done.3
  342.6 0.0 copy-start.4
  342.6 0.8 copy-done.4
  343.5 6.2 %closing.1 = (bf16[64,2048]{1,0:T(8,128)(2,1)S(1)}, f32[3,2048]{1,0:T(4,128)S(1)}, f32[3,2048]{1,0:T(4,128)S(1)}) custom-call(bf16[64,2048]{1,0:T(8,128)(2,1)S(1)} %copy-done, f32[64,2048]{1,0:T(8,128)S(1)} %copy-done.2, bf16[64,2048]{1,0:T(8,128)(2,1)} %collective-permute-done.2.far, bf16[64,2048]{1,0:T(8,128)(2,1)S(1)} %copy-done.3, ...), custom_call_target="tpu_custom_call" | custom-call | tf_op jit(solution)/shard_map/closing/pallas_call | solution.py:768
  349.7 0.7 copy.41
  350.4 0.6 copy.42
  351.0 0.6 copy.43
Async XLA Ops:
  171.1 16.1 %collective-permute-start = (bf16[64,2048]{1,0:T(8,128)(2,1)}, bf16[64,2048]{1,0:T(8,128)(2,1)}, u32[]{:S(2)}, u32[]{:S(2)}) collective-permute-start(bf16[64,2048]{1,0:T(8,128)(2,1)} %get-tuple-element.102), channel_id=1, source_target_pairs={{0,2},{1,3},{2,0},{3,1},{4,6},{5,7},{6,4},{7,5}} | collective-permute-start | bytes 786440 | tf_op jit(solution)/shard_map/ppermute | solution.py:819
  248.3 16.1 %collective-permute-start.1 = (bf16[64,2048]{1,0:T(8,128)(2,1)}, bf16[64,2048]{1,0:T(8,128)(2,1)}, u32[]{:S(2)}, u32[]{:S(2)}) collective-permute-start(bf16[64,2048]{1,0:T(8,128)(2,1)} %get-tuple-element.112), channel_id=1, source_target_pairs={{0,2},{1,3},{2,0},{3,1},{4,6},{5,7},{6,4},{7,5}} | collective-permute-start | bytes 786440 | tf_op jit(solution)/shard_map/ppermute | solution.py:819
  325.5 16.2 %collective-permute-start.2 = (bf16[64,2048]{1,0:T(8,128)(2,1)}, bf16[64,2048]{1,0:T(8,128)(2,1)}, u32[]{:S(2)}, u32[]{:S(2)}) collective-permute-start(bf16[64,2048]{1,0:T(8,128)(2,1)} %get-tuple-element.136), channel_id=1, source_target_pairs={{0,2},{1,3},{2,0},{3,1},{4,6},{5,7},{6,4},{7,5}} | collective-permute-start | bytes 786440 | tf_op jit(solution)/shard_map/ppermute | solution.py:819
  326.5 15.2 %copy-start = (bf16[64,2048]{1,0:T(8,128)(2,1)S(1)}, bf16[64,2048]{1,0:T(8,128)(2,1)}, u32[]{:S(2)}) copy-start(bf16[64,2048]{1,0:T(8,128)(2,1)} %x.3) | copy-start | bytes 786436
  326.5 15.2 %copy-start.1 = (f32[3,2048]{1,0:T(4,128)S(1)}, f32[3,2048]{1,0:T(4,128)}, u32[]{:S(2)}) copy-start(f32[3,2048]{1,0:T(4,128)} %ga.3) | copy-start | bytes 73732
  326.5 15.2 %copy-start.2 = (f32[64,2048]{1,0:T(8,128)S(1)}, f32[64,2048]{1,0:T(8,128)}, u32[]{:S(2)}) copy-start(f32[64,2048]{1,0:T(8,128)} %get-tuple-element.135.own) | copy-start | bytes 1572868
  341.7 1.0 copy-start.3
  342.6 0.8 copy-start.4

commit v8 on v7

--- a/solution.py
+++ b/solution.py
@@ -375,7 +375,7 @@
         load(1, layer).wait()
 
         def project(half):
-            scatter.run(half, lambda rows, cols: dot(o[rows, :], wo[:, cols]))
+            scatter.run(half, lambda rows, cols: dot(o[rows, :], wo[:, cols]), True)
             scatter.mids(half)
 
         loop(2, project)
@@ -624,7 +624,7 @@
     y_in = take(1) if passed else ()
     gqkv_h, gout_h, ggate_h, gup_h, gdown_h = take(5)
     y_out = take(1) if passed else ()
-    u, dqkv, lhs, rhs, gqkv, gwide, y_buf = take(7)
+    u, dqkv, lhs, rhs, gqkv, gwide, y_buf, turned = take(8)
     isem, osem, ysem = take(3)
     y_load = [pltpu.make_async_copy(y, y_buf, ysem.at[0]) for y in y_in]
     y_save = [pltpu.make_async_copy(y_buf, y, ysem.at[1]) for y in y_out]
@@ -634,11 +634,14 @@
     for load in loads + y_load:
         load.start()
 
-    def tiles(a, b, stage, first, count):
-        for i in [first + k for k in range(count)]:
-            left = a[:, ds(i, S)].T
+    def pair(a, b, stage, i, following, j):
+        for k in range(2):
             for c in range(b.shape[1] // 512):
-                stage[ds(i, S), ds(c, 512)] = dot(left, b[:, ds(c, 512)]).astype(BF16)
+                stage[ds(2 * i + k, S), ds(c, 512)] = dot(turned[k], b[:, ds(c, 512)]).astype(BF16)
+            if k == 0:
+                turned[1] = a[:, ds(2 * i + 1, S)].T
+            else:
+                turned[0] = following[:, ds(2 * j, S)].T
 
     def copy(stage, out, i, sem):
         return pltpu.make_async_copy(stage.at[ds(i, 2 * S), :], out.at[layer, ds(i, 2 * S), :], sem)
@@ -647,16 +650,20 @@
     loads[0].wait()
     loads[1].wait()
 
+    turned[0] = lhs[0, :, :S].T
+
     def wide(step):
         which, i = step // 4, lax.rem(step, 4)
-        for at, needed in ((4, loads[2:3]), (8, loads[3:5]), (12, loads[5:7])):
+        after = jnp.minimum(step + 1, 12)
+        for at, needed in ((3, loads[2:3]), (7, loads[3:5]), (11, loads[5:7])):
             @pl.when(step == at)
             def _():
                 for load in needed:
                     load.wait()
 
         stage = gwide.at[which]
-        tiles(lhs.at[jnp.maximum(which - 1, 0)], rhs.at[which], stage, i * 2, 2)
+        left = lhs.at[jnp.maximum(which - 1, 0)]
+        pair(left, rhs.at[which], stage, i, lhs.at[jnp.maximum(after // 4 - 1, 0)], lax.rem(after, 4))
         for k, out in enumerate(wide_outs):
             @pl.when(which == k)
             def _():
@@ -668,8 +675,10 @@
     for save in y_save:
         save.start()
 
+    turned[0] = u[:, :S].T
+
     def qkv(i):
-        tiles(u, dqkv, gqkv, i * 2, 2)
+        pair(u, dqkv, gqkv, i, u, jnp.minimum(i + 1, 3))
         copy(gqkv, gqkv_h, i, osem.at[4, i]).start()
 
     loop(4, qkv)
@@ -790,9 +799,9 @@
         out_specs=[hbm()] * (5 + len(y)),
         input_output_aliases={9 + i: i for i in range(n_alias)},
         scratch_shapes=[pltpu.VMEM(shape, BF16) for shape in SAVED[:2]]
-        + [pltpu.VMEM(shape, BF16) for shape in ((3, S, D), (4, S, D), GRADS[0], (4, D, D), (R, D))]
+        + [pltpu.VMEM(shape, BF16) for shape in ((3, S, D), (4, S, D), GRADS[0], (4, D, D), (R, D), (2, S, S))]
         + [dma((9,)), dma((5, 4)), dma((2,))],
-        compiler_params=pltpu.CompilerParams(vmem_limit_bytes=VMEM_LIMIT if layer > 0 else 66_200_000),
+        compiler_params=pltpu.CompilerParams(vmem_limit_bytes=VMEM_LIMIT if layer > 0 else 65_600_000),
         cost_estimate=pl.CostEstimate(flops=8_600_000_000, bytes_accessed=42_000_000, transcendentals=0),
     )(*saved, *grads, *y)
 

time: 352 us -> 349 us (level)
  no operation moved by 1% of the time
where the time goes in v8:
time: 349 us
  Pallas kernels  343 us (98%)
    pallas_call x3, Pallas kernels, run_backward(): pl.pallas_call(functools.partial(backward_kernel, layer), name=f'backward...  183 us
    pallas_call x1, Pallas kernels, run_forward(): pl.pallas_call(forward_kernel, name='forward', out_shape=[jax.ShapeDtypeS...  110 us
    pallas_call x3, Pallas kernels, run_wgrad(): pl.pallas_call(functools.partial(wgrad_kernel, layer, n_alias), name=f'wg...  44.9 us
  transfers between devices with their start and end apart: 3, of which 0 were waited for; matrix products, arithmetic and copies ran while one was open for 0% of the time, Pallas kernels for 13%

profile of v8, /device:TPU:0, one launch (start us, length us, event | category | flops | bytes accessed | tf_op | source)
XLA Modules:
  0.0 348.6 jit_solution(9996461974436668818)
XLA Ops:
  0.6 109.6 %forward.1 = (bf16[64,2048]{1,0:T(8,128)(2,1)}, bf16[64,2048]{1,0:T(8,128)(2,1)}, bf16[64,2048]{1,0:T(8,128)(2,1)}) custom-call(bf16[64,2048]{1,0:T(8,128)(2,1)} %x.3, f32[3,2048]{1,0:T(4,128)} %ga.3, f32[3,2048]{1,0:T(4,128)} %refs_6_.5, bf16[3,2048,1536]{2,1,0:T(8,128)(2,1)} %refs_7_.5, bf16[3,512,2048]{2,1,0:T(8,128)(2,1)} %refs_8_.3, ...), custom_call_target="tpu_custom_call" | custom-call | tf_op jit(solution)/shard_map/forward/pallas_call | solution.py:721
  110.2 60.7 %backward2.1 = (f32[64,2048]{1,0:T(8,128)}, bf16[64,2048]{1,0:T(8,128)(2,1)}, bf16[64,2048]{1,0:T(8,128)(2,1)}, f32[8,2048]{1,0:T(8,128)}, bf16[256,2048]{1,0:T(...) custom-call(bf16[64,2048]{1,0:T(8,128)(2,1)} %get-tuple-element.88.h, ...), custom_call_target="tpu_custom_call" | custom-call | tf_op jit(solution)/shard_map/backward2/pallas_call | solution.py:747
  171.0 1.0 collective-permute-start
  172.0 14.9 %wgrad2.1 = (bf16[3,2048,1536]{2,1,0:T(8,128)(2,1)}, bf16[3,512,2048]{2,1,0:T(8,128)(2,1)}, bf16[3,2048,2048]{2,1,0:T(8,128)(2,1)}, bf16[3,2048,2048]{2,1,0:T(8,...) custom-call(bf16[256,2048]{1,0:T(8,128)(2,1)} %get-tuple-element.89.u_h, ...), custom_call_target="tpu_custom_call" | custom-call | flops 8600000512 | bytes 42000000 | tf_op jit(solution)/shard_map/wgrad2/pallas_call | solution.py:793
  186.9 0.0 collective-permute-done.refs_2_
  186.9 61.3 %backward1.1 = (f32[64,2048]{1,0:T(8,128)}, bf16[64,2048]{1,0:T(8,128)(2,1)}, bf16[64,2048]{1,0:T(8,128)(2,1)}, f32[8,2048]{1,0:T(8,128)}, bf16[256,2048]{1,0:T(...) custom-call(bf16[64,2048]{1,0:T(8,128)(2,1)} %get-tuple-element.100., ...), custom_call_target="tpu_custom_call" | custom-call | tf_op jit(solution)/shard_map/backward1/pallas_call | solution.py:747
  248.2 1.0 collective-permute-start.1
  249.2 14.9 %wgrad1.1 = (bf16[3,2048,1536]{2,1,0:T(8,128)(2,1)}, bf16[3,512,2048]{2,1,0:T(8,128)(2,1)}, bf16[3,2048,2048]{2,1,0:T(8,128)(2,1)}, bf16[3,2048,2048]{2,1,0:T(8,128)(2,1)}, bf16[3,2048,2048]{2,1,0:T(8,128)(2,1)}) custom-call(bf16[256,2048]{1,0:T(8,128)(2,1)} %get-tuple-element.113.u_h,, ...), custom_call_target="tpu_custom_call", output_to_operand_aliasing={{0}: (9, {}), {1}: (10, {}), {2}: (11, {}), {3}: (12, {}), ... | custom-call | flops 8600000512 | bytes 42000000 | tf_op jit(solution)/shard_map/wgrad1/pallas_call | solution.py:793
  264.1 0.0 collective-permute-done.1.refs_2_
  264.1 61.1 %backward0.1 = (f32[64,2048]{1,0:T(8,128)}, bf16[64,2048]{1,0:T(8,128)(2,1)}, bf16[64,2048]{1,0:T(8,128)(2,1)}, f32[8,2048]{1,0:T(8,128)}, bf16[256,2048]{1,0:T(...) custom-call(bf16[64,2048]{1,0:T(8,128)(2,1)} %x.3, ...), custom_call_target="tpu_custom_call" | custom-call | tf_op jit(solution)/shard_map/backward0/pallas_call | solution.py:747
  325.2 1.0 collective-permute-start.2
  326.2 0.0 copy-start
  326.2 0.0 copy-start.1
  326.2 0.0 copy-start.2
  326.2 0.0 copy-start.3
  326.2 0.0 copy-start.4
  326.2 15.0 %wgrad0.1 = (bf16[3,2048,1536]{2,1,0:T(8,128)(2,1)}, bf16[3,512,2048]{2,1,0:T(8,128)(2,1)}, bf16[3,2048,2048]{2,1,0:T(8,128)(2,1)}, bf16[3,2048,2048]{2,1,0:T(8,128)(2,1)}, bf16[3,2048,2048]{2,1,0:T(8,128)(2,1)}) custom-call(bf16[256,2048]{1,0:T(8,128)(2,1)} %get-tuple-element.137.u_h,, ...), custom_call_target="tpu_custom_call", output_to_operand_aliasing={{0}: (9, {}), {1}: (10, {}), {2}: (11, {}), {3}: (12, {}), ... | custom-call | flops 8600000512 | bytes 42000000 | tf_op jit(solution)/shard_map/wgrad0/pallas_call | solution.py:793
  341.2 0.0 collective-permute-done.2.far
  341.2 0.0 copy-done
  341.2 0.0 copy-done.1
  341.3 0.0 copy-done.2
  341.3 0.0 copy-done.3
  341.3 0.0 copy-done.4
  341.3 5.3 %closing.1 = (bf16[64,2048]{1,0:T(8,128)(2,1)S(1)}, f32[3,2048]{1,0:T(4,128)S(1)}, f32[3,2048]{1,0:T(4,128)S(1)}) custom-call(bf16[64,2048]{1,0:T(8,128)(2,1)S(1)} %copy-done, f32[64,2048]{1,0:T(8,128)S(1)} %copy-done.2, bf16[64,2048]{1,0:T(8,128)(2,1)S(1)} %collective-permute-done.2.far, bf16[64,2048]{1,0:T(8,128)(2,1)S(1)} %copy-done.3, ...), custom_call_target="tpu_custom_call" | custom-call | tf_op jit(solution)/shard_map/closing/pallas_call | solution.py:777
  346.6 0.7 copy.41
  347.3 0.6 copy.42
  347.9 0.6 copy.43
Async XLA Ops:
  171.0 15.9 %collective-permute-start = (bf16[64,2048]{1,0:T(8,128)(2,1)}, bf16[64,2048]{1,0:T(8,128)(2,1)}, u32[]{:S(2)}, u32[]{:S(2)}) collective-permute-start(bf16[64,2048]{1,0:T(8,128)(2,1)} %get-tuple-element.102), channel_id=1, source_target_pairs={{0,2},{1,3},{2,0},{3,1},{4,6},{5,7},{6,4},{7,5}} | collective-permute-start | bytes 786440 | tf_op jit(solution)/shard_map/ppermute | solution.py:828
  248.2 15.9 %collective-permute-start.1 = (bf16[64,2048]{1,0:T(8,128)(2,1)}, bf16[64,2048]{1,0:T(8,128)(2,1)}, u32[]{:S(2)}, u32[]{:S(2)}) collective-permute-start(bf16[64,2048]{1,0:T(8,128)(2,1)} %get-tuple-element.112), channel_id=1, source_target_pairs={{0,2},{1,3},{2,0},{3,1},{4,6},{5,7},{6,4},{7,5}} | collective-permute-start | bytes 786440 | tf_op jit(solution)/shard_map/ppermute | solution.py:828
  325.2 16.0 %collective-permute-start.2 = (bf16[64,2048]{1,0:T(8,128)(2,1)}, bf16[64,2048]{1,0:T(8,128)(2,1)S(1)}, u32[]{:S(2)}, u32[]{:S(2)}) collective-permute-start(bf16[64,2048]{1,0:T(8,128)(2,1)} %get-tuple-element.136), channel_id=1, source_target_pairs={{0,2},{1,3},{2,0},{3,1},{4,6},{5,7},{6,4},{7,5}} | collective-permute-start | bytes 786440 | tf_op jit(solution)/shard_map/ppermute | solution.py:828
  326.2 15.1 %copy-start = (bf16[64,2048]{1,0:T(8,128)(2,1)S(1)}, bf16[64,2048]{1,0:T(8,128)(2,1)}, u32[]{:S(2)}) copy-start(bf16[64,2048]{1,0:T(8,128)(2,1)} %x.3) | copy-start | bytes 786436
  326.2 15.1 %copy-start.1 = (f32[3,2048]{1,0:T(4,128)S(1)}, f32[3,2048]{1,0:T(4,128)}, u32[]{:S(2)}) copy-start(f32[3,2048]{1,0:T(4,128)} %ga.3) | copy-start | bytes 73732
  326.2 15.1 %copy-start.2 = (f32[64,2048]{1,0:T(8,128)S(1)}, f32[64,2048]{1,0:T(8,128)}, u32[]{:S(2)}) copy-start(f32[64,2048]{1,0:T(8,128)} %get-tuple-element.135.own) | copy-start | bytes 1572868
  326.2 15.1 %copy-start.3 = (bf16[64,2048]{1,0:T(8,128)(2,1)S(1)}, bf16[64,2048]{1,0:T(8,128)(2,1)}, u32[]{:S(2)}) copy-start(bf16[64,2048]{1,0:T(8,128)(2,1)} %get-tuple-element.157.d_mid) | copy-start | bytes 786436
  326.2 15.1 %copy-start.4 = (f32[8,2048]{1,0:T(8,128)S(1)}, f32[8,2048]{1,0:T(8,128)}, u32[]{:S(2)}) copy-start(f32[8,2048]{1,0:T(8,128)} %get-tuple-element.158.gin) | copy-start | bytes 196612

commit v9 on v8

--- a/solution.py
+++ b/solution.py
@@ -438,16 +438,14 @@
     first_call, last_call = layer == LAYERS - 1, layer == 0
     refs = list(refs)
     take = lambda k: [refs.pop(0) for _ in range(k)]
-    if first_call:
-        (dy,) = take(1)
-    else:
-        h_above, above_own, above_far, above_mid, gin = take(5)
-    ga, gm, wq_h, wo_h, wg_h, wu_h, wd_h = take(7)
+    above_h = take(1 if first_call else 5)
+    ga_h, gm_h, wq_h, wo_h, wg_h, wu_h, wd_h = take(7)
     own_out, far_out, mid_out, gout = take(4)
     saved_h = take(9)
     u, dqkv, o, da, n, dg, du, m, dd = saved = take(9)
     wq, wo, wg, wu, wd = take(5)
-    hm, acc1, acc3, qkv, probs, dgated, dh, part, near, out, far, gbuf, gmid, gfar, dy_buf = take(15)
+    hm, acc1, acc3, qkv, probs, dgated, dh, part, near, out, far, gbuf, gmid, gfar, dy = take(15)
+    h, ga, gm, h_above, above_own, above_far, above_mid, isem = take(8)
     wsem, osem, gsend, grecv, ssend, srecv, rsend, rrecv = take(8)
 
     p = Peers()
@@ -455,9 +453,19 @@
     loads = [pltpu.make_async_copy(src.at[layer], dst, wsem.at[i]) for i, (src, dst) in enumerate(pairs)]
     saves = [pltpu.make_async_copy(src, dst, osem.at[i]) for i, (src, dst) in enumerate(zip(saved, saved_h))]
     p.here()
+    held = (dy,) if first_call else (h_above, above_own, above_far, above_mid, gbuf)
+    inputs = [
+        pltpu.make_async_copy(src, dst, isem.at[i])
+        for i, (src, dst) in enumerate(zip((hin, ga_h, gm_h, *above_h), (h, ga, gm, *held)))
+    ]
+    for copy in inputs:
+        copy.start()
     for i in (0, 1, 4, 2, 3):
         loads[i].start()
-    h = hin
+    if first_call:
+        gbuf[...] = jnp.zeros_like(gbuf)
+    for copy in inputs[:3]:
+        copy.wait()
     gain_a, gain_m = ga[pl.ds(layer, 1), :], gm[pl.ds(layer, 1), :]
     gu, gd, gn, gda = (Gather(p, buf, gsend, grecv, i) for i, buf in enumerate((u, dd, n, da)))
     two = Scatter(p, part, near, out, far, ssend, srecv, 2)
@@ -465,12 +473,6 @@
 
     def enter(half):
         u[owned(p.me, half), :] = norm(h[ds(half, HR), :], gain_a)
-
-    if first_call:
-        gbuf[...] = jnp.zeros_like(gbuf)
-    else:
-        dy = dy_buf
-        gbuf[...] = gin[...]
 
     def enter_d(half):
         rows = ds(half, HR)
@@ -485,6 +487,8 @@
     loop(2, enter)
     p.ready()
     loop(2, gu.start)
+    for copy in inputs[3:]:
+        copy.wait()
     loop(2, enter_d)
 
     loads[0].wait()
@@ -748,7 +752,7 @@
         functools.partial(backward_kernel, layer),
         name=f"backward{layer}",
         out_shape=[jax.ShapeDtypeStruct(*result) for result in results],
-        in_specs=[vmem()] * (3 + len(above)) + [hbm()] * 5,
+        in_specs=[hbm()] * (8 + len(above)),
         out_specs=[vmem()] * 4 + [hbm()] * 9,
         scratch_shapes=[pltpu.VMEM(shape, BF16) for shape in SAVED]
         + WEIGHT_SCRATCH
@@ -763,8 +767,10 @@
         ]
         + SCATTER_SCRATCH
         + [pltpu.VMEM((8, D), F32)] * 3
-        + [pltpu.VMEM((R, D), BF16)]
-        + [dma((5,)), dma((9,)), dma((4, 3, 2, 2)), dma((4, 3, 2, 2)), dma((3, 2, 4)), dma((3, 2, 4)), dma((2,)), dma((2,))],
+        + [pltpu.VMEM((R, D), BF16)] * 2
+        + [pltpu.VMEM((LAYERS, D), F32)] * 2
+        + [pltpu.VMEM((R, D), dtype) for dtype in (BF16, F32, BF16, BF16)]
+        + [dma((8,)), dma((5,)), dma((9,)), dma((4, 3, 2, 2)), dma((4, 3, 2, 2)), dma((3, 2, 4)), dma((3, 2, 4)), dma((2,)), dma((2,))],
         compiler_params=pltpu.CompilerParams(
             collective_id=1 + layer, has_side_effects=True, vmem_limit_bytes=VMEM_LIMIT
         ),

time: 349 us -> 361 us (1.034)
  Pallas kernels: 343 us -> 355 us
    pallas_call x3, Pallas kernels: 183 us -> 196 us  [run_backward(): pl.pallas_call(functools.partial(backward_kernel, layer), name=f'backward...]
  transfers between devices with their start and end apart: 3 -> 3, of which waited for: 0 -> 0; matrix products, arithmetic and copies ran while one was open for 0% -> 0% of each run, Pallas kernels for 13% -> 12%
where the time goes in v9:
time: 361 us
  Pallas kernels  355 us (98%)
    pallas_call x3, Pallas kernels, run_backward(): pl.pallas_call(functools.partial(backward_kernel, layer), name=f'backward...  196 us
    pallas_call x1, Pallas kernels, run_forward(): pl.pallas_call(forward_kernel, name='forward', out_shape=[jax.ShapeDtypeS...  110 us
    pallas_call x3, Pallas kernels, run_wgrad(): pl.pallas_call(functools.partial(wgrad_kernel, layer, n_alias), name=f'wg...  44.9 us
  transfers between devices with their start and end apart: 3, of which 0 were waited for; matrix products, arithmetic and copies ran while one was open for 0% of the time, Pallas kernels for 12%

profile of v9, /device:TPU:0, one launch (start us, length us, event | category | flops | bytes accessed | tf_op | source)
XLA Modules:
  0.0 361.4 jit_solution(345550242769218563)
XLA Ops:
  0.6 109.6 %forward.1 = (bf16[64,2048]{1,0:T(8,128)(2,1)}, bf16[64,2048]{1,0:T(8,128)(2,1)}, bf16[64,2048]{1,0:T(8,128)(2,1)}) custom-call(bf16[64,2048]{1,0:T(8,128)(2,1)} %x.3, f32[3,2048]{1,0:T(4,128)} %ga.3, f32[3,2048]{1,0:T(4,128)} %refs_6_.5, bf16[3,2048,1536]{2,1,0:T(8,128)(2,1)} %refs_7_.5, bf16[3,512,2048]{2,1,0:T(8,128)(2,1)} %refs_8_.3, ...), custom_call_target="tpu_custom_call" | custom-call | tf_op jit(solution)/shard_map/forward/pallas_call | solution.py:725
  110.2 67.2 %backward2.1 = (f32[64,2048]{1,0:T(8,128)}, bf16[64,2048]{1,0:T(8,128)(2,1)}, bf16[64,2048]{1,0:T(8,128)(2,1)}, f32[8,2048]{1,0:T(8,128)}, bf16[256,2048]{1,0:T(...) custom-call(bf16[64,2048]{1,0:T(8,128)(2,1)} %get-tuple-element.88.h, ...), custom_call_target="tpu_custom_call" | custom-call | tf_op jit(solution)/shard_map/backward2/pallas_call | solution.py:751
  177.4 1.1 collective-permute-start
  178.5 14.9 %wgrad2.1 = (bf16[3,2048,1536]{2,1,0:T(8,128)(2,1)}, bf16[3,512,2048]{2,1,0:T(8,128)(2,1)}, bf16[3,2048,2048]{2,1,0:T(8,128)(2,1)}, bf16[3,2048,2048]{2,1,0:T(8,...) custom-call(bf16[256,2048]{1,0:T(8,128)(2,1)} %get-tuple-element.89.u_h, ...), custom_call_target="tpu_custom_call" | custom-call | flops 8600000512 | bytes 42000000 | tf_op jit(solution)/shard_map/wgrad2/pallas_call | solution.py:799
  193.4 0.0 collective-permute-done.refs_2_
  193.4 64.5 %backward1.1 = (f32[64,2048]{1,0:T(8,128)}, bf16[64,2048]{1,0:T(8,128)(2,1)}, bf16[64,2048]{1,0:T(8,128)(2,1)}, f32[8,2048]{1,0:T(8,128)}, bf16[256,2048]{1,0:T(...) custom-call(bf16[64,2048]{1,0:T(8,128)(2,1)} %get-tuple-element.100., ...), custom_call_target="tpu_custom_call" | custom-call | tf_op jit(solution)/shard_map/backward1/pallas_call | solution.py:751
  257.9 1.1 collective-permute-start.1
  259.0 14.9 %wgrad1.1 = (bf16[3,2048,1536]{2,1,0:T(8,128)(2,1)}, bf16[3,512,2048]{2,1,0:T(8,128)(2,1)}, bf16[3,2048,2048]{2,1,0:T(8,128)(2,1)}, bf16[3,2048,2048]{2,1,0:T(8,128)(2,1)}, bf16[3,2048,2048]{2,1,0:T(8,128)(2,1)}) custom-call(bf16[256,2048]{1,0:T(8,128)(2,1)} %get-tuple-element.113.u_h,, ...), custom_call_target="tpu_custom_call", output_to_operand_aliasing={{0}: (9, {}), {1}: (10, {}), {2}: (11, {}), {3}: (12, {}), ... | custom-call | flops 8600000512 | bytes 42000000 | tf_op jit(solution)/shard_map/wgrad1/pallas_call | solution.py:799
  273.9 0.0 collective-permute-done.1.refs_2_
  273.9 64.0 %backward0.1 = (f32[64,2048]{1,0:T(8,128)}, bf16[64,2048]{1,0:T(8,128)(2,1)}, bf16[64,2048]{1,0:T(8,128)(2,1)}, f32[8,2048]{1,0:T(8,128)}, bf16[256,2048]{1,0:T(...) custom-call(bf16[64,2048]{1,0:T(8,128)(2,1)} %x.3, ...), custom_call_target="tpu_custom_call" | custom-call | tf_op jit(solution)/shard_map/backward0/pallas_call | solution.py:751
  337.9 1.1 collective-permute-start.2
  339.0 0.0 copy-start
  339.0 0.0 copy-start.1
  339.0 0.0 copy-start.2
  339.0 0.0 copy-start.3
  339.0 0.0 copy-start.4
  339.0 15.0 %wgrad0.1 = (bf16[3,2048,1536]{2,1,0:T(8,128)(2,1)}, bf16[3,512,2048]{2,1,0:T(8,128)(2,1)}, bf16[3,2048,2048]{2,1,0:T(8,128)(2,1)}, bf16[3,2048,2048]{2,1,0:T(8,128)(2,1)}, bf16[3,2048,2048]{2,1,0:T(8,128)(2,1)}) custom-call(bf16[256,2048]{1,0:T(8,128)(2,1)} %get-tuple-element.137.u_h,, ...), custom_call_target="tpu_custom_call", output_to_operand_aliasing={{0}: (9, {}), {1}: (10, {}), {2}: (11, {}), {3}: (12, {}), ... | custom-call | flops 8600000512 | bytes 42000000 | tf_op jit(solution)/shard_map/wgrad0/pallas_call | solution.py:799
  354.0 0.0 collective-permute-done.2.far
  354.1 0.0 copy-done
  354.1 0.0 copy-done.1
  354.1 0.0 copy-done.2
  354.1 0.0 copy-done.3
  354.1 0.0 copy-done.4
  354.1 5.3 %closing.1 = (bf16[64,2048]{1,0:T(8,128)(2,1)S(1)}, f32[3,2048]{1,0:T(4,128)S(1)}, f32[3,2048]{1,0:T(4,128)S(1)}) custom-call(bf16[64,2048]{1,0:T(8,128)(2,1)S(1)} %copy-done, f32[64,2048]{1,0:T(8,128)S(1)} %copy-done.2, bf16[64,2048]{1,0:T(8,128)(2,1)S(1)} %collective-permute-done.2.far, bf16[64,2048]{1,0:T(8,128)(2,1)S(1)} %copy-done.3, ...), custom_call_target="tpu_custom_call" | custom-call | tf_op jit(solution)/shard_map/closing/pallas_call | solution.py:783
  359.4 0.7 copy.41
  360.2 0.6 copy.42
  360.8 0.6 copy.43
Async XLA Ops:
  177.4 16.0 %collective-permute-start = (bf16[64,2048]{1,0:T(8,128)(2,1)}, bf16[64,2048]{1,0:T(8,128)(2,1)}, u32[]{:S(2)}, u32[]{:S(2)}) collective-permute-start(bf16[64,2048]{1,0:T(8,128)(2,1)} %get-tuple-element.102), channel_id=1, source_target_pairs={{0,2},{1,3},{2,0},{3,1},{4,6},{5,7},{6,4},{7,5}} | collective-permute-start | bytes 786440 | tf_op jit(solution)/shard_map/ppermute | solution.py:834
  257.9 16.0 %collective-permute-start.1 = (bf16[64,2048]{1,0:T(8,128)(2,1)}, bf16[64,2048]{1,0:T(8,128)(2,1)}, u32[]{:S(2)}, u32[]{:S(2)}) collective-permute-start(bf16[64,2048]{1,0:T(8,128)(2,1)} %get-tuple-element.112), channel_id=1, source_target_pairs={{0,2},{1,3},{2,0},{3,1},{4,6},{5,7},{6,4},{7,5}} | collective-permute-start | bytes 786440 | tf_op jit(solution)/shard_map/ppermute | solution.py:834
  337.9 16.1 %collective-permute-start.2 = (bf16[64,2048]{1,0:T(8,128)(2,1)}, bf16[64,2048]{1,0:T(8,128)(2,1)S(1)}, u32[]{:S(2)}, u32[]{:S(2)}) collective-permute-start(bf16[64,2048]{1,0:T(8,128)(2,1)} %get-tuple-element.136), channel_id=1, source_target_pairs={{0,2},{1,3},{2,0},{3,1},{4,6},{5,7},{6,4},{7,5}} | collective-permute-start | bytes 786440 | tf_op jit(solution)/shard_map/ppermute | solution.py:834
  339.0 15.1 %copy-start = (bf16[64,2048]{1,0:T(8,128)(2,1)S(1)}, bf16[64,2048]{1,0:T(8,128)(2,1)}, u32[]{:S(2)}) copy-start(bf16[64,2048]{1,0:T(8,128)(2,1)} %x.3) | copy-start | bytes 786436
  339.0 15.1 %copy-start.1 = (f32[3,2048]{1,0:T(4,128)S(1)}, f32[3,2048]{1,0:T(4,128)}, u32[]{:S(2)}) copy-start(f32[3,2048]{1,0:T(4,128)} %ga.3) | copy-start | bytes 73732
  339.0 15.1 %copy-start.2 = (f32[64,2048]{1,0:T(8,128)S(1)}, f32[64,2048]{1,0:T(8,128)}, u32[]{:S(2)}) copy-start(f32[64,2048]{1,0:T(8,128)} %get-tuple-element.135.own) | copy-start | bytes 1572868
  339.0 15.1 %copy-start.3 = (bf16[64,2048]{1,0:T(8,128)(2,1)S(1)}, bf16[64,2048]{1,0:T(8,128)(2,1)}, u32[]{:S(2)}) copy-start(bf16[64,2048]{1,0:T(8,128)(2,1)} %get-tuple-element.157.d_mid) | copy-start | bytes 786436
  339.0 15.1 %copy-start.4 = (f32[8,2048]{1,0:T(8,128)S(1)}, f32[8,2048]{1,0:T(8,128)}, u32[]{:S(2)}) copy-start(f32[8,2048]{1,0:T(8,128)} %get-tuple-element.158.gin) | copy-start | bytes 196612

commit v10 on v8

--- a/solution.py
+++ b/solution.py
@@ -41,6 +41,13 @@
 
 def ds(i, n):
     return pl.ds(i * n if isinstance(i, int) else pl.multiple_of(i * n, n), n)
+
+
+def short(n, body):
+    if n > 2:
+        return loop(n, body)
+    for i in range(n):
+        body(i)
 
 
 def loop(n, body):
@@ -183,7 +190,7 @@
             self._far(half, chunk).start()
 
     def mids(self, half):
-        loop(self.chunks, lambda chunk: self._mid(half, chunk))
+        short(self.chunks, lambda chunk: self._mid(half, chunk))
 
     def run(self, half, compute, unrolled=False):
         def step(chunk):
@@ -227,10 +234,10 @@
             self._near(1, half, chunk).wait_send()
             self._far(half, chunk).wait_send()
 
-        loop(self.chunks, waits)
+        short(self.chunks, waits)
         rows = ds(half, HR)
         total = self.part[owned(self.p.me, half), :] + self.near[1, rows, :] + self.far[rows, :].astype(F32)
-        loop(self.chunks, sent)
+        short(self.chunks, sent)
         return total.astype(BF16)
 
 

time: 349 us -> 349 us (level)
  no operation moved by 1% of the time
where the time goes in v10:
time: 349 us; the launch traced here: 348 us
  Pallas kernels  343 us (98%)
    pallas_call x3, Pallas kernels, run_backward(): pl.pallas_call(functools.partial(backward_kernel, layer), name=f'backward...  183 us
    pallas_call x1, Pallas kernels, run_forward(): pl.pallas_call(forward_kernel, name='forward', out_shape=[jax.ShapeDtypeS...  110 us
    pallas_call x3, Pallas kernels, run_wgrad(): pl.pallas_call(functools.partial(wgrad_kernel, layer, n_alias), name=f'wg...  44.9 us
  transfers between devices with their start and end apart: 3, of which 0 were waited for; matrix products, arithmetic and copies ran while one was open for 0% of the time, Pallas kernels for 13%

profile of v10, /device:TPU:0, one launch (start us, length us, event | category | flops | bytes accessed | tf_op | source)
XLA Modules:
  0.0 348.5 jit_solution(3002687951912830022)
XLA Ops:
  0.6 109.6 %forward.1 = (bf16[64,2048]{1,0:T(8,128)(2,1)}, bf16[64,2048]{1,0:T(8,128)(2,1)}, bf16[64,2048]{1,0:T(8,128)(2,1)}) custom-call(bf16[64,2048]{1,0:T(8,128)(2,1)} %x.3, f32[3,2048]{1,0:T(4,128)} %ga.3, f32[3,2048]{1,0:T(4,128)} %refs_6_.5, bf16[3,2048,1536]{2,1,0:T(8,128)(2,1)} %refs_7_.5, bf16[3,512,2048]{2,1,0:T(8,128)(2,1)} %refs_8_.3, ...), custom_call_target="tpu_custom_call" | custom-call | tf_op jit(solution)/shard_map/forward/pallas_call | solution.py:728
  110.2 60.7 %backward2.1 = (f32[64,2048]{1,0:T(8,128)}, bf16[64,2048]{1,0:T(8,128)(2,1)}, bf16[64,2048]{1,0:T(8,128)(2,1)}, f32[8,2048]{1,0:T(8,128)}, bf16[256,2048]{1,0:T(...) custom-call(bf16[64,2048]{1,0:T(8,128)(2,1)} %get-tuple-element.88.h, ...), custom_call_target="tpu_custom_call" | custom-call | tf_op jit(solution)/shard_map/backward2/pallas_call | solution.py:754
  171.0 1.0 collective-permute-start
  171.9 14.9 %wgrad2.1 = (bf16[3,2048,1536]{2,1,0:T(8,128)(2,1)}, bf16[3,512,2048]{2,1,0:T(8,128)(2,1)}, bf16[3,2048,2048]{2,1,0:T(8,128)(2,1)}, bf16[3,2048,2048]{2,1,0:T(8,...) custom-call(bf16[256,2048]{1,0:T(8,128)(2,1)} %get-tuple-element.89.u_h, ...), custom_call_target="tpu_custom_call" | custom-call | flops 8600000512 | bytes 42000000 | tf_op jit(solution)/shard_map/wgrad2/pallas_call | solution.py:800
  186.9 0.0 collective-permute-done.refs_2_
  186.9 61.3 %backward1.1 = (f32[64,2048]{1,0:T(8,128)}, bf16[64,2048]{1,0:T(8,128)(2,1)}, bf16[64,2048]{1,0:T(8,128)(2,1)}, f32[8,2048]{1,0:T(8,128)}, bf16[256,2048]{1,0:T(...) custom-call(bf16[64,2048]{1,0:T(8,128)(2,1)} %get-tuple-element.100., ...), custom_call_target="tpu_custom_call" | custom-call | tf_op jit(solution)/shard_map/backward1/pallas_call | solution.py:754
  248.2 1.0 collective-permute-start.1
  249.1 14.9 %wgrad1.1 = (bf16[3,2048,1536]{2,1,0:T(8,128)(2,1)}, bf16[3,512,2048]{2,1,0:T(8,128)(2,1)}, bf16[3,2048,2048]{2,1,0:T(8,128)(2,1)}, bf16[3,2048,2048]{2,1,0:T(8,128)(2,1)}, bf16[3,2048,2048]{2,1,0:T(8,128)(2,1)}) custom-call(bf16[256,2048]{1,0:T(8,128)(2,1)} %get-tuple-element.113.u_h,, ...), custom_call_target="tpu_custom_call", output_to_operand_aliasing={{0}: (9, {}), {1}: (10, {}), {2}: (11, {}), {3}: (12, {}), ... | custom-call | flops 8600000512 | bytes 42000000 | tf_op jit(solution)/shard_map/wgrad1/pallas_call | solution.py:800
  264.1 0.0 collective-permute-done.1.refs_2_
  264.1 61.1 %backward0.1 = (f32[64,2048]{1,0:T(8,128)}, bf16[64,2048]{1,0:T(8,128)(2,1)}, bf16[64,2048]{1,0:T(8,128)(2,1)}, f32[8,2048]{1,0:T(8,128)}, bf16[256,2048]{1,0:T(...) custom-call(bf16[64,2048]{1,0:T(8,128)(2,1)} %x.3, ...), custom_call_target="tpu_custom_call" | custom-call | tf_op jit(solution)/shard_map/backward0/pallas_call | solution.py:754
  325.1 1.0 collective-permute-start.2
  326.1 0.0 copy-start
  326.1 0.0 copy-start.1
  326.1 0.0 copy-start.2
  326.1 0.0 copy-start.3
  326.1 0.0 copy-start.4
  326.1 15.0 %wgrad0.1 = (bf16[3,2048,1536]{2,1,0:T(8,128)(2,1)}, bf16[3,512,2048]{2,1,0:T(8,128)(2,1)}, bf16[3,2048,2048]{2,1,0:T(8,128)(2,1)}, bf16[3,2048,2048]{2,1,0:T(8,128)(2,1)}, bf16[3,2048,2048]{2,1,0:T(8,128)(2,1)}) custom-call(bf16[256,2048]{1,0:T(8,128)(2,1)} %get-tuple-element.137.u_h,, ...), custom_call_target="tpu_custom_call", output_to_operand_aliasing={{0}: (9, {}), {1}: (10, {}), {2}: (11, {}), {3}: (12, {}), ... | custom-call | flops 8600000512 | bytes 42000000 | tf_op jit(solution)/shard_map/wgrad0/pallas_call | solution.py:800
  341.2 0.0 collective-permute-done.2.far
  341.2 0.0 copy-done
  341.2 0.0 copy-done.1
  341.2 0.0 copy-done.2
  341.2 0.0 copy-done.3
  341.2 0.0 copy-done.4
  341.2 5.3 %closing.1 = (bf16[64,2048]{1,0:T(8,128)(2,1)S(1)}, f32[3,2048]{1,0:T(4,128)S(1)}, f32[3,2048]{1,0:T(4,128)S(1)}) custom-call(bf16[64,2048]{1,0:T(8,128)(2,1)S(1)} %copy-done, f32[64,2048]{1,0:T(8,128)S(1)} %copy-done.2, bf16[64,2048]{1,0:T(8,128)(2,1)S(1)} %collective-permute-done.2.far, bf16[64,2048]{1,0:T(8,128)(2,1)S(1)} %copy-done.3, ...), custom_call_target="tpu_custom_call" | custom-call | tf_op jit(solution)/shard_map/closing/pallas_call | solution.py:784
  346.6 0.7 copy.41
  347.3 0.6 copy.42
  347.9 0.6 copy.43
Async XLA Ops:
  171.0 15.9 %collective-permute-start = (bf16[64,2048]{1,0:T(8,128)(2,1)}, bf16[64,2048]{1,0:T(8,128)(2,1)}, u32[]{:S(2)}, u32[]{:S(2)}) collective-permute-start(bf16[64,2048]{1,0:T(8,128)(2,1)} %get-tuple-element.102), channel_id=1, source_target_pairs={{0,2},{1,3},{2,0},{3,1},{4,6},{5,7},{6,4},{7,5}} | collective-permute-start | bytes 786440 | tf_op jit(solution)/shard_map/ppermute | solution.py:835
  248.2 15.9 %collective-permute-start.1 = (bf16[64,2048]{1,0:T(8,128)(2,1)}, bf16[64,2048]{1,0:T(8,128)(2,1)}, u32[]{:S(2)}, u32[]{:S(2)}) collective-permute-start(bf16[64,2048]{1,0:T(8,128)(2,1)} %get-tuple-element.112), channel_id=1, source_target_pairs={{0,2},{1,3},{2,0},{3,1},{4,6},{5,7},{6,4},{7,5}} | collective-permute-start | bytes 786440 | tf_op jit(solution)/shard_map/ppermute | solution.py:835
  325.1 16.0 %collective-permute-start.2 = (bf16[64,2048]{1,0:T(8,128)(2,1)}, bf16[64,2048]{1,0:T(8,128)(2,1)S(1)}, u32[]{:S(2)}, u32[]{:S(2)}) collective-permute-start(bf16[64,2048]{1,0:T(8,128)(2,1)} %get-tuple-element.136), channel_id=1, source_target_pairs={{0,2},{1,3},{2,0},{3,1},{4,6},{5,7},{6,4},{7,5}} | collective-permute-start | bytes 786440 | tf_op jit(solution)/shard_map/ppermute | solution.py:835
  326.1 15.1 %copy-start = (bf16[64,2048]{1,0:T(8,128)(2,1)S(1)}, bf16[64,2048]{1,0:T(8,128)(2,1)}, u32[]{:S(2)}) copy-start(bf16[64,2048]{1,0:T(8,128)(2,1)} %x.3) | copy-start | bytes 786436
  326.1 15.1 %copy-start.1 = (f32[3,2048]{1,0:T(4,128)S(1)}, f32[3,2048]{1,0:T(4,128)}, u32[]{:S(2)}) copy-start(f32[3,2048]{1,0:T(4,128)} %ga.3) | copy-start | bytes 73732
  326.1 15.1 %copy-start.2 = (f32[64,2048]{1,0:T(8,128)S(1)}, f32[64,2048]{1,0:T(8,128)}, u32[]{:S(2)}) copy-start(f32[64,2048]{1,0:T(8,128)} %get-tuple-element.135.own) | copy-start | bytes 1572868
  326.1 15.1 %copy-start.3 = (bf16[64,2048]{1,0:T(8,128)(2,1)S(1)}, bf16[64,2048]{1,0:T(8,128)(2,1)}, u32[]{:S(2)}) copy-start(bf16[64,2048]{1,0:T(8,128)(2,1)} %get-tuple-element.157.d_mid) | copy-start | bytes 786436
  326.1 15.1 %copy-start.4 = (f32[8,2048]{1,0:T(8,128)S(1)}, f32[8,2048]{1,0:T(8,128)}, u32[]{:S(2)}) copy-start(f32[8,2048]{1,0:T(8,128)} %get-tuple-element.158.gin) | copy-start | bytes 196612
